TPU v7x, 8 devices: a whole 2x2x1 slice. The times are simulated.
8 devices in a mesh: model: 4 (over z, y, x), fsdp: 2 (over core).
Axes of the slice: x: 2, y: 2, z: 1, core: 2. Of those that a mesh axis runs over, the one named last changes fastest.
Arguments:
- tok_ids: int32 [2, 2048], P('fsdp')
- tok_labels: int32 [2, 2048], P('fsdp')
- emb_table: bfloat16 [50304, 1024], P(('model', 'fsdp'))
- w_gate: bfloat16 [1024, 4096], P('fsdp')
- w_up: bfloat16 [1024, 4096], P('fsdp')
- w_down: bfloat16 [4096, 1024], P('fsdp')
- gain_in: float32 [1024], replicated
- gain_out: float32 [1024], replicated
Outputs:
- output 1: float32 [], replicated
- output 2: float32 [50304, 1024], P(('model', 'fsdp'))
- output 3: float32 [1024, 4096], P('fsdp')
- output 4: float32 [1024, 4096], P('fsdp')
- output 5: float32 [4096, 1024], P('fsdp')
All inputs are finite; a program needn't handle non-finite values.
Results may differ from a plain program's by a relative error of at most 0.00931599.
Values are sent between devices in bfloat16 or wider.
A program may use at most 1 GiB of HBM per device.

v0:
```python
import jax
import jax.numpy as jnp
from jax import lax
from jax.sharding import PartitionSpec as P

EPS = 1e-6


def rms_scale(values, gain_vec):
    mean_sq = jnp.mean(values * values, axis=-1, keepdims=True)
    return values * lax.rsqrt(mean_sq + EPS) * gain_vec


def mlp_forward(x_emb, gain_in, w_gate, w_up, w_down):
    normed_in, norm_in_back = jax.vjp(lambda values: rms_scale(values, gain_in), x_emb)
    normed_bf = normed_in.astype(jnp.bfloat16)
    gate_f = jnp.dot(normed_bf, w_gate, preferred_element_type=jnp.float32).astype(jnp.bfloat16).astype(jnp.float32)
    up_f = jnp.dot(normed_bf, w_up, preferred_element_type=jnp.float32).astype(jnp.bfloat16).astype(jnp.float32)
    gate_sig = jax.nn.sigmoid(gate_f)
    silu_gate = gate_f * gate_sig
    act_bf = (silu_gate * up_f).astype(jnp.bfloat16)
    mlp_out = jnp.dot(act_bf, w_down, preferred_element_type=jnp.float32).astype(jnp.bfloat16)
    h_res = x_emb + mlp_out.astype(jnp.float32)
    return h_res, (norm_in_back, normed_bf, gate_f, up_f, gate_sig, silu_gate, act_bf)


def mlp_backward(d_hidden, saved, w_gate, w_up, w_down):
    norm_in_back, normed_bf, gate_f, up_f, gate_sig, silu_gate, act_bf = saved
    d_mlp = d_hidden.astype(jnp.bfloat16)
    d_act = jnp.einsum("td,fd->tf", d_mlp, w_down, preferred_element_type=jnp.float32)
    grad_down = jnp.einsum("tf,td->fd", act_bf, d_mlp, preferred_element_type=jnp.float32)
    d_gate = (d_act * up_f * (gate_sig * (1.0 + gate_f * (1.0 - gate_sig)))).astype(jnp.bfloat16)
    d_up = (d_act * silu_gate).astype(jnp.bfloat16)
    grad_gate = jnp.einsum("td,tf->df", normed_bf, d_gate, preferred_element_type=jnp.float32)
    grad_up = jnp.einsum("td,tf->df", normed_bf, d_up, preferred_element_type=jnp.float32)
    d_normed = jnp.einsum("tf,df->td", d_gate, w_gate, preferred_element_type=jnp.float32) + jnp.einsum("tf,df->td", d_up, w_up, preferred_element_type=jnp.float32)
    d_x = d_hidden + norm_in_back(d_normed)[0]
    return d_x, grad_gate, grad_up, grad_down


def solution(mesh):
    fsdp_size = mesh.shape["fsdp"]
    tok_spec = P("fsdp", None)
    row_spec = P(("model", "fsdp"), None)
    weight_spec = P("fsdp", None)

    def device_step(tok_ids, tok_labels, table_shard, gate_shard, up_shard, down_shard, gain_in, gain_out):
        local_count = tok_ids.shape[0] * tok_ids.shape[1]
        num_tokens = local_count * fsdp_size
        table_part = lax.all_gather(table_shard, "fsdp", axis=0, tiled=True)
        w_gate = lax.all_gather(gate_shard, "fsdp", axis=0, tiled=True)
        w_up = lax.all_gather(up_shard, "fsdp", axis=0, tiled=True)
        w_down = lax.all_gather(down_shard, "fsdp", axis=0, tiled=True)
        vocab_part = table_part.shape[0]
        vocab_start = lax.axis_index("model") * vocab_part
        local_ids = tok_ids.reshape(local_count) - vocab_start
        id_inside = (local_ids >= 0) & (local_ids < vocab_part)
        safe_ids = jnp.where(id_inside, local_ids, 0)
        emb_rows = jnp.where(id_inside[:, None], jnp.take(table_part, safe_ids, axis=0), 0)
        x_emb = lax.psum(emb_rows, "model").astype(jnp.float32)
        h_res, saved = mlp_forward(x_emb, gain_in, w_gate, w_up, w_down)
        hn_f, norm_out_back = jax.vjp(lambda values: rms_scale(values, gain_out), h_res)
        hn_bf = hn_f.astype(jnp.bfloat16)
        logits = jnp.einsum("td,vd->tv", hn_bf, table_part, preferred_element_type=jnp.float32)
        row_max = lax.pmax(jnp.max(logits, axis=-1), "model")
        exp_shift = jnp.exp(logits - row_max[:, None])
        local_labels = tok_labels.reshape(local_count) - vocab_start
        onehot = lax.broadcasted_iota(jnp.int32, logits.shape, 1) == local_labels[:, None]
        part_stats = jnp.stack([jnp.sum(exp_shift, axis=-1), jnp.sum(jnp.where(onehot, logits, 0.0), axis=-1)])
        tok_stats = lax.psum(part_stats, "model")
        sum_exp = tok_stats[0]
        tok_loss = row_max + jnp.log(sum_exp) - tok_stats[1]
        loss = lax.psum(jnp.sum(tok_loss), "fsdp") / num_tokens
        soft_probs = exp_shift / sum_exp[:, None]
        d_logits = (jnp.where(onehot, soft_probs - 1.0, soft_probs) / num_tokens).astype(jnp.bfloat16)
        d_head = jnp.einsum("tv,td->vd", d_logits, hn_bf, preferred_element_type=jnp.float32)
        d_hn = lax.psum(jnp.einsum("tv,vd->td", d_logits, table_part, preferred_element_type=jnp.float32), "model")
        d_hidden = norm_out_back(d_hn)[0]
        d_x, grad_gate, grad_up, grad_down = mlp_backward(d_hidden, saved, w_gate, w_up, w_down)
        d_in = jax.ops.segment_sum(jnp.where(id_inside[:, None], d_x, 0.0), safe_ids, num_segments=vocab_part)
        grad_table = lax.psum_scatter(d_head + d_in, "fsdp", scatter_dimension=0, tiled=True)
        grad_gate = lax.psum_scatter(grad_gate, "fsdp", scatter_dimension=0, tiled=True)
        grad_up = lax.psum_scatter(grad_up, "fsdp", scatter_dimension=0, tiled=True)
        grad_down = lax.psum_scatter(grad_down, "fsdp", scatter_dimension=0, tiled=True)
        return loss, grad_table, grad_gate, grad_up, grad_down

    return jax.shard_map(device_step, mesh=mesh, in_specs=(tok_spec, tok_spec, row_spec, weight_spec, weight_spec, weight_spec, P(), P()), out_specs=(P(), row_spec, weight_spec, weight_spec, weight_spec), check_vma=False)
```

profile of v0, /device:TPU:0, one launch (start us, length us, event | category | flops | bytes accessed | tf_op | source)
XLA Modules:
  0.0 1063.6 jit_solution(4178124902470757364)
XLA Ops:
  7.2 0.0 all-gather.5.cloned.1.call-start
  7.2 0.7 all-gather.5.cloned.1.call-update
  7.9 0.0 all-reduce.3.cloned.1.call-start
  8.0 0.6 compare_select_fusion
  8.6 44.2 %all-gather.5.cloned.1.call-done = bf16[12576,1024]{1,0:T(8,128)(2,1)} async-done(((bf16[6288,1024]{1,0:T(8,128)(2,1)}), bf16[12576,1024]{1,0:T(8,128)(2,1)}) %all-gather.5.cloned.1.call-update) | async-done | bytes 25755664 | tf_op jit(solution)/shard_map/all_gather | solution.py:50
  52.8 22.6 %gather_fusion = bf16[2048,1024]{1,0:T(8,128)(2,1)} fusion(bf16[12576,1024]{1,0:T(8,128)(2,1)} %all-gather.5.cloned.1.call-done, s32[2048]{0:T(1024)S(1)} %broadcast_clamp_fusion), kind=kCustom, calls=%fused_computation | custom fusion | bytes 8396800 | tf_op jit(solution)/shard_map/jit(_take)/gather | solution.py:59
  75.4 6.4 copy.15
  81.8 4.7 select_select_fusion
  86.4 0.0 all-reduce.3.cloned.1.call-update
  86.5 0.0 all-gather.7.cloned.1.call-start
  86.5 0.7 all-gather.7.cloned.1.call-update
  87.2 0.0 all-gather.9.cloned.1.call-start
  87.3 0.5 all-gather.9.cloned.1.call-update
  87.8 0.0 all-gather.11.cloned.1.call-start
  87.8 0.5 all-gather.11.cloned.1.call-update
  88.4 0.2 all-reduce.5.cloned.1.call-start
  88.6 0.6 broadcast_subtract_fusion
  89.2 90.5 %all-reduce.3.cloned.1.call-done = bf16[2048,1024]{0,1:T(8,128)(2,1)} async-done(((bf16[2048,1024]{0,1:T(8,128)(2,1)}), bf16[2048,1024]{0,1:T(8,128)(2,1)}) %all-reduce.3.cloned.1.call-update) | async-done | bytes 4194320 | tf_op jit(solution)/shard_map/psum | solution.py:60
  179.7 3.1 fusion.13
  182.8 0.6 copy-done.9
  183.4 15.9 %all-gather.7.cloned.1.call-done = bf16[1024,4096]{1,0:T(8,128)(2,1)} async-done(((bf16[512,4096]{1,0:T(8,128)(2,1)}), bf16[1024,4096]{1,0:T(8,128)(2,1)}) %all-gather.7.cloned.1.call-update) | async-done | bytes 8388624 | tf_op jit(solution)/shard_map/all_gather | solution.py:51
  199.3 25.7 %convolution_convert_fusion.1 = bf16[2048,4096]{1,0:T(8,128)(2,1)} fusion(bf16[1024,4096]{1,0:T(8,128)(2,1)} %all-gather.7.cloned.1.call-done, bf16[2048,1024]{0,1:T(8,128)(2,1)} %all-reduce.3.cloned.1.call-done, f32[1024]{0:T(1024)S(1)} %copy-done.33, f32[2048]{0:T(1024)S(1)} %fusion.21), kind=kOutput, calls=%fused_computation.29 | convolution fusion | flops 17196646400 | bytes 29372416 | tf_op jit(solution)/shard_map/dot_general | solution.py:17
  225.1 34.8 %fusion.3 = (bf16[2048,4096]{1,0:T(8,128)(2,1)}, bf16[2048,4096]{1,0:T(8,128)(2,1)}) fusion(bf16[2048,4096]{1,0:T(8,128)(2,1)} %convolution_convert_fusion.1, bf16[1024,4096]{1,0:T(8,128)(2,1)} %all-gather.9.cloned.1.call-done, bf16[2048,1024]{0,1:T(8,128)(2,1)} %all-reduce.3.cloned.1.call-done, f32[1024]{0:T(1024)S(1)} %copy-done.33, f32[2048]{0:T(1024)S(1)} %fusion.21), kind=kOutput, calls=%fused_computation.14 | convolution fusion | flops 17263755264 | bytes 62926848 | tf_op jit(solution)/shard_map/dot_general | solution.py:18
  259.8 24.7 %multiply_reduce_fusion.1 = (f32[2048]{0:T(1024)S(1)}, bf16[2048,1024]{0,1:T(8,128)(2,1)}) fusion(bf16[2048,1024]{0,1:T(8,128)(2,1)} %all-reduce.3.cloned.1.call-done, bf16[2048,4096]{1,0:T(8,128)(2,1)} %get-tuple-element.16, bf16[4096,1024]{1,0:T(8,128)(2,1)} %all-gather.11.cloned.1.call-done), kind=kOutput, calls=%fused_computation.41 | convolution fusion | flops 17192450048 | bytes 33562624 | tf_op jit(solution)/shard_map/dot_general | solution.py:22
  284.6 66.3 %fusion.32 = (f32[2048]{0:T(1024)S(1)}, f32[2048,12576]{0,1:T(8,128)}) fusion(bf16[12576,1024]{1,0:T(8,128)(2,1)} %all-gather.5.cloned.1.call-done, bf16[2048,1024]{0,1:T(8,128)(2,1)} %get-tuple-element.19, bf16[2048,1024]{0,1:T(8,128)(2,1)S(1)} %copy-done.1, f32[1024]{0:T(1024)S(1)} %copy-done.19, f32[2048]{0:T(1024)S(1)} %fusion.22), kind=kOutput, calls=%fused_computation.69 | convolution fusion | flops 52785905664 | bytes 137187328 | tf_op jit(solution)/shard_map/td,vd->tv/dot_general | solution.py:64
  350.9 10.2 pmax.7
  361.1 32.1 %fusion.2 = (f32[2048]{0:T(1024)S(1)}, f32[2048]{0:T(1024)S(1)}) fusion(f32[2048,12576]{0,1:T(8,128)} %get-tuple-element.21, f32[2048]{0:T(1024)S(1)} %pmax.7, s32[2048]{0:T(1024)S(1)} %bitcast.33), kind=kLoop, calls=%fused_computation.8 | loop fusion | flops 128774144 | bytes 103055360 | tf_op jit(solution)/shard_map/reduce_sum | solution.py:69
  393.3 14.1 %psum.29 = f32[2,2048]{1,0:T(2,128)S(1)} all-reduce(f32[2,2048]{1,0:T(2,128)S(1)} %pad_maximum_fusion), channel_id=1, replica_groups=mesh['model'=4,'fsdp'=2] {'model'}, use_global_device_ids=true, to_apply=%region_7.8 | all-reduce | flops 4096 | bytes 32768 | tf_op jit(solution)/shard_map/psum | solution.py:70
  407.4 0.6 fusion.31
  408.0 50.3 %fusion.1 = bf16[2048,12576]{0,1:T(8,128)(2,1)} fusion(f32[2048,12576]{0,1:T(8,128)} %get-tuple-element.21, f32[2048]{0:T(1024)S(1)} %bitcast.35, s32[2048]{0:T(1024)S(1)} %bitcast.34, f32[2048]{0:T(1024)S(1)} %pmax.7), kind=kLoop, calls=%fused_computation.4 | loop fusion | flops 180289536 | bytes 154558464 | tf_op jit(solution)/shard_map/convert_element_type | solution.py:75
  458.3 64.7 %fusion.33 = f32[2048,1024]{0,1:T(8,128)} fusion(bf16[2048,12576]{0,1:T(8,128)(2,1)} %fusion.1, bf16[12576,1024]{1,0:T(8,128)(2,1)} %all-gather.5.cloned.1.call-done), kind=kOutput, calls=%fused_computation.70 | convolution fusion | flops 52747567104 | bytes 85655552 | tf_op jit(solution)/shard_map/tv,vd->td/dot_general | solution.py:77
  523.0 0.0 all-reduce.5.cloned.1.call-update
  523.0 0.0 reduce-scatter.7.cloned.1.call-start
  523.1 160.5 %all-reduce.5.cloned.1.call-done = f32[2048,1024]{0,1:T(8,128)} async-done(((f32[2048,1024]{0,1:T(8,128)}), f32[2048,1024]{0,1:T(8,128)}) %all-reduce.5.cloned.1.call-update) | async-done | bytes 8388624 | tf_op jit(solution)/shard_map/psum | solution.py:77
  683.5 7.5 multiply_reduce_fusion
  691.1 0.6 copy-done
  691.7 1.2 copy-done.2
  692.9 1.2 copy-done.4
  694.1 4.7 fusion.20.clone.4
  698.9 43.3 %multiply_convert_fusion = (bf16[2048,4096]{1,0:T(8,128)(2,1)}, bf16[2048,4096]{1,0:T(8,128)(2,1)}) fusion(bf16[2048,4096]{1,0:T(8,128)(2,1)} %convolution_convert_fusion.1, bf16[2048,4096]{1,0:T(8,128)(2,1)} %get-tuple-element.17, bf16[4096,1024]{1,0:T(8,128)(2,1)} %all-gather.11.cloned.1.call-done, bf16[2048,1024]{0,1:T(8,128)(2,1)} %fusion.20.clone.4), kind=kOutput, calls=%fused_computation.22 | convolution fusion | flops 17305698304 | bytes 79691776 | tf_op jit(solution)/shard_map/td,fd->tf/dot_general | solution.py:30
  742.2 24.0 %fusion.27 = f32[1024,4096]{1,0:T(8,128)} fusion(bf16[2048,4096]{1,0:T(8,128)(2,1)} %get-tuple-element.11, bf16[2048,1024]{0,1:T(8,128)(2,1)} %all-reduce.3.cloned.1.call-done, f32[1024]{0:T(1024)S(1)} %copy-done.34, f32[2048]{0:T(1024)S(1)} %copy-done.27), kind=kOutput, calls=%fused_computation.67 | convolution fusion | flops 17188257792 | bytes 37761024 | tf_op jit(solution)/shard_map/td,tf->df/dot_general | solution.py:34
  766.2 0.0 reduce-scatter.7.cloned.1.call-update
  766.2 0.0 reduce-scatter.9.cloned.1.call-start
  766.3 23.6 %fusion.25 = f32[1024,4096]{1,0:T(8,128)} fusion(bf16[2048,4096]{1,0:T(8,128)(2,1)} %get-tuple-element.10, bf16[2048,1024]{0,1:T(8,128)(2,1)} %all-reduce.3.cloned.1.call-done, f32[1024]{0:T(1024)S(1)} %copy-done.34, f32[2048]{0:T(1024)S(1)} %copy-done.27), kind=kOutput, calls=%fused_computation.66 | convolution fusion | flops 17188257792 | bytes 37761024 | tf_op jit(solution)/shard_map/td,tf->df/dot_general | solution.py:35
  789.9 0.0 reduce-scatter.9.cloned.1.call-update
  789.9 0.0 reduce-scatter.11.cloned.1.call-start
  790.0 0.6 copy-done.14
  790.6 28.5 %fusion.17 = f32[4096,1024]{1,0:T(8,128)} fusion(bf16[2048,4096]{1,0:T(8,128)(2,1)} %get-tuple-element.16, f32[2048,1024]{0,1:T(8,128)} %all-reduce.5.cloned.1.call-done, bf16[2048,1024]{0,1:T(8,128)(2,1)} %get-tuple-element.19, bf16[2048,1024]{0,1:T(8,128)(2,1)} %all-reduce.3.cloned.1.call-done, f32[2048]{0:T(1024)S(1)} %copy-done.14, ...), kind=kOutput, calls=%fused_computation.44 | convolution fusion | flops 17198743552 | bytes 50352128 | tf_op jit(solution)/shard_map/tf,td->fd/dot_general | solution.py:31
  819.1 0.0 reduce-scatter.11.cloned.1.call-update
  819.1 0.0 reduce-scatter.5.cloned.1.call-start
  819.2 65.7 %fusion.23 = f32[12576,1024]{1,0:T(8,128)} fusion(bf16[2048,12576]{0,1:T(8,128)(2,1)} %fusion.1, bf16[2048,1024]{0,1:T(8,128)(2,1)} %get-tuple-element.19, bf16[2048,1024]{0,1:T(8,128)(2,1)} %all-reduce.3.cloned.1.call-done, f32[1024]{0:T(1024)S(1)} %copy-done.21, f32[2048]{0:T(1024)S(1)} %copy-done.18), kind=kOutput, calls=%fused_computation.64 | convolution fusion | flops 52760150016 | bytes 111423488 | tf_op jit(solution)/shard_map/tv,td->vd/dot_general | solution.py:76
  884.9 24.3 %fusion.34 = f32[2048,1024]{0,1:T(8,128)} fusion(bf16[2048,4096]{1,0:T(8,128)(2,1)} %get-tuple-element.11, bf16[1024,4096]{1,0:T(8,128)(2,1)} %all-gather.7.cloned.1.call-done), kind=kOutput, calls=%fused_computation.71 | convolution fusion | flops 17179869184 | bytes 33554432 | tf_op jit(solution)/shard_map/tf,df->td/dot_general | solution.py:36
  909.3 25.6 %fusion.16 = (f32[2048]{0:T(1024)S(1)}, f32[2048,1024]{0,1:T(8,128)}) fusion(bf16[2048,1024]{0,1:T(8,128)(2,1)S(1)} %copy-done.3, f32[1024]{0:T(1024)S(1)} %copy-done.35, f32[2048,1024]{0,1:T(8,128)} %fusion.34, bf16[2048,4096]{1,0:T(8,128)(2,1)} %get-tuple-element.10, bf16[1024,4096]{1,0:T(8,128)(2,1)} %all-gather.9.cloned.1.call-done), kind=kOutput, calls=%fused_computation.37 | convolution fusion | flops 17190352896 | bytes 46149632 | tf_op jit(solution)/shard_map/tf,df->td/dot_general | solution.py:36
  935.0 8.8 fusion.12
  943.8 9.3 copy.17
  953.1 51.7 %scatter_fusion = f32[12576,1024]{1,0:T(8,128)} fusion(f32[12576,1024]{1,0:T(8,128)} %fusion.23, s32[2048]{0:T(1024)S(1)} %bitcast.37, f32[2048,1024]{1,0:T(8,128)} %copy.17), kind=kCustom, calls=%fused_computation.1 | custom fusion | flops 2097152 | bytes 25174016 | tf_op jit(solution)/shard_map/scatter-add | solution.py:80
  1004.8 0.0 reduce-scatter.5.cloned.1.call-update
  1004.8 0.7 copy-done.7
  1005.5 0.6 subtract_reduce_fusion
  1006.1 3.1 psum.30
  1009.9 0.0 reduce-scatter.7.cloned.1.call-done
  1009.9 0.0 reduce-scatter.9.cloned.1.call-done
  1009.9 0.0 reduce-scatter.11.cloned.1.call-done
  1009.9 45.4 %reduce-scatter.5.cloned.1.call-done = f32[6288,1024]{1,0:T(8,128)} async-done(((f32[12576,1024]{1,0:T(8,128)}), f32[6288,1024]{1,0:T(8,128)}) %reduce-scatter.5.cloned.1.call-update) | async-done | bytes 25755664 | tf_op jit(solution)/shard_map/reduce_scatter | solution.py:81
  (80 shorter events, 0.3 us)
Async XLA Ops:
  7.2 0.8 copy-start.32
  7.2 45.6 %all-gather.5.cloned.1.call-start = ((), (), s32[]{:S(2)}) async-start(), calls=%async_computation.4 | async-start | bytes 38633472 | tf_op jit(solution)/shard_map/all_gather | solution.py:50
  7.9 171.8 %all-reduce.3.cloned.1.call-start = ((), (), s32[]{:S(2)}) async-start(), calls=%async_computation.5 | async-start | bytes 8388608 | tf_op jit(solution)/shard_map/psum | solution.py:60
  8.6 73.2 %copy-start.29 = (pred[2048]{0:T(1024)(128)(4,1)}, pred[2048]{0:T(1024)(128)(4,1)S(1)}, u32[]{:S(2)}) copy-start(pred[2048]{0:T(1024)(128)(4,1)S(1)} %get-tuple-element.14) | copy-start | bytes 6148
  86.4 2.2 copy-start.31
  86.5 112.9 %copy-start.33 = (f32[1024]{0:T(1024)S(1)}, f32[1024]{0:T(1024)}, u32[]{:S(2)}) copy-start(f32[1024]{0:T(1024)} %param.14) | copy-start | bytes 12292
  86.5 112.8 %all-gather.7.cloned.1.call-start = ((), (), s32[]{:S(2)}) async-start(), calls=%async_computation.6 | async-start | bytes 12582912 | tf_op jit(solution)/shard_map/all_gather | solution.py:51
  87.2 137.8 %all-gather.9.cloned.1.call-start = ((), (), s32[]{:S(2)}) async-start(), calls=%async_computation.7 | async-start | bytes 12582912 | tf_op jit(solution)/shard_map/all_gather | solution.py:52
  87.8 172.0 %all-gather.11.cloned.1.call-start = ((), (), s32[]{:S(2)}) async-start(), calls=%async_computation.8 | async-start | bytes 12582912 | tf_op jit(solution)/shard_map/all_gather | solution.py:53
  88.4 595.1 %all-reduce.5.cloned.1.call-start = ((), (), s32[]{:S(2)}) async-start(), calls=%async_computation.9 | async-start | bytes 16777216 | tf_op jit(solution)/shard_map/psum | solution.py:77
  182.8 0.6 copy-start.9
  183.4 41.6 %copy-start.26 = (f32[2048]{0:T(1024)}, f32[2048]{0:T(1024)S(1)}, u32[]{:S(2)}) copy-start(f32[2048]{0:T(1024)S(1)} %fusion.21) | copy-start | bytes 24580
  259.8 24.8 %copy-start.1 = (bf16[2048,1024]{0,1:T(8,128)(2,1)S(1)}, bf16[2048,1024]{0,1:T(8,128)(2,1)}, u32[]{:S(2)}) copy-start(bf16[2048,1024]{0,1:T(8,128)(2,1)} %all-reduce.3.cloned.1.call-done) | copy-start | bytes 12582916
  259.8 24.8 %copy-start.19 = (f32[1024]{0:T(1024)S(1)}, f32[1024]{0:T(1024)}, u32[]{:S(2)}) copy-start(f32[1024]{0:T(1024)} %param.15) | copy-start | bytes 12292
  284.6 66.3 %copy-start.23 = (f32[2048]{0:T(1024)}, f32[2048]{0:T(1024)S(1)}, u32[]{:S(2)}) copy-start(f32[2048]{0:T(1024)S(1)} %get-tuple-element.18) | copy-start | bytes 24580
  284.6 66.3 %copy-start.16 = (f32[2048]{0:T(1024)}, f32[2048]{0:T(1024)S(1)}, u32[]{:S(2)}) copy-start(f32[2048]{0:T(1024)S(1)} %fusion.22) | copy-start | bytes 24580
  284.6 76.5 %copy-start.8 = (s32[1,2048]{1,0:T(1,128)S(1)}, s32[1,2048]{1,0:T(1,128)}, u32[]{:S(2)}) copy-start(s32[1,2048]{1,0:T(1,128)} %broadcast_subtract_fusion) | copy-start | bytes 24580
  361.1 46.9 %copy-start.6 = (f32[2048]{0:T(1024)}, f32[2048]{0:T(1024)S(1)}, u32[]{:S(2)}) copy-start(f32[2048]{0:T(1024)S(1)} %pmax.7) | copy-start | bytes 24580
  408.0 50.3 %copy-start.11 = (f32[1,2048]{1,0:T(1,128)}, f32[1,2048]{1,0:T(1,128)S(1)}, u32[]{:S(2)}) copy-start(f32[1,2048]{1,0:T(1,128)S(1)} %get-tuple-element.12) | copy-start | bytes 24580
  523.0 160.6 %copy-start.20 = (f32[1024]{0:T(1024)S(1)}, f32[1024]{0:T(1024)}, u32[]{:S(2)}) copy-start(f32[1024]{0:T(1024)} %param.15) | copy-start | bytes 12292
  523.0 168.1 %copy-start.24 = (f32[2048]{0:T(1024)S(1)}, f32[2048]{0:T(1024)}, u32[]{:S(2)}) copy-start(f32[2048]{0:T(1024)} %copy-done.23) | copy-start | bytes 24580
  523.0 168.1 %copy-start.17 = (f32[2048]{0:T(1024)S(1)}, f32[2048]{0:T(1024)}, u32[]{:S(2)}) copy-start(f32[2048]{0:T(1024)} %copy-done.16) | copy-start | bytes 24580
  523.0 486.9 %reduce-scatter.7.cloned.1.call-start = ((), (), s32[]{:S(2)}) async-start(), calls=%async_computation.11 | async-start | bytes 25165824 | tf_op jit(solution)/shard_map/reduce_scatter | solution.py:82
  683.5 8.2 copy-start
  683.5 9.4 copy-start.2
  683.5 10.6 copy-start.4
  694.1 4.8 copy-start.13
  698.9 43.3 %copy-start.27 = (f32[2048]{0:T(1024)S(1)}, f32[2048]{0:T(1024)}, u32[]{:S(2)}) copy-start(f32[2048]{0:T(1024)} %copy-done.26) | copy-start | bytes 24580
  698.9 43.3 %copy-start.34 = (f32[1024]{0:T(1024)S(1)}, f32[1024]{0:T(1024)}, u32[]{:S(2)}) copy-start(f32[1024]{0:T(1024)} %param.14) | copy-start | bytes 12292
  766.2 243.7 %reduce-scatter.9.cloned.1.call-start = ((), (), s32[]{:S(2)}) async-start(), calls=%async_computation.12 | async-start | bytes 25165824 | tf_op jit(solution)/shard_map/reduce_scatter | solution.py:83
  789.9 0.7 copy-start.14
  789.9 0.7 copy-start.18
  789.9 0.7 copy-start.21
  789.9 220.0 %reduce-scatter.11.cloned.1.call-start = ((), (), s32[]{:S(2)}) async-start(), calls=%async_computation.13 | async-start | bytes 25165824 | tf_op jit(solution)/shard_map/reduce_scatter | solution.py:84
  819.1 236.2 %reduce-scatter.5.cloned.1.call-start = ((), (), s32[]{:S(2)}) async-start(), calls=%async_computation.10 | async-start | bytes 77266944 | tf_op jit(solution)/shard_map/reduce_scatter | solution.py:81
  884.9 24.3 %copy-start.3 = (bf16[2048,1024]{0,1:T(8,128)(2,1)S(1)}, bf16[2048,1024]{0,1:T(8,128)(2,1)}, u32[]{:S(2)}) copy-start(bf16[2048,1024]{0,1:T(8,128)(2,1)} %all-reduce.3.cloned.1.call-done) | copy-start | bytes 12582916
  884.9 24.3 %copy-start.35 = (f32[1024]{0:T(1024)S(1)}, f32[1024]{0:T(1024)}, u32[]{:S(2)}) copy-start(f32[1024]{0:T(1024)} %param.14) | copy-start | bytes 12292
  884.9 50.0 %slice-start = ((s8[8388608]{0:T(1024)(128)(4,1)}), s8[4194304]{0:T(1024)(128)(4,1)S(1)}, s32[]{:S(2)}) async-start(s8[8388608]{0:T(1024)(128)(4,1)} %bitcast.31), calls=%async_computation.14 | async-start | bytes 8388608
  909.2 25.6 %copy-start.10 = (f32[2048]{0:T(1024)S(1)}, f32[2048]{0:T(1024)}, u32[]{:S(2)}) copy-start(f32[2048]{0:T(1024)} %copy-done.9) | copy-start | bytes 24580
  909.2 25.7 %slice-start.1 = ((s8[8388608]{0:T(1024)(128)(4,1)}), s8[4194304]{0:T(1024)(128)(4,1)S(1)}, s32[]{:S(2)}) async-start(s8[8388608]{0:T(1024)(128)(4,1)} %bitcast.31), calls=%async_computation.15 | async-start | bytes 8388608
  909.2 25.7 %copy-start.5 = (bf16[2048,1024]{0,1:T(8,128)(2,1)S(1)}, bf16[2048,1024]{0,1:T(8,128)(2,1)}, u32[]{:S(2)}) copy-start(bf16[2048,1024]{0,1:T(8,128)(2,1)} %get-tuple-element.19) | copy-start | bytes 12582916
  909.3 25.7 %copy-start.15 = (f32[2048]{0:T(1024)S(1)}, f32[2048]{0:T(1024)}, u32[]{:S(2)}) copy-start(f32[2048]{0:T(1024)} %copy-done.13) | copy-start | bytes 24580
  909.3 25.7 %copy-start.28 = (f32[2048]{0:T(1024)S(1)}, f32[2048]{0:T(1024)}, u32[]{:S(2)}) copy-start(f32[2048]{0:T(1024)} %copy-done.26) | copy-start | bytes 24580
  909.3 25.7 %copy-start.30 = (pred[2048]{0:T(1024)(128)(4,1)S(1)}, pred[2048]{0:T(1024)(128)(4,1)}, u32[]{:S(2)}) copy-start(pred[2048]{0:T(1024)(128)(4,1)} %copy-done.29) | copy-start | bytes 6148
  943.8 9.3 copy-start.22
  1004.8 0.7 copy-start.7
  1004.8 0.7 copy-start.12
  1004.8 0.7 copy-start.25
Sparse Core Ops, SparseCore 0:
  9.5 43.2 all-gather.4
  86.6 93.1 all-reduce.2
  181.3 18.0 all-gather.6
  200.7 19.1 all-gather.8
  221.3 19.1 all-gather.10
  523.1 160.3 all-reduce.4
  766.3 22.4 reduce-scatter.6
  791.7 22.9 reduce-scatter.8
  819.3 22.4 reduce-scatter.10
  1004.9 50.3 reduce-scatter.4
where the time goes:
time: 1070 us; the launch traced here: 1060 us
  matrix products  451 us (42%)
  waiting for transfers between devices  359 us (34%)
  other arithmetic  165 us (15%)
  local copies, waits for them, and re-layouts  44 us (4%)
  blocking collectives  27.4 us (3%)
  between operations  16.5 us (2%)
    psum x1, waiting for transfers between devices, device_step(): lax.psum(jnp.einsum('tv,vd->td', d_logits, table_part, preferred_element_...  160 us
    psum x1, waiting for transfers between devices, device_step(): x_emb = lax.psum(emb_rows, 'model').astype(jnp.float32)  90.5 us
    dot_general x1, matrix products, device_step(): jnp.einsum('td,vd->tv', hn_bf, table_part, preferred_element_type=jnp.flo...  66.3 us
    dot_general x1, matrix products, device_step(): jnp.einsum('tv,td->vd', d_logits, hn_bf, preferred_element_type=jnp.float32)  65.7 us
    dot_general x1, matrix products, device_step(): jnp.einsum('tv,vd->td', d_logits, table_part, preferred_element_type=jnp....  64.7 us
    scatter-add x1, other arithmetic, device_step(): jax.ops.segment_sum(jnp.where(id_inside[:, None], d_x, 0.0), safe_ids, nu...  51.7 us
    convert_element_type x1, other arithmetic, device_step(): (jnp.where(onehot, soft_probs - 1.0, soft_probs) / num_tokens).astype(jnp...  50.3 us
    reduce_scatter x1, waiting for transfers between devices, device_step(): lax.psum_scatter(d_head + d_in, 'fsdp', scatter_dimension=0, tiled=True)  45.4 us
  transfers between devices with their start and end apart: 10, of which 5 were waited for; matrix products, arithmetic and copies ran while one was open for 28% of the time, Pallas kernels for 0%

commit v1 on v0

v1 whole, which is shorter than its diff:
```python
import functools

import jax
import jax.numpy as jnp
from jax import lax
from jax.experimental import pallas as pl
from jax.experimental.pallas import tpu as pltpu
from jax.sharding import PartitionSpec as P

EPS = 1e-6
VMEM_LIMIT = 63 * 1024 * 1024
LANES = 128


def rms_scale(values, gain_vec):
    mean_sq = jnp.mean(values * values, axis=-1, keepdims=True)
    return values * lax.rsqrt(mean_sq + EPS) * gain_vec


def mlp_forward(x_emb, gain_in, w_gate, w_up, w_down):
    normed_in, norm_in_back = jax.vjp(lambda values: rms_scale(values, gain_in), x_emb)
    normed_bf = normed_in.astype(jnp.bfloat16)
    gate_f = jnp.dot(normed_bf, w_gate, preferred_element_type=jnp.float32).astype(jnp.bfloat16).astype(jnp.float32)
    up_f = jnp.dot(normed_bf, w_up, preferred_element_type=jnp.float32).astype(jnp.bfloat16).astype(jnp.float32)
    gate_sig = jax.nn.sigmoid(gate_f)
    silu_gate = gate_f * gate_sig
    act_bf = (silu_gate * up_f).astype(jnp.bfloat16)
    mlp_out = jnp.dot(act_bf, w_down, preferred_element_type=jnp.float32).astype(jnp.bfloat16)
    h_res = x_emb + mlp_out.astype(jnp.float32)
    return h_res, (norm_in_back, normed_bf, gate_f, up_f, gate_sig, silu_gate, act_bf)


def mlp_backward(d_hidden, saved, w_gate, w_up, w_down):
    norm_in_back, normed_bf, gate_f, up_f, gate_sig, silu_gate, act_bf = saved
    d_mlp = d_hidden.astype(jnp.bfloat16)
    d_act = jnp.einsum("td,fd->tf", d_mlp, w_down, preferred_element_type=jnp.float32)
    grad_down = jnp.einsum("tf,td->fd", act_bf, d_mlp, preferred_element_type=jnp.float32)
    d_gate = (d_act * up_f * (gate_sig * (1.0 + gate_f * (1.0 - gate_sig)))).astype(jnp.bfloat16)
    d_up = (d_act * silu_gate).astype(jnp.bfloat16)
    grad_gate = jnp.einsum("td,tf->df", normed_bf, d_gate, preferred_element_type=jnp.float32)
    grad_up = jnp.einsum("td,tf->df", normed_bf, d_up, preferred_element_type=jnp.float32)
    d_normed = jnp.einsum("tf,df->td", d_gate, w_gate, preferred_element_type=jnp.float32) + jnp.einsum("tf,df->td", d_up, w_up, preferred_element_type=jnp.float32)
    d_x = d_hidden + norm_in_back(d_normed)[0]
    return d_x, grad_gate, grad_up, grad_down


def slow_step(tok_ids, tok_labels, table_shard, gate_shard, up_shard, down_shard, gain_in, gain_out):
    fsdp_size = lax.axis_size("fsdp")
    local_count = tok_ids.shape[0] * tok_ids.shape[1]
    num_tokens = local_count * fsdp_size
    table_part = lax.all_gather(table_shard, "fsdp", axis=0, tiled=True)
    w_gate = lax.all_gather(gate_shard, "fsdp", axis=0, tiled=True)
    w_up = lax.all_gather(up_shard, "fsdp", axis=0, tiled=True)
    w_down = lax.all_gather(down_shard, "fsdp", axis=0, tiled=True)
    vocab_part = table_part.shape[0]
    vocab_start = lax.axis_index("model") * vocab_part
    local_ids = tok_ids.reshape(local_count) - vocab_start
    id_inside = (local_ids >= 0) & (local_ids < vocab_part)
    safe_ids = jnp.where(id_inside, local_ids, 0)
    emb_rows = jnp.where(id_inside[:, None], jnp.take(table_part, safe_ids, axis=0), 0)
    x_emb = lax.psum(emb_rows, "model").astype(jnp.float32)
    h_res, saved = mlp_forward(x_emb, gain_in, w_gate, w_up, w_down)
    hn_f, norm_out_back = jax.vjp(lambda values: rms_scale(values, gain_out), h_res)
    hn_bf = hn_f.astype(jnp.bfloat16)
    logits = jnp.einsum("td,vd->tv", hn_bf, table_part, preferred_element_type=jnp.float32)
    row_max = lax.pmax(jnp.max(logits, axis=-1), "model")
    exp_shift = jnp.exp(logits - row_max[:, None])
    local_labels = tok_labels.reshape(local_count) - vocab_start
    onehot = lax.broadcasted_iota(jnp.int32, logits.shape, 1) == local_labels[:, None]
    part_stats = jnp.stack([jnp.sum(exp_shift, axis=-1), jnp.sum(jnp.where(onehot, logits, 0.0), axis=-1)])
    tok_stats = lax.psum(part_stats, "model")
    sum_exp = tok_stats[0]
    tok_loss = row_max + jnp.log(sum_exp) - tok_stats[1]
    loss = lax.psum(jnp.sum(tok_loss), "fsdp") / num_tokens
    soft_probs = exp_shift / sum_exp[:, None]
    d_logits = (jnp.where(onehot, soft_probs - 1.0, soft_probs) / num_tokens).astype(jnp.bfloat16)
    d_head = jnp.einsum("tv,td->vd", d_logits, hn_bf, preferred_element_type=jnp.float32)
    d_hn = lax.psum(jnp.einsum("tv,vd->td", d_logits, table_part, preferred_element_type=jnp.float32), "model")
    d_hidden = norm_out_back(d_hn)[0]
    d_x, grad_gate, grad_up, grad_down = mlp_backward(d_hidden, saved, w_gate, w_up, w_down)
    d_in = jax.ops.segment_sum(jnp.where(id_inside[:, None], d_x, 0.0), safe_ids, num_segments=vocab_part)
    grad_table = lax.psum_scatter(d_head + d_in, "fsdp", scatter_dimension=0, tiled=True)
    grad_gate = lax.psum_scatter(grad_gate, "fsdp", scatter_dimension=0, tiled=True)
    grad_up = lax.psum_scatter(grad_up, "fsdp", scatter_dimension=0, tiled=True)
    grad_down = lax.psum_scatter(grad_down, "fsdp", scatter_dimension=0, tiled=True)
    return loss, grad_table, grad_gate, grad_up, grad_down


def lane_chunks(width, chunk):
    return [(lo, min(chunk, width - lo)) for lo in range(0, width, chunk)]

def logits_kernel(chunk, hn_ref, emb_ref, lab_ref, z_ref, stat_ref):
    rows, vocab = z_ref.shape
    hn = hn_ref[...]
    label = lab_ref[...]
    lane = lax.broadcasted_iota(jnp.int32, (rows, LANES), 1)
    run_max = jnp.full((rows, LANES), -jnp.inf, jnp.float32)
    run_sum = jnp.zeros((rows, LANES), jnp.float32)
    run_lab = jnp.zeros((rows, LANES), jnp.float32)
    tail = None
    for lo, width in lane_chunks(vocab, chunk):
        z = lax.dot_general(hn, emb_ref[lo:lo + width, :], (((1,), (1,)), ((), ())), preferred_element_type=jnp.float32)
        z_ref[:, lo:lo + width] = z
        groups = width // LANES
        new_max = run_max
        for g in range(groups):
            part = z[:, g * LANES:(g + 1) * LANES]
            new_max = jnp.maximum(new_max, part)
            run_lab = run_lab + jnp.where(lane == label - (lo + g * LANES), part, 0.0)
        run_sum = run_sum * jnp.exp(run_max - new_max)
        for g in range(groups):
            run_sum = run_sum + jnp.exp(z[:, g * LANES:(g + 1) * LANES] - new_max)
        run_max = new_max
        if width % LANES:
            tail = (lo + groups * LANES, z[:, groups * LANES:])
    row_max = jnp.max(run_max, axis=1, keepdims=True)
    if tail is not None:
        row_max = jnp.maximum(row_max, jnp.max(tail[1], axis=1, keepdims=True))
    row_sum = jnp.sum(run_sum * jnp.exp(run_max - row_max), axis=1, keepdims=True)
    row_lab = jnp.sum(run_lab, axis=1, keepdims=True)
    if tail is not None:
        start, z = tail
        tail_lane = lax.broadcasted_iota(jnp.int32, z.shape, 1)
        row_sum = row_sum + jnp.sum(jnp.exp(z - row_max), axis=1, keepdims=True)
        row_lab = row_lab + jnp.sum(jnp.where(tail_lane == label - start, z, 0.0), axis=1, keepdims=True)
    stat_ref[...] = jnp.where(lane == 0, row_max, jnp.where(lane == 1, row_sum, row_lab))

def head_logits(hn, table, labels, blk=256, chunk=1024):
    tokens, depth = hn.shape
    vocab = table.shape[0]
    return pl.pallas_call(
        functools.partial(logits_kernel, chunk),
        grid=(tokens // blk,),
        in_specs=[
            pl.BlockSpec((blk, depth), lambda i: (i, 0)),
            pl.BlockSpec((vocab, depth), lambda i: (0, 0), pipeline_mode=pl.Buffered(1)),
            pl.BlockSpec((blk, 1), lambda i: (i, 0)),
        ],
        out_specs=[
            pl.BlockSpec((blk, vocab), lambda i: (i, 0)),
            pl.BlockSpec((blk, LANES), lambda i: (i, 0)),
        ],
        out_shape=[jax.ShapeDtypeStruct((tokens, vocab), jnp.float32), jax.ShapeDtypeStruct((tokens, LANES), jnp.float32)],
        cost_estimate=pl.CostEstimate(flops=2 * tokens * vocab * depth, bytes_accessed=4 * tokens * vocab, transcendentals=tokens * vocab),
        compiler_params=pltpu.CompilerParams(vmem_limit_bytes=VMEM_LIMIT),
        name="head_logits",
    )(hn, table, labels)

def dlogits_kernel(inv_tokens, chunk, z_ref, emb_ref, stat_ref, lab_ref, dz_ref, dhn_ref):
    rows, vocab = z_ref.shape
    row_max = stat_ref[:, 0:1]
    scale = stat_ref[:, 1:2]
    label = lab_ref[...]
    total = None
    for n, (lo, width) in enumerate(lane_chunks(vocab, chunk)):
        prob = jnp.exp(z_ref[:, lo:lo + width] - row_max) * scale
        lane = lax.broadcasted_iota(jnp.int32, (rows, width), 1)
        prob = jnp.where(lane == label - lo, prob - 1.0, prob)
        dz = (prob * inv_tokens).astype(jnp.bfloat16)
        dz_ref[:, lo:lo + width] = dz
        part = jnp.dot(dz, emb_ref[lo:lo + width, :], preferred_element_type=jnp.float32)
        total = part if total is None else total + part
    dhn_ref[...] = total

def head_dlogits(z, table, stats, labels, inv_tokens, blk=256, chunk=1024):
    tokens, vocab = z.shape
    depth = table.shape[1]
    return pl.pallas_call(
        functools.partial(dlogits_kernel, inv_tokens, chunk),
        grid=(tokens // blk,),
        in_specs=[
            pl.BlockSpec((blk, vocab), lambda i: (i, 0)),
            pl.BlockSpec((vocab, depth), lambda i: (0, 0), pipeline_mode=pl.Buffered(1)),
            pl.BlockSpec((blk, LANES), lambda i: (i, 0)),
            pl.BlockSpec((blk, 1), lambda i: (i, 0)),
        ],
        out_specs=[
            pl.BlockSpec((blk, vocab), lambda i: (i, 0)),
            pl.BlockSpec((blk, depth), lambda i: (i, 0)),
        ],
        out_shape=[jax.ShapeDtypeStruct((tokens, vocab), jnp.bfloat16), jax.ShapeDtypeStruct((tokens, depth), jnp.float32)],
        cost_estimate=pl.CostEstimate(flops=2 * tokens * vocab * depth, bytes_accessed=6 * tokens * vocab, transcendentals=tokens * vocab),
        compiler_params=pltpu.CompilerParams(vmem_limit_bytes=VMEM_LIMIT),
        name="head_dlogits",
    )(z, table, stats, labels)

TN = (((0,), (0,)), ((), ()))
NT = (((1,), (1,)), ((), ()))

def dhead_kernel(a_ref, ha_ref, b_ref, hb_ref, out_ref):
    out_ref[...] = (lax.dot_general(a_ref[...], ha_ref[...], TN, preferred_element_type=jnp.float32)
                    + lax.dot_general(b_ref[...], hb_ref[...], TN, preferred_element_type=jnp.float32))

def head_dtable(dz_a, hn_a, dz_b, hn_b, tile=640):
    tokens, vocab = dz_a.shape
    depth = hn_a.shape[1]
    dz_spec = pl.BlockSpec((tokens, tile), lambda i: (0, i))
    hn_spec = pl.BlockSpec((tokens, depth), lambda i: (0, 0), pipeline_mode=pl.Buffered(1))
    return pl.pallas_call(
        dhead_kernel,
        grid=(pl.cdiv(vocab, tile),),
        in_specs=[dz_spec, hn_spec, dz_spec, hn_spec],
        out_specs=pl.BlockSpec((tile, depth), lambda i: (i, 0)),
        out_shape=jax.ShapeDtypeStruct((vocab, depth), jnp.float32),
        cost_estimate=pl.CostEstimate(flops=4 * tokens * vocab * depth, bytes_accessed=4 * tokens * vocab + 4 * vocab * depth, transcendentals=0),
        compiler_params=pltpu.CompilerParams(vmem_limit_bytes=VMEM_LIMIT),
        name="head_dtable",
    )(dz_a, hn_a, dz_b, hn_b)

def norm(values, gain):
    return values * lax.rsqrt(jnp.mean(values * values, axis=-1, keepdims=True) + EPS) * gain

def mlp_kernel(chunk, x_ref, g1_ref, g2_ref, wg_ref, wu_ref, wd_ref, a_ref, gt_ref, up_ref, q_ref, h_ref, hn_ref):
    x = x_ref[...]
    a = norm(x, g1_ref[...]).astype(jnp.bfloat16)
    a_ref[...] = a
    total = None
    for lo in range(0, gt_ref.shape[1], chunk):
        cols = slice(lo, lo + chunk)
        gt = jnp.dot(a, wg_ref[:, cols], preferred_element_type=jnp.float32).astype(jnp.bfloat16)
        up = jnp.dot(a, wu_ref[:, cols], preferred_element_type=jnp.float32).astype(jnp.bfloat16)
        gt_ref[:, cols] = gt
        up_ref[:, cols] = up
        gate = gt.astype(jnp.float32)
        q = (gate * jax.nn.sigmoid(gate) * up.astype(jnp.float32)).astype(jnp.bfloat16)
        q_ref[:, cols] = q
        part = jnp.dot(q, wd_ref[cols, :], preferred_element_type=jnp.float32)
        total = part if total is None else total + part
    h = x + total.astype(jnp.bfloat16).astype(jnp.float32)
    h_ref[...] = h
    hn_ref[...] = norm(h, g2_ref[...]).astype(jnp.bfloat16)

def mlp_forward_kernel(x, g1, g2, wg, wu, wd, tokens, blk=256, chunk=1024):
    depth = x.shape[1]
    width = wg.shape[1]
    row = lambda n: pl.BlockSpec((blk, n), lambda i: (i, 0))
    whole = lambda s: pl.BlockSpec(s, lambda i: (0, 0), pipeline_mode=pl.Buffered(1))
    shape = lambda n, t: jax.ShapeDtypeStruct((tokens, n), t)
    return pl.pallas_call(
        functools.partial(mlp_kernel, chunk),
        grid=(tokens // blk,),
        in_specs=[row(depth), whole((1, depth)), whole((1, depth)), whole(wg.shape), whole(wu.shape), whole(wd.shape)],
        out_specs=[row(depth), row(width), row(width), row(width), row(depth), row(depth)],
        out_shape=[shape(depth, jnp.bfloat16), shape(width, jnp.bfloat16), shape(width, jnp.bfloat16), shape(width, jnp.bfloat16), shape(depth, jnp.float32), shape(depth, jnp.bfloat16)],
        cost_estimate=pl.CostEstimate(flops=6 * tokens * width * depth, bytes_accessed=6 * tokens * width, transcendentals=tokens * width),
        compiler_params=pltpu.CompilerParams(vmem_limit_bytes=VMEM_LIMIT),
        name="mlp_forward",
    )(x, g1.reshape(1, -1), g2.reshape(1, -1), wg, wu, wd)

def dact_kernel(chunk, dm_ref, wd_ref, gt_ref, up_ref, dgt_ref, dup_ref):
    dm = dm_ref[...]
    for lo in range(0, gt_ref.shape[1], chunk):
        cols = slice(lo, lo + chunk)
        dq = lax.dot_general(dm, wd_ref[cols, :], NT, preferred_element_type=jnp.float32)
        gate = gt_ref[:, cols].astype(jnp.float32)
        up = up_ref[:, cols].astype(jnp.float32)
        sig = jax.nn.sigmoid(gate)
        dgt_ref[:, cols] = (dq * up * (sig * (1.0 + gate * (1.0 - sig)))).astype(jnp.bfloat16)
        dup_ref[:, cols] = (dq * (gate * sig)).astype(jnp.bfloat16)

def mlp_dact(dm, wd, gt, up, blk=256, chunk=1024):
    tokens, depth = dm.shape
    width = wd.shape[0]
    row = lambda n: pl.BlockSpec((blk, n), lambda i: (i, 0))
    return pl.pallas_call(
        functools.partial(dact_kernel, chunk),
        grid=(tokens // blk,),
        in_specs=[row(depth), pl.BlockSpec(wd.shape, lambda i: (0, 0), pipeline_mode=pl.Buffered(1)), row(width), row(width)],
        out_specs=[row(width), row(width)],
        out_shape=[jax.ShapeDtypeStruct((tokens, width), jnp.bfloat16)] * 2,
        cost_estimate=pl.CostEstimate(flops=2 * tokens * width * depth, bytes_accessed=8 * tokens * width, transcendentals=tokens * width),
        compiler_params=pltpu.CompilerParams(vmem_limit_bytes=VMEM_LIMIT),
        name="mlp_dact",
    )(dm, wd, gt, up)

def dweight_kernel(a_ref, b_ref, out_ref):
    out_ref[...] = lax.dot_general(a_ref[...], b_ref[...], TN, preferred_element_type=jnp.float32)

def dweight(a, b, rows, cols):
    tokens, m = a.shape
    n = b.shape[1]
    whole = pl.Buffered(1)
    a_spec = pl.BlockSpec((tokens, rows), lambda i, j: (0, i)) if rows < m else pl.BlockSpec((tokens, m), lambda i, j: (0, 0), pipeline_mode=whole)
    b_spec = pl.BlockSpec((tokens, cols), lambda i, j: (0, j)) if cols < n else pl.BlockSpec((tokens, n), lambda i, j: (0, 0), pipeline_mode=whole)
    return pl.pallas_call(
        dweight_kernel,
        grid=(m // rows, n // cols),
        in_specs=[a_spec, b_spec],
        out_specs=pl.BlockSpec((rows, cols), lambda i, j: (i, j)),
        out_shape=jax.ShapeDtypeStruct((m, n), jnp.float32),
        cost_estimate=pl.CostEstimate(flops=2 * tokens * m * n, bytes_accessed=2 * tokens * (m + n) + 4 * m * n, transcendentals=0),
        compiler_params=pltpu.CompilerParams(vmem_limit_bytes=VMEM_LIMIT),
        name="dweight",
    )(a, b)


def add_rows_kernel(bound_ref, ids_ref, base_ref, rows_ref, out_ref):
    tile = pl.program_id(0)
    out_ref[...] = base_ref[...]
    start = tile * out_ref.shape[0]
    for part in range(rows_ref.shape[0]):
        def body(t, carry, part=part):
            row = ids_ref[part, t] - start
            out_ref[pl.ds(row, 1), :] = out_ref[pl.ds(row, 1), :] + rows_ref[part, pl.ds(t, 1), :]
            return carry
        lax.fori_loop(bound_ref[part, tile], bound_ref[part, tile + 1], body, 0)


def add_rows(base, rows, ids, bounds, tile):
    vocab, depth = base.shape
    return pl.pallas_call(
        add_rows_kernel,
        grid_spec=pltpu.PrefetchScalarGridSpec(
            num_scalar_prefetch=2,
            grid=(vocab // tile,),
            in_specs=[
                pl.BlockSpec((tile, depth), lambda i, *_: (i, 0)),
                pl.BlockSpec(rows.shape, lambda i, *_: (0, 0, 0), pipeline_mode=pl.Buffered(1)),
            ],
            out_specs=pl.BlockSpec((tile, depth), lambda i, *_: (i, 0)),
        ),
        out_shape=jax.ShapeDtypeStruct(base.shape, base.dtype),
        input_output_aliases={2: 0},
        cost_estimate=pl.CostEstimate(flops=2 * vocab * depth, bytes_accessed=8 * vocab * depth, transcendentals=0),
        compiler_params=pltpu.CompilerParams(vmem_limit_bytes=VMEM_LIMIT),
        name="add_rows",
    )(bounds, ids, base, rows)


def place_kernel(start_ref, blocks_ref, out_ref, *scratch):
    rows = scratch[0] if scratch else out_ref
    blocks, cap, depth = blocks_ref.shape
    sub = lax.broadcasted_iota(jnp.int32, (8, depth), 0)
    for b in range(blocks):
        base = pl.multiple_of(start_ref[b] // 8 * 8, 8)
        shift = start_ref[b] % 8
        turned = pltpu.roll(blocks_ref[b].astype(jnp.float32), shift, 0)
        head = turned[:8]
        rows[pl.ds(base, 8), :] = jnp.where(sub < shift, rows[pl.ds(base, 8), :], head)
        rows[pl.ds(pl.multiple_of(base + 8, 8), cap - 8), :] = turned[8:]
        tail = pl.ds(pl.multiple_of(base + cap, 8), 8)
        rows[tail, :] = jnp.where(sub < shift, head, rows[tail, :])
    if scratch:
        out_ref[...] = rows[:out_ref.shape[0]].astype(out_ref.dtype)


def place_rows(blocks, starts, count, dtype):
    depth = blocks.shape[2]
    in_vmem = pl.BlockSpec(memory_space=pltpu.VMEM)
    return pl.pallas_call(
        place_kernel,
        in_specs=[pl.BlockSpec(memory_space=pltpu.SMEM), in_vmem],
        out_specs=in_vmem,
        out_shape=jax.ShapeDtypeStruct((count, depth), dtype),
        scratch_shapes=[] if dtype == jnp.float32 else [pltpu.VMEM((count + 8, depth), jnp.float32)],
        cost_estimate=pl.CostEstimate(flops=8 * count * depth, bytes_accessed=8 * count * depth, transcendentals=0),
        compiler_params=pltpu.CompilerParams(vmem_limit_bytes=VMEM_LIMIT),
        name="place_rows",
    )(starts, blocks)


def window_kernel(first_ref, a_ref, b_ref, out_ref, total_ref):
    count, depth = a_ref.shape
    windows, cap, _ = out_ref.shape
    total_ref[:count] = a_ref[...] + b_ref[...]
    for c in range(windows):
        base = pl.multiple_of(first_ref[c] // 8 * 8, 8)
        shift = first_ref[c] % 8
        piece = total_ref[pl.ds(base, cap + 8), :]
        out_ref[c] = pltpu.roll(piece, (cap + 8) - shift, 0)[:cap]


def sum_windows(a, b, first, cap):
    depth = a.shape[1]
    in_vmem = pl.BlockSpec(memory_space=pltpu.VMEM)
    return pl.pallas_call(
        window_kernel,
        in_specs=[pl.BlockSpec(memory_space=pltpu.SMEM), in_vmem, in_vmem],
        out_specs=in_vmem,
        out_shape=jax.ShapeDtypeStruct((first.shape[0], cap, depth), jnp.float32),
        scratch_shapes=[pltpu.VMEM((a.shape[0] + 8, depth), jnp.float32)],
        cost_estimate=pl.CostEstimate(flops=8 * a.size, bytes_accessed=12 * a.size, transcendentals=0),
        compiler_params=pltpu.CompilerParams(vmem_limit_bytes=VMEM_LIMIT),
        name="sum_windows",
    )(first, a, b)


def swap_cores(values):
    return lax.ppermute(values, "fsdp", [(0, 1), (1, 0)])


def fast_step(sorted_ids, sorted_labels, starts, sizes, table_shard, gate_shard, up_shard, down_shard, gain_in, gain_out):
    model_size, fsdp_size, dev_cap, chip_cap = sizes
    vocab, depth = table_shard.shape
    chip = lax.axis_index("model")
    core = lax.axis_index("fsdp")
    device = chip * fsdp_size + core
    count = sorted_ids.shape[1]
    num_tokens = count * fsdp_size
    own = lambda values: lax.dynamic_index_in_dim(values, core, 0, keepdims=False)
    other = lambda values: lax.dynamic_index_in_dim(values, 1 - core, 0, keepdims=False)

    w_gate = lax.all_gather(gate_shard, "fsdp", axis=0, tiled=True)
    w_up = lax.all_gather(up_shard, "fsdp", axis=0, tiled=True)
    with jax.named_scope("gather_rows"):
        slot = lax.dynamic_slice(starts, (0, device), (fsdp_size, 1)) + jnp.arange(dev_cap, dtype=jnp.int32)[None, :]
        wanted = jnp.take_along_axis(sorted_ids, jnp.minimum(slot, count - 1), axis=1) - device * vocab
        rows = jnp.take(table_shard, jnp.clip(wanted, 0, vocab - 1).reshape(-1), axis=0, mode="clip").reshape(fsdp_size, dev_cap, depth)
        theirs = swap_cores(other(rows))
        mine = own(rows)
        pair = jnp.where(core == 0, jnp.stack([mine, theirs]), jnp.stack([theirs, mine]))
        pair, w_gate, w_up = lax.optimization_barrier((pair, w_gate, w_up))
        blocks = lax.all_gather(pair, "model", axis=0, tiled=True)
        my_starts = own(starts)
        x_buf = place_rows(blocks, my_starts, count + dev_cap + 8, jnp.float32)
    w_down = lax.all_gather(down_shard, "fsdp", axis=0, tiled=True)

    normed_bf, gate_bf, up_bf, act_bf, h_res, hn_own = mlp_forward_kernel(x_buf, gain_in, gain_out, w_gate, w_up, w_down, count)
    hn_other = swap_cores(hn_own)
    local_labels = sorted_labels - device * vocab
    labels_own = own(local_labels)[:, None]
    labels_other = other(local_labels)[:, None]
    z_own, stat_own = head_logits(hn_own, table_shard, labels_own)
    z_other, stat_other = head_logits(hn_other, table_shard, labels_other)
    part_own = stat_own[:, :3].T
    part_other = stat_other[:, :3].T
    part = jnp.where(core == 0, jnp.stack([part_own, part_other]), jnp.stack([part_other, part_own]))
    all_stats = lax.all_gather(part.reshape(fsdp_size * 3, count), ("model", "fsdp"), axis=0).reshape(-1, fsdp_size, 3, count)
    row_max = jnp.max(all_stats[:, :, 0], axis=0)
    sum_exp = jnp.sum(all_stats[:, :, 1] * jnp.exp(all_stats[:, :, 0] - row_max[None]), axis=0)
    label_logit = jnp.sum(all_stats[:, :, 2], axis=0)
    loss = jnp.sum(row_max + jnp.log(sum_exp) - label_logit) / num_tokens
    lane = lax.broadcasted_iota(jnp.int32, (fsdp_size, count, LANES), 2)
    stats = jnp.where(lane == 0, row_max[:, :, None], (1.0 / sum_exp)[:, :, None])
    dz_other, d_hn_other = head_dlogits(z_other, table_shard, other(stats), labels_other, 1.0 / num_tokens)
    d_hn_theirs = swap_cores(d_hn_other)
    dz_own, d_hn_own = head_dlogits(z_own, table_shard, own(stats), labels_own, 1.0 / num_tokens)

    first = jnp.minimum(my_starts[0:model_size * fsdp_size:fsdp_size], count - chip_cap)
    windows = sum_windows(d_hn_own, d_hn_theirs, first, chip_cap)
    d_hn = lax.psum_scatter(windows.reshape(model_size * chip_cap, depth), "model", scatter_dimension=0, tiled=True)
    d_head = head_dtable(dz_own, hn_own, dz_other, hn_other)
    d_hn, d_head = lax.optimization_barrier((d_hn, d_head))
    my_first = lax.dynamic_index_in_dim(first, chip, 0, keepdims=False)
    h_window = lax.dynamic_slice(h_res, (my_first, 0), (chip_cap, depth))
    _, norm_out_back = jax.vjp(lambda values: rms_scale(values, gain_out), h_window)
    d_hidden = norm_out_back(d_hn)[0]
    dm_blocks = lax.all_gather(d_hidden.astype(jnp.bfloat16), "model", axis=0)
    d_mlp = place_rows(dm_blocks, first, count, jnp.bfloat16)

    d_gate, d_up = mlp_dact(d_mlp, w_down, gate_bf, up_bf)
    grad_down = jnp.einsum("tf,td->fd", act_bf, d_mlp, preferred_element_type=jnp.float32)
    grad_gate = jnp.einsum("td,tf->df", normed_bf, d_gate, preferred_element_type=jnp.float32)
    grad_up = jnp.einsum("td,tf->df", normed_bf, d_up, preferred_element_type=jnp.float32)
    d_gate_own = lax.dynamic_slice(d_gate, (my_first, 0), (chip_cap, d_gate.shape[1]))
    d_up_own = lax.dynamic_slice(d_up, (my_first, 0), (chip_cap, d_up.shape[1]))
    x_window = lax.dynamic_slice(x_buf, (my_first, 0), (chip_cap, depth))
    d_normed = jnp.einsum("tf,df->td", d_gate_own, w_gate, preferred_element_type=jnp.float32) + jnp.einsum("tf,df->td", d_up_own, w_up, preferred_element_type=jnp.float32)
    _, norm_in_back = jax.vjp(lambda values: rms_scale(values, gain_in), x_window)
    d_x = d_hidden + norm_in_back(d_normed)[0]
    d_x_theirs = swap_cores(d_x)
    d_x_pair = jnp.where(core == 0, jnp.stack([d_x, d_x_theirs]), jnp.stack([d_x_theirs, d_x]))

    tile = vocab // 6
    pair_first = jnp.minimum(lax.dynamic_index_in_dim(starts, chip * fsdp_size, 1, keepdims=False), count - chip_cap)
    own_ids = jnp.stack([lax.dynamic_slice(sorted_ids[p], (pair_first[p],), (chip_cap,)) for p in range(fsdp_size)]) - device * vocab
    edges = jnp.arange(vocab // tile + 1, dtype=jnp.int32) * tile
    bounds = jnp.sum((own_ids[:, :, None] < edges[None, None, :]).astype(jnp.int32), axis=1)
    grad_table = add_rows(d_head, d_x_pair, own_ids, bounds, tile)

    grad_gate = lax.psum_scatter(grad_gate, "fsdp", scatter_dimension=0, tiled=True)
    grad_up = lax.psum_scatter(grad_up, "fsdp", scatter_dimension=0, tiled=True)
    grad_down = lax.psum_scatter(grad_down, "fsdp", scatter_dimension=0, tiled=True)
    return loss, grad_table, grad_gate, grad_up, grad_down


def capacity(tokens, shares, lists):
    mean = tokens / shares
    return -(-int((mean + 4.5 * mean ** 0.5) / lists) // 16) * 16


def solution(mesh):
    fsdp_size = mesh.shape["fsdp"]
    model_size = mesh.shape["model"]
    tok_spec = P("fsdp", None)
    row_spec = P(("model", "fsdp"), None)
    weight_spec = P("fsdp", None)

    def device_step(tok_ids, tok_labels, table_shard, gate_shard, up_shard, down_shard, gain_in, gain_out):
        count = tok_ids.shape[0] * tok_ids.shape[1]
        vocab = table_shard.shape[0]
        devices = model_size * fsdp_size
        both = lax.all_gather(jnp.stack([tok_ids.reshape(-1), tok_labels.reshape(-1)]), "fsdp", axis=1, tiled=True)
        ids, labels = lax.sort((both[0], both[1]), num_keys=1)
        sorted_ids = ids.reshape(count, fsdp_size).T
        sorted_labels = labels.reshape(count, fsdp_size).T
        edges = jnp.arange(devices + 1, dtype=jnp.int32) * vocab
        starts = jnp.sum((sorted_ids[:, :, None] < edges[None, None, :]).astype(jnp.int32), axis=1)
        dev_cap = capacity(count * fsdp_size, devices, fsdp_size)
        chip_cap = capacity(count * fsdp_size, model_size, fsdp_size)
        dev_counts = starts[:, 1:] - starts[:, :-1]
        chip_starts = starts[:, ::fsdp_size]
        chip_counts = chip_starts[:, 1:] - chip_starts[:, :-1]
        fits = (jnp.max(dev_counts) <= dev_cap) & (jnp.max(chip_counts) <= chip_cap)
        weights = (table_shard, gate_shard, up_shard, down_shard, gain_in, gain_out)
        return lax.cond(
            fits,
            lambda: fast_step(sorted_ids, sorted_labels, starts, (model_size, fsdp_size, dev_cap, chip_cap), *weights),
            lambda: slow_step(tok_ids, tok_labels, *weights),
        )

    return jax.shard_map(device_step, mesh=mesh, in_specs=(tok_spec, tok_spec, row_spec, weight_spec, weight_spec, weight_spec, P(), P()), out_specs=(P(), row_spec, weight_spec, weight_spec, weight_spec), check_vma=False)
```

time: 1070 us -> 790 us (0.74)
  Pallas kernels: 0 us -> 411 us
  matrix products: 451 us -> 91.2 us
  waiting for transfers between devices: 359 us -> 165 us
  other arithmetic: 165 us -> 29.9 us
  loops' own time: 0 us -> 17.4 us
  blocking collectives: 27.4 us -> 15.9 us
    pallas_call x0 -> x11, Pallas kernels: none -> 411 us  [the longest x2 94.1 us: head_logits(): pl.pallas_call(functools.partial(logits_kernel, chunk), grid=(tokens // b...]
    dot_general x12 -> x5, matrix products: 451 us -> 91.2 us  [the longest x1 24.3 us: fast_step(): jnp.einsum('tf,td->fd', act_bf, d_mlp, preferred_element_type=jnp.float32)]
    psum x2 -> x0, waiting for transfers between devices: 251 us -> none  [the longest x1 160 us: device_step(): lax.psum(jnp.einsum('tv,vd->td', d_logits, table_part, preferred_element_...]
    all_gather x4 -> x5, waiting for transfers between devices: 60.1 us -> 136 us  [the longest x1 57.7 us: fast_step(): blocks = lax.all_gather(pair, 'model', axis=0, tiled=True)]
    scatter-add x1 -> x0, other arithmetic: 51.7 us -> none  [device_step(): jax.ops.segment_sum(jnp.where(id_inside[:, None], d_x, 0.0), safe_ids, nu...]
    convert_element_type x2 -> x1, other arithmetic: 55 us -> 4.08 us  [fast_step(): dm_blocks = lax.all_gather(d_hidden.astype(jnp.bfloat16), 'model', axis=0)]
    reduce_sum x3 -> x4, other arithmetic: 40.3 us -> 0.75 us  [the longest x1 0.35 us: device_step(): jnp.sum((sorted_ids[:, :, None] < edges[None, None, :]).astype(jnp.int32)...]
    reduce_scatter x4, waiting for transfers between devices: 45.5 us -> 25.3 us  [the longest x1 25.3 us: fast_step(): lax.psum_scatter(windows.reshape(model_size * chip_cap, depth), 'model',...]
  transfers between devices with their start and end apart: 10 -> 13, of which waited for: 5 -> 6; matrix products, arithmetic and copies ran while one was open for 28% -> 14% of each run, Pallas kernels for 0% -> 24%
where the time goes in v1:
time: 790 us; the launch traced here: 783 us
  Pallas kernels  411 us (52%)
  waiting for transfers between devices  165 us (21%)
  matrix products  91.2 us (12%)
  local copies, waits for them, and re-layouts  34 us (4%)
  other arithmetic  29.9 us (4%)
  loops' own time  17.4 us (2%)
  between operations  16.4 us (2%)
  blocking collectives  15.9 us (2%)
    pallas_call x2, Pallas kernels, head_logits(): pl.pallas_call(functools.partial(logits_kernel, chunk), grid=(tokens // b...  94.1 us
    pallas_call x2, Pallas kernels, head_dlogits(): pl.pallas_call(functools.partial(dlogits_kernel, inv_tokens, chunk), grid...  84.8 us
    pallas_call x1, Pallas kernels, mlp_forward_kernel(): pl.pallas_call(functools.partial(mlp_kernel, chunk), grid=(tokens // blk,...  69.7 us
    pallas_call x1, Pallas kernels, head_dtable(): pl.pallas_call(dhead_kernel, grid=(pl.cdiv(vocab, tile),), in_specs=[dz_s...  62.9 us
    all_gather x1, waiting for transfers between devices, fast_step(): blocks = lax.all_gather(pair, 'model', axis=0, tiled=True)  57.7 us
    all_gather x1, waiting for transfers between devices, fast_step(): dm_blocks = lax.all_gather(d_hidden.astype(jnp.bfloat16), 'model', axis=0)  52.2 us
    pallas_call x1, Pallas kernels, mlp_dact(): pl.pallas_call(functools.partial(dact_kernel, chunk), grid=(tokens // blk...  36.5 us
    reduce_scatter x1, waiting for transfers between devices, fast_step(): lax.psum_scatter(windows.reshape(model_size * chip_cap, depth), 'model',...  25.3 us
  transfers between devices with their start and end apart: 13, of which 6 were waited for; matrix products, arithmetic and copies ran while one was open for 14% of the time, Pallas kernels for 24%

profile of v1, /device:TPU:0, one launch (start us, length us, event | category | flops | bytes accessed | tf_op | source)
XLA Modules:
  0.0 782.7 jit_solution(15851919620125525426)
XLA Ops:
  7.2 0.7 pad_add_fusion
  7.9 2.3 all_gather.36
  10.3 5.9 sort.23
  16.2 1.0 reshape.335
  17.2 0.3 copy.72
  17.5 0.3 fusion.52
  17.9 0.6 fusion.53
  19.2 0.6 subtract_reduce_fusion.2
  20.5 2.0 reshape.336
  22.5 752.4 %conditional.1 = (f32[]{:T(128)}, f32[6288,1024]{1,0:T(8,128)}, f32[512,4096]{1,0:T(8,128)}, f32[512,4096]{1,0:T(8,128)}, f32[2048,1024]{1,0:T(8,128)}) conditional(s32[]{:T(128)} %convert_element_type.57, (s32[1,2048]{1,0:T(1,128)}, bf16[6288,1024]{1,0:T(8,128)(2,1)}, f32[1024]{0:T(1024)}, bf16[512,4096]{1,0:T(8,128)(2,1)}, ...), branch_computations={%region_4.23_spmd, %region_23.37_spmd} | conditional | flops 313584418816 | bytes 2052397440 | solution.py:506
  31.2 0.7 all-gather.19.cloned.1.call-update
  31.9 0.7 all-gather.21.cloned.1.call-update
  32.7 1.6 copy.73
  34.3 0.6 fusion.50
  35.3 5.7 gather_fusion.2
  41.1 10.2 %gather_fusion.1 = bf16[640,1024]{1,0:T(8,128)(2,1)S(1)} fusion(bf16[6288,1024]{1,0:T(8,128)(2,1)} %get-tuple-element.45.emb_ref, s32[1024]{0:T(1024)S(1)} %pad_clamp_fusion), kind=kCustom, calls=%fused_computation.1 | custom fusion | bytes 2624000 | tf_op jit(solution)/shard_map/cond/branch_1_fun/gather_rows/jit(_take)/gather | solution.py:408
  51.4 0.4 collective-permute-start
  51.8 2.7 collective-permute-done
  54.4 1.3 maximum_select_fusion.1
  55.7 19.0 %all-gather.21.cloned.1.call-done.wu_ref = bf16[1024,4096]{1,0:T(8,128)(2,1)} async-done(((bf16[512,4096]{1,0:T(8,128)(2,1)}), bf16[1024,4096]{1,0:T(8,128)(2,1)}) %all-gather.21.cloned.1.call-update) | async-done | bytes 8388624 | tf_op jit(solution)/shard_map/cond/branch_1_fun/all_gather | solution.py:404
  74.8 0.5 all-gather.25.cloned.1.call-update
  75.4 0.7 dynamic-slice_reduce_fusion.start_ref
  76.1 57.7 %all-gather.23.cloned.1.call-done.blocks_ref = bf16[8,320,1024]{2,1,0:T(8,128)(2,1)} async-done(((bf16[2,320,1024]{2,1,0:T(8,128)(2,1)}), bf16[8,320,1024]{2,1,0:T(8,128)(2,1)}) %all-gather.23.cloned.1.call-update) | async-done | bytes 5242896 | tf_op jit(solution)/shard_map/cond/branch_1_fun/gather_rows/all_gather | solution.py:413
  133.9 12.8 %place_rows.2.x_ref = f32[2376,1024]{1,0:T(8,128)} custom-call(s32[9]{0:T(128)} %dynamic-slice_reduce_fusion.start_ref, bf16[8,320,1024]{2,1,0:T(8,128)(2,1)} %all-gather.23.cloned.1.call-done.blocks_ref), custom_call_target="tpu_custom_call" | custom-call | flops 19464192 | bytes 19464192 | tf_op jit(solution)/shard_map/cond/branch_1_fun/gather_rows/place_rows/pallas_call | solution.py:350
  146.7 6.6 all-gather.25.cloned.1.call-done.wd_ref
  153.3 69.7 %mlp_forward.1 = (bf16[2048,1024]{1,0:T(8,128)(2,1)}, bf16[2048,4096]{1,0:T(8,128)(2,1)}, bf16[2048,4096]{1,0:T(8,128)(2,1)}, bf16[2048,4096]{1,0:T(8,128)(2,1)}...) custom-call(f32[2376,1024]{1,0:T(8,128)} %place_rows.2.x_ref, f32[1,1024]{1,0:T(1,128)S(1)} %bitcast.120, ...), custom_call_target="tpu_custom_call" | custom-call | flops 51539607552 | bytes 50331648 | tf_op jit(solution)/shard_map/cond/branch_1_fun/mlp_forward/pallas_call | solution.py:239
  223.2 1.6 copy.74
  224.8 1.3 copy.58.lab_ref
  226.2 1.3 copy.57.lab_ref
  227.5 46.9 %head_logits.2 = (f32[2048,6288]{1,0:T(8,128)}, f32[2048,128]{1,0:T(8,128)}) custom-call(bf16[2048,1024]{1,0:T(8,128)(2,1)} %get-tuple-element.55.hn_ref.ha_ref, bf16[6288,1024]{1,0:T(8,128)(2,1)} %get-tuple-element.45.emb_ref, s32[2048,1]{1,0:T(8,128)} %copy.57.lab_ref), custom_call_target="tpu_custom_call" | custom-call | flops 26373783552 | bytes 51511296 | tf_op jit(solution)/shard_map/cond/branch_1_fun/head_logits/pallas_call | solution.py:131
  274.4 1.3 slice_bitcast_fusion.1
  275.7 0.3 copy.59
  276.1 47.1 %head_logits.3 = (f32[2048,6288]{1,0:T(8,128)}, f32[2048,128]{1,0:T(8,128)}) custom-call(bf16[2048,1024]{1,0:T(8,128)(2,1)} %collective-permute-done.1.hn_ref.hb_ref, bf16[6288,1024]{1,0:T(8,128)(2,1)} %get-tuple-element.45.emb_ref, s32[2048,1]{1,0:T(8,128)} %copy.58.lab_ref), custom_call_target="tpu_custom_call" | custom-call | flops 26373783552 | bytes 51511296 | tf_op jit(solution)/shard_map/cond/branch_1_fun/head_logits/pallas_call | solution.py:131
  323.2 1.3 slice_bitcast_fusion
  324.5 0.3 copy.60
  325.0 13.6 %all_gather.32 = f32[8,6,2048]{2,1,0:T(8,128)S(1)} all-gather(f32[1,6,2048]{2,1,0:T(8,128)S(1)} %select_n.156), channel_id=1, replica_groups=mesh['model'=4,'fsdp'=2] {'model','fsdp'}, dimensions={0}, use_global_device_ids=true | all-gather | bytes 442368 | tf_op jit(solution)/shard_map/cond/branch_1_fun/all_gather | solution.py:428
  339.0 0.6 broadcast_divide_fusion
  339.6 1.1 broadcast_select_fusion
  340.7 1.5 dynamic-slice_bitcast_fusion
  342.2 42.3 %head_dlogits.3 = (bf16[2048,6288]{1,0:T(8,128)(2,1)}, f32[2048,1024]{1,0:T(8,128)}) custom-call(f32[2048,6288]{1,0:T(8,128)} %get-tuple-element.61.z_ref, bf16[6288,1024]{1,0:T(8,128)(2,1)} %get-tuple-element.45.emb_ref, f32[2048,128]{1,0:T(8,128)} %get-tuple-element.124.stat_ref, s32[2048,1]{1,0:T(8,128)} %copy.58.lab_ref), custom_call_target="tpu_custom_call" | custom-call | flops 26373783552 | bytes 77266944 | tf_op jit(solution)/shard_map/cond/branch_1_fun/head_dlogits/pallas_call | solution.py:168
  384.6 0.5 broadcast_minimum_fusion.first_ref.start_ref
  385.1 42.5 %head_dlogits.2 = (bf16[2048,6288]{1,0:T(8,128)(2,1)}, f32[2048,1024]{1,0:T(8,128)}) custom-call(f32[2048,6288]{1,0:T(8,128)} %get-tuple-element.59.z_ref, bf16[6288,1024]{1,0:T(8,128)(2,1)} %get-tuple-element.45.emb_ref, f32[2048,128]{1,0:T(8,128)} %get-tuple-element.125.stat_ref, s32[2048,1]{1,0:T(8,128)} %copy.57.lab_ref), custom_call_target="tpu_custom_call" | custom-call | flops 26373783552 | bytes 77266944 | tf_op jit(solution)/shard_map/cond/branch_1_fun/head_dlogits/pallas_call | solution.py:168
  427.6 16.6 %sum_windows.1 = f32[4,592,1024]{2,1,0:T(8,128)} custom-call(s32[4]{0:T(128)} %broadcast_minimum_fusion.first_ref.start_ref, f32[2048,1024]{1,0:T(8,128)} %get-tuple-element.60.a_ref, f32[2048,1024]{1,0:T(8,128)} %collective-permute-done.2.b_ref), custom_call_target="tpu_custom_call" | custom-call | flops 16777216 | bytes 25165824 | tf_op jit(solution)/shard_map/cond/branch_1_fun/sum_windows/pallas_call | solution.py:376
  444.3 0.6 copy-done.43
  444.9 0.7 dynamic_slice.49
  447.6 62.9 %head_dtable.1.base_ref = f32[6288,1024]{1,0:T(8,128)} custom-call(bf16[2048,6288]{1,0:T(8,128)(2,1)} %get-tuple-element.63.a_ref, bf16[2048,1024]{1,0:T(8,128)(2,1)} %get-tuple-element.55.hn_ref.ha_ref, bf16[2048,6288]{1,0:T(8,128)(2,1)} %get-tuple-element.64.b_ref, bf16[2048,1024]{1,0:T(8,128)(2,1)} %collective-permute-done.1.hn_ref.hb_ref), custom_call_target="tpu_custom_call" | custom-call | flops 52747567104 | bytes 77266944 | tf_op jit(solution)/shard_map/cond/branch_1_fun/head_dtable/pallas_call | solution.py:199
  510.5 25.3 %reduce-scatter.17.cloned.1.call-done = f32[592,1024]{1,0:T(8,128)} async-done(((f32[2368,1024]{1,0:T(8,128)}), f32[592,1024]{1,0:T(8,128)}) %reduce-scatter.17.cloned.1.call-update) | async-done | bytes 2424848 | tf_op jit(solution)/shard_map/cond/branch_1_fun/reduce_scatter | solution.py:441
  535.8 3.1 multiply_reduce_fusion.5
  538.9 4.1 fusion.51
  543.0 0.3 reduce-scatter.19.cloned.1.call-start
  543.3 52.2 %all-gather.27.cloned.1.call-done = bf16[2368,1024]{1,0:T(8,128)(2,1)} async-done(((bf16[592,1024]{1,0:T(8,128)(2,1)}), bf16[2368,1024]{1,0:T(8,128)(2,1)}) %all-gather.27.cloned.1.call-update) | async-done | bytes 4849680 | tf_op jit(solution)/shard_map/cond/branch_1_fun/all_gather | solution.py:448
  595.4 12.0 %place_rows.3.dm_ref = bf16[2048,1024]{1,0:T(8,128)(2,1)} custom-call(s32[4]{0:T(128)} %broadcast_minimum_fusion.first_ref.start_ref, bf16[4,592,1024]{2,1,0:T(8,128)(2,1)} %bitcast.101), custom_call_target="tpu_custom_call" | custom-call | flops 16777216 | bytes 16777216 | tf_op jit(solution)/shard_map/cond/branch_1_fun/place_rows/pallas_call | solution.py:350
  607.5 36.5 %mlp_dact.1 = (bf16[2048,4096]{1,0:T(8,128)(2,1)}, bf16[2048,4096]{1,0:T(8,128)(2,1)}) custom-call(bf16[2048,1024]{1,0:T(8,128)(2,1)} %place_rows.3.dm_ref, bf16[4096,1024]{1,0:T(8,128)(2,1)} %all-gather.25.cloned.1.call-done.wd_ref, bf16[2048,4096]{1,0:T(8,128)(2,1)} %get-tuple-element.68.gt_ref, bf16[2048,4096]{1,0:T(8,128)(2,1)} %get-tuple-element.69.up_ref), custom_call_target="tpu_custom_call" | custom-call | flops 17179869184 | bytes 67108864 | tf_op jit(solution)/shard_map/cond/branch_1_fun/mlp_dact/pallas_call | solution.py:265
  643.9 23.7 %fusion.59 = f32[1024,4096]{1,0:T(8,128)} fusion(bf16[2048,1024]{1,0:T(8,128)(2,1)} %get-tuple-element.72, bf16[2048,4096]{1,0:T(8,128)(2,1)} %get-tuple-element.70), kind=kOutput, calls=%fused_computation.146 | convolution fusion | flops 17179869184 | bytes 37748736 | tf_op jit(solution)/shard_map/cond/branch_1_fun/td,tf->df/dot_general | solution.py:453
  667.7 23.8 %fusion.60 = f32[1024,4096]{1,0:T(8,128)} fusion(bf16[2048,1024]{1,0:T(8,128)(2,1)} %get-tuple-element.72, bf16[2048,4096]{1,0:T(8,128)(2,1)} %get-tuple-element.71), kind=kOutput, calls=%fused_computation.147 | convolution fusion | flops 17179869184 | bytes 37748736 | tf_op jit(solution)/shard_map/cond/branch_1_fun/td,tf->df/dot_general | solution.py:454
  691.6 24.3 %fusion.61 = f32[4096,1024]{1,0:T(8,128)} fusion(bf16[2048,4096]{1,0:T(8,128)(2,1)} %get-tuple-element.73, bf16[2048,1024]{1,0:T(8,128)(2,1)} %place_rows.3.dm_ref), kind=kOutput, calls=%fused_computation.148 | convolution fusion | flops 17179869184 | bytes 37748736 | tf_op jit(solution)/shard_map/cond/branch_1_fun/tf,td->fd/dot_general | solution.py:452
  717.2 9.1 %fusion.31 = f32[592,1024]{1,0:T(8,128)S(1)} fusion(bf16[1024,4096]{1,0:T(8,128)(2,1)} %all-gather.21.cloned.1.call-done.wu_ref, bf16[2048,4096]{1,0:T(8,128)(2,1)} %get-tuple-element.71, s32[]{:T(128)S(6)} %select_n.163), kind=kOutput, calls=%fused_computation.71 | convolution fusion | flops 4966055936 | bytes 15663108 | tf_op jit(solution)/shard_map/cond/branch_1_fun/tf,df->td/dot_general | solution.py:458
  726.4 10.3 %multiply_reduce_fusion.3 = (f32[592]{0:T(1024)S(1)}, f32[592]{0:T(1024)S(1)}, f32[592,1024]{1,0:T(8,128)S(1)}) fusion(f32[2376,1024]{1,0:T(8,128)} %place_rows.2.x_ref, s32[]{:T(128)S(6)} %select_n.164, f32[1024]{0:T(1024)S(1)} %copy-done.49, f32[592,1024]{1,0:T(8,128)S(1)} %fusion.31, bf16[1024,4096]{1,0:T(8,128)(2,1)} %all-gather.19.cloned.1.call-done.wg_ref, ...), kind=kOutput, calls=%fused_computation.79 | convolution fusion | flops 4969692160 | bytes 20521608 | tf_op jit(solution)/shard_map/cond/branch_1_fun/tf,df->td/dot_general | solution.py:458
  736.8 3.7 fusion.35
  740.5 0.7 fusion.55
  745.3 0.3 fusion.41
  745.6 0.7 copy.68.bound_ref
  746.9 6.0 maximum_select_fusion.rows_ref
  752.9 21.7 %add_rows.1 = f32[6288,1024]{1,0:T(8,128)} custom-call(s32[2,7]{1,0:T(2,128)} %copy.68.bound_ref, s32[2,592]{1,0:T(2,128)} %copy-done.30, f32[6288,1024]{1,0:T(8,128)} %head_dtable.1.base_ref, f32[2,592,1024]{2,1,0:T(8,128)} %maximum_select_fusion.rows_ref), custom_call_target="tpu_custom_call", output_to_operand_aliasing={{}: (2, {})} | custom-call | flops 12877824 | bytes 51511296 | tf_op jit(solution)/shard_map/cond/branch_1_fun/add_rows/pallas_call | solution.py:311
  (81 shorter events, 2.2 us)
Async XLA Ops:
  31.1 1.6 copy-start.9
  31.2 9.9 %copy-start.17 = (s32[2,9]{0,1:T(8,128)}, s32[2,9]{0,1:T(8,128)S(1)}, u32[]{:S(2)}) copy-start(s32[2,9]{0,1:T(8,128)S(1)} %get-tuple-element.44) | copy-start | bytes 220 | tf_op jit(solution)/shard_map/cond
  31.2 24.5 %all-gather.19.cloned.1.call-start = ((), (), s32[]{:S(2)}) async-start(), calls=%async_computation.18 | async-start | bytes 12582912 | tf_op jit(solution)/shard_map/cond/branch_1_fun/all_gather | solution.py:403
  31.9 42.8 %all-gather.21.cloned.1.call-start = ((), (), s32[]{:S(2)}) async-start(), calls=%async_computation.19 | async-start | bytes 12582912 | tf_op jit(solution)/shard_map/cond/branch_1_fun/all_gather | solution.py:404
  32.7 101.2 %all-gather.23.cloned.1.call-start = ((), (), s32[]{:S(2)}) async-start(), calls=%async_computation.20 | async-start | bytes 6553600 | tf_op jit(solution)/shard_map/cond/branch_1_fun/gather_rows/all_gather | solution.py:413
  34.3 17.1 %copy-start = (s32[2,2048]{1,0:T(2,128)}, s32[2,2048]{1,0:T(2,128)S(1)}, u32[]{:S(2)}) copy-start(s32[2,2048]{1,0:T(2,128)S(1)} %copy.73) | copy-start | bytes 49156 | tf_op jit(solution)/shard_map/cond
  41.0 34.4 %copy-start.18 = (s32[2,9]{0,1:T(8,128)S(1)}, s32[2,9]{0,1:T(8,128)}, u32[]{:S(2)}) copy-start(s32[2,9]{0,1:T(8,128)} %copy-done.17) | copy-start | bytes 220 | tf_op jit(solution)/shard_map/cond
  51.4 3.1 collective-permute-start
  74.8 78.5 %all-gather.25.cloned.1.call-start = ((), (), s32[]{:S(2)}) async-start(), calls=%async_computation.21 | async-start | bytes 12582912 | tf_op jit(solution)/shard_map/cond/branch_1_fun/all_gather | solution.py:416
  75.3 77.9 %copy-start.13 = (f32[1024]{0:T(1024)S(1)}, f32[1024]{0:T(1024)}, u32[]{:S(2)}) copy-start(f32[1024]{0:T(1024)} %get-tuple-element.51) | copy-start | bytes 12292 | tf_op jit(solution)/shard_map/cond
  75.4 77.9 %copy-start.48 = (f32[1024]{0:T(1024)S(1)}, f32[1024]{0:T(1024)}, u32[]{:S(2)}) copy-start(f32[1024]{0:T(1024)} %get-tuple-element.50) | copy-start | bytes 12292 | tf_op jit(solution)/shard_map/cond
  75.4 460.4 %reduce-scatter.17.cloned.1.call-start = ((), (), s32[]{:S(2)}) async-start(), calls=%async_computation.22 | async-start | bytes 12124160 | tf_op jit(solution)/shard_map/cond/branch_1_fun/reduce_scatter | solution.py:441
  223.0 53.1 %collective-permute-start.1 = (bf16[2048,1024]{1,0:T(8,128)(2,1)}, bf16[2048,1024]{1,0:T(8,128)(2,1)}, u32[]{:S(2)}, u32[]{:S(2)}) collective-permute-start(bf16[2048,1024]{1,0:T(8,128)(2,1)} %get-tuple-element.55.hn_ref.ha_ref), channel_id=1, source_target_pairs={{0,1},{1,0},{2,3},{3,2},{4,5},{5,4},{6,7},{7,6}} | collective-permute-start | bytes 12582920 | tf_op jit(solution)/shard_map/cond/branch_1_fun/ppermute | solution.py:389
  342.2 42.3 %copy-start.44 = (s32[9]{0:T(128)S(1)}, s32[9]{0:T(128)}, u32[]{:S(2)}) copy-start(s32[9]{0:T(128)} %dynamic-slice_reduce_fusion.start_ref) | copy-start | bytes 112 | tf_op jit(solution)/shard_map/cond
  384.5 43.1 %collective-permute-start.2 = (f32[2048,1024]{1,0:T(8,128)}, f32[2048,1024]{1,0:T(8,128)}, u32[]{:S(2)}, u32[]{:S(2)}) collective-permute-start(f32[2048,1024]{1,0:T(8,128)} %get-tuple-element.62), channel_id=1, source_target_pairs={{0,1},{1,0},{2,3},{3,2},{4,5},{5,4},{6,7},{7,6}} | collective-permute-start | bytes 25165832 | tf_op jit(solution)/shard_map/cond/branch_1_fun/ppermute | solution.py:389
  444.2 0.7 copy-start.43
  444.2 151.2 %all-gather.27.cloned.1.call-start = ((), (), s32[]{:S(2)}) async-start(), calls=%async_computation.26 | async-start | bytes 6062080 | tf_op jit(solution)/shard_map/cond/branch_1_fun/all_gather | solution.py:448
  447.6 88.2 %copy-start.14 = (f32[1024]{0:T(1024)S(1)}, f32[1024]{0:T(1024)}, u32[]{:S(2)}) copy-start(f32[1024]{0:T(1024)} %get-tuple-element.51) | copy-start | bytes 12292 | tf_op jit(solution)/shard_map/cond
  543.0 231.6 %reduce-scatter.19.cloned.1.call-start = ((), (), s32[]{:S(2)}) async-start(), calls=%async_computation.23 | async-start | bytes 25165824 | tf_op jit(solution)/shard_map/cond/branch_1_fun/reduce_scatter | solution.py:471
  667.7 106.9 %reduce-scatter.21.cloned.1.call-start = ((), (), s32[]{:S(2)}) async-start(), calls=%async_computation.24 | async-start | bytes 25165824 | tf_op jit(solution)/shard_map/cond/branch_1_fun/reduce_scatter | solution.py:472
  691.5 83.1 %reduce-scatter.23.cloned.1.call-start = ((), (), s32[]{:S(2)}) async-start(), calls=%async_computation.25 | async-start | bytes 25165824 | tf_op jit(solution)/shard_map/cond/branch_1_fun/reduce_scatter | solution.py:473
  717.2 9.2 %copy-start.49 = (f32[1024]{0:T(1024)S(1)}, f32[1024]{0:T(1024)}, u32[]{:S(2)}) copy-start(f32[1024]{0:T(1024)} %get-tuple-element.50) | copy-start | bytes 12292 | tf_op jit(solution)/shard_map/cond
  726.4 10.4 %copy-start.8 = (f32[592,1024]{1,0:T(8,128)S(1)}, f32[592,1024]{1,0:T(8,128)}, u32[]{:S(2)}) copy-start(f32[592,1024]{1,0:T(8,128)} %reduce-scatter.17.cloned.1.call-done) | copy-start | bytes 7274500 | tf_op jit(solution)/shard_map/cond
  736.8 3.7 copy-start.42
  736.8 8.4 %copy-start.1 = (s32[2,2048]{1,0:T(2,128)S(1)}, s32[2,2048]{1,0:T(2,128)}, u32[]{:S(2)}) copy-start(s32[2,2048]{1,0:T(2,128)} %copy-done) | copy-start | bytes 49156 | tf_op jit(solution)/shard_map/cond
  740.5 6.4 collective-permute-start.3
  745.3 7.5 copy-start.30
Sparse Core Ops, SparseCore 0:
  33.5 21.2 all-gather.18
  56.3 18.3 all-gather.20
  77.1 56.7 all-gather.22
  135.2 18.0 all-gather.24
  444.4 91.3 reduce-scatter.16
  543.1 52.2 all-gather.26
  667.8 21.8 reduce-scatter.18
  692.5 22.9 reduce-scatter.20
  718.3 22.9 reduce-scatter.22

commit v2 on v1

v2 whole, which is shorter than its diff:
```python
import functools

import jax
import jax.numpy as jnp
from jax import lax
from jax.experimental import pallas as pl
from jax.experimental.pallas import tpu as pltpu
from jax.sharding import PartitionSpec as P

EPS = 1e-6
VMEM_LIMIT = 63 * 1024 * 1024
LANES = 128
TN = (((0,), (0,)), ((), ()))
NT = (((1,), (1,)), ((), ()))


def rms_scale(values, gain_vec):
    mean_sq = jnp.mean(values * values, axis=-1, keepdims=True)
    return values * lax.rsqrt(mean_sq + EPS) * gain_vec


def mlp_forward(x_emb, gain_in, w_gate, w_up, w_down):
    normed_in, norm_in_back = jax.vjp(lambda values: rms_scale(values, gain_in), x_emb)
    normed_bf = normed_in.astype(jnp.bfloat16)
    gate_f = jnp.dot(normed_bf, w_gate, preferred_element_type=jnp.float32).astype(jnp.bfloat16).astype(jnp.float32)
    up_f = jnp.dot(normed_bf, w_up, preferred_element_type=jnp.float32).astype(jnp.bfloat16).astype(jnp.float32)
    gate_sig = jax.nn.sigmoid(gate_f)
    silu_gate = gate_f * gate_sig
    act_bf = (silu_gate * up_f).astype(jnp.bfloat16)
    mlp_out = jnp.dot(act_bf, w_down, preferred_element_type=jnp.float32).astype(jnp.bfloat16)
    h_res = x_emb + mlp_out.astype(jnp.float32)
    return h_res, (norm_in_back, normed_bf, gate_f, up_f, gate_sig, silu_gate, act_bf)


def mlp_backward(d_hidden, saved, w_gate, w_up, w_down):
    norm_in_back, normed_bf, gate_f, up_f, gate_sig, silu_gate, act_bf = saved
    d_mlp = d_hidden.astype(jnp.bfloat16)
    d_act = jnp.einsum("td,fd->tf", d_mlp, w_down, preferred_element_type=jnp.float32)
    grad_down = jnp.einsum("tf,td->fd", act_bf, d_mlp, preferred_element_type=jnp.float32)
    d_gate = (d_act * up_f * (gate_sig * (1.0 + gate_f * (1.0 - gate_sig)))).astype(jnp.bfloat16)
    d_up = (d_act * silu_gate).astype(jnp.bfloat16)
    grad_gate = jnp.einsum("td,tf->df", normed_bf, d_gate, preferred_element_type=jnp.float32)
    grad_up = jnp.einsum("td,tf->df", normed_bf, d_up, preferred_element_type=jnp.float32)
    d_normed = jnp.einsum("tf,df->td", d_gate, w_gate, preferred_element_type=jnp.float32) + jnp.einsum("tf,df->td", d_up, w_up, preferred_element_type=jnp.float32)
    d_x = d_hidden + norm_in_back(d_normed)[0]
    return d_x, grad_gate, grad_up, grad_down


def slow_step(tok_ids, tok_labels, halves, table_shard, gain_in, gain_out):
    fsdp_size = lax.axis_size("fsdp")
    local_count = tok_ids.shape[0] * tok_ids.shape[1]
    num_tokens = local_count * fsdp_size
    table_part = lax.all_gather(table_shard, "fsdp", axis=0, tiled=True)
    w_gate, w_up, w_down = (by_core(lax.axis_index("fsdp"), mine, theirs) for mine, theirs in halves)
    vocab_part = table_part.shape[0]
    vocab_start = lax.axis_index("model") * vocab_part
    local_ids = tok_ids.reshape(local_count) - vocab_start
    id_inside = (local_ids >= 0) & (local_ids < vocab_part)
    safe_ids = jnp.where(id_inside, local_ids, 0)
    emb_rows = jnp.where(id_inside[:, None], jnp.take(table_part, safe_ids, axis=0), 0)
    x_emb = lax.psum(emb_rows, "model").astype(jnp.float32)
    h_res, saved = mlp_forward(x_emb, gain_in, w_gate, w_up, w_down)
    hn_f, norm_out_back = jax.vjp(lambda values: rms_scale(values, gain_out), h_res)
    hn_bf = hn_f.astype(jnp.bfloat16)
    logits = jnp.einsum("td,vd->tv", hn_bf, table_part, preferred_element_type=jnp.float32)
    row_max = lax.pmax(jnp.max(logits, axis=-1), "model")
    exp_shift = jnp.exp(logits - row_max[:, None])
    local_labels = tok_labels.reshape(local_count) - vocab_start
    onehot = lax.broadcasted_iota(jnp.int32, logits.shape, 1) == local_labels[:, None]
    part_stats = jnp.stack([jnp.sum(exp_shift, axis=-1), jnp.sum(jnp.where(onehot, logits, 0.0), axis=-1)])
    tok_stats = lax.psum(part_stats, "model")
    sum_exp = tok_stats[0]
    tok_loss = row_max + jnp.log(sum_exp) - tok_stats[1]
    loss = lax.psum(jnp.sum(tok_loss), "fsdp") / num_tokens
    soft_probs = exp_shift / sum_exp[:, None]
    d_logits = (jnp.where(onehot, soft_probs - 1.0, soft_probs) / num_tokens).astype(jnp.bfloat16)
    d_head = jnp.einsum("tv,td->vd", d_logits, hn_bf, preferred_element_type=jnp.float32)
    d_hn = lax.psum(jnp.einsum("tv,vd->td", d_logits, table_part, preferred_element_type=jnp.float32), "model")
    d_hidden = norm_out_back(d_hn)[0]
    d_x, grad_gate, grad_up, grad_down = mlp_backward(d_hidden, saved, w_gate, w_up, w_down)
    d_in = jax.ops.segment_sum(jnp.where(id_inside[:, None], d_x, 0.0), safe_ids, num_segments=vocab_part)
    grad_table = lax.psum_scatter(d_head + d_in, "fsdp", scatter_dimension=0, tiled=True)
    grad_gate = lax.psum_scatter(grad_gate, "fsdp", scatter_dimension=0, tiled=True)
    grad_up = lax.psum_scatter(grad_up, "fsdp", scatter_dimension=0, tiled=True)
    grad_down = lax.psum_scatter(grad_down, "fsdp", scatter_dimension=0, tiled=True)
    return loss, grad_table, grad_gate, grad_up, grad_down


def lane_chunks(width, chunk):
    return [(lo, min(chunk, width - lo)) for lo in range(0, width, chunk)]

def logits_kernel(chunk, hn_ref, emb_ref, off_ref, z_ref, stat_ref):
    rows, vocab = z_ref.shape
    hn = hn_ref[...]
    off = off_ref[...]
    lane = lax.broadcasted_iota(jnp.int32, (rows, LANES), 1)
    run_max = jnp.full((rows, LANES), -jnp.inf, jnp.float32)
    run_sum = jnp.zeros((rows, LANES), jnp.float32)
    run_lab = jnp.zeros((rows, LANES), jnp.float32)
    for lo, width in lane_chunks(vocab, chunk):
        z = lax.dot_general(hn, emb_ref[lo:lo + width, :], NT, preferred_element_type=jnp.float32)
        z_ref[:, lo:lo + width] = z
        groups = width // LANES
        parts = [z[:, g * LANES:(g + 1) * LANES] for g in range(groups)]
        if width % LANES:
            short = width % LANES
            filler = jnp.full((rows, LANES - short), -jnp.inf, jnp.float32)
            parts.append(jnp.concatenate([z[:, groups * LANES:], filler], axis=1))
        new_max = run_max
        for g, part in enumerate(parts):
            new_max = jnp.maximum(new_max, part)
            run_lab = jnp.where(off == -(lo + g * LANES), part, run_lab)
        run_sum = run_sum * jnp.exp(run_max - new_max)
        for part in parts:
            run_sum = run_sum + jnp.exp(part - new_max)
        run_max = new_max
    row_max = jnp.max(run_max, axis=1, keepdims=True)
    row_sum = jnp.sum(run_sum * jnp.exp(run_max - row_max), axis=1, keepdims=True)
    row_lab = jnp.sum(run_lab, axis=1, keepdims=True)
    stat_ref[...] = jnp.where(lane == 0, row_max, jnp.where(lane == 1, row_sum, row_lab))


def head_logits(hn, table, off, blk=256, chunk=1024):
    tokens, depth = hn.shape
    vocab = table.shape[0]
    return pl.pallas_call(
        functools.partial(logits_kernel, chunk),
        grid=(tokens // blk,),
        in_specs=[
            pl.BlockSpec((blk, depth), lambda i: (i, 0)),
            pl.BlockSpec((vocab, depth), lambda i: (0, 0), pipeline_mode=pl.Buffered(1)),
            pl.BlockSpec((blk, LANES), lambda i: (i, 0)),
        ],
        out_specs=[
            pl.BlockSpec((blk, vocab), lambda i: (i, 0)),
            pl.BlockSpec((blk, LANES), lambda i: (i, 0)),
        ],
        out_shape=[jax.ShapeDtypeStruct((tokens, vocab), jnp.float32), jax.ShapeDtypeStruct((tokens, LANES), jnp.float32)],
        cost_estimate=pl.CostEstimate(flops=2 * tokens * vocab * depth, bytes_accessed=4 * tokens * vocab, transcendentals=tokens * vocab),
        compiler_params=pltpu.CompilerParams(vmem_limit_bytes=VMEM_LIMIT),
        name="head_logits",
    )(hn, table, off)


def dlogits_kernel(inv_tokens, chunk, z_ref, emb_ref, max_ref, scale_ref, off_ref, dz_ref, dhn_ref):
    vocab = z_ref.shape[1]
    row_max = max_ref[...]
    scale = scale_ref[...]
    off = off_ref[...]
    total = None
    for lo, width in lane_chunks(vocab, chunk):
        for g in range(0, width, LANES):
            lanes = min(LANES, width - g)
            cols = slice(lo + g, lo + g + lanes)
            grad = jnp.exp(z_ref[:, cols] - row_max[:, :lanes]) * scale[:, :lanes]
            grad = jnp.where(off[:, :lanes] == -(lo + g), grad - inv_tokens, grad)
            dz_ref[:, cols] = grad.astype(jnp.bfloat16)
        part = jnp.dot(dz_ref[:, lo:lo + width], emb_ref[lo:lo + width, :], preferred_element_type=jnp.float32)
        total = part if total is None else total + part
    dhn_ref[...] = total


def head_dlogits(z, table, row_max, scale, off, inv_tokens, cols, blk=512, chunk=1024):
    tokens, vocab = z.shape
    row = pl.BlockSpec((blk, LANES), lambda i: (i, 0))
    return pl.pallas_call(
        functools.partial(dlogits_kernel, inv_tokens, chunk),
        grid=(tokens // blk,),
        in_specs=[
            pl.BlockSpec((blk, vocab), lambda i: (i, 0)),
            pl.BlockSpec((vocab, cols), lambda i: (0, 0), pipeline_mode=pl.Buffered(1)),
            row,
            row,
            row,
        ],
        out_specs=[
            pl.BlockSpec((blk, vocab), lambda i: (i, 0)),
            pl.BlockSpec((blk, cols), lambda i: (i, 0)),
        ],
        out_shape=[jax.ShapeDtypeStruct((tokens, vocab), jnp.bfloat16), jax.ShapeDtypeStruct((tokens, cols), jnp.float32)],
        cost_estimate=pl.CostEstimate(flops=2 * tokens * vocab * cols, bytes_accessed=6 * tokens * vocab, transcendentals=tokens * vocab),
        compiler_params=pltpu.CompilerParams(vmem_limit_bytes=VMEM_LIMIT),
        name="head_dlogits",
    )(z, table, row_max, scale, off)


def dhn_kernel(dz_ref, emb_ref, dhn_ref):
    dhn_ref[...] = jnp.dot(dz_ref[...], emb_ref[...], preferred_element_type=jnp.float32)


def head_dhn(dz, table, cols, index, blk=512):
    tokens, vocab = dz.shape
    return pl.pallas_call(
        dhn_kernel,
        grid=(tokens // blk,),
        in_specs=[
            pl.BlockSpec((blk, vocab), lambda i: (i, 0)),
            pl.BlockSpec((vocab, cols), lambda i: (0, index), pipeline_mode=pl.Buffered(1)),
        ],
        out_specs=pl.BlockSpec((blk, cols), lambda i: (i, 0)),
        out_shape=jax.ShapeDtypeStruct((tokens, cols), jnp.float32),
        cost_estimate=pl.CostEstimate(flops=2 * tokens * vocab * cols, bytes_accessed=2 * tokens * vocab, transcendentals=0),
        compiler_params=pltpu.CompilerParams(vmem_limit_bytes=VMEM_LIMIT),
        name="head_dhn",
    )(dz, table)


def dtable_kernel(a_ref, ha_ref, b_ref, hb_ref, *refs):
    out_ref = refs[-1]
    out_ref[...] = (lax.dot_general(a_ref[...], ha_ref[...], TN, preferred_element_type=jnp.float32)
                    + lax.dot_general(b_ref[...], hb_ref[...], TN, preferred_element_type=jnp.float32))


def head_dtable(dz_a, hn_a, dz_b, hn_b, partial, tile=640, early=0.7):
    tokens, vocab = dz_a.shape
    depth = hn_a.shape[1]
    tiles = pl.cdiv(vocab, tile)
    split = int(early * tiles)
    start, steps = (0, split) if partial is None else (split, tiles - split)
    dz_spec = pl.BlockSpec((tokens, tile), lambda i: (0, i + start))
    hn_spec = pl.BlockSpec((tokens, depth), lambda i: (0, 0), pipeline_mode=pl.Buffered(1))
    rest = () if partial is None else (partial,)
    return pl.pallas_call(
        dtable_kernel,
        grid=(steps,),
        in_specs=[dz_spec, hn_spec, dz_spec, hn_spec] + [pl.BlockSpec(memory_space=pl.ANY)] * len(rest),
        out_specs=pl.BlockSpec((tile, depth), lambda i: (i + start, 0)),
        out_shape=jax.ShapeDtypeStruct((vocab, depth), jnp.float32),
        input_output_aliases={4: 0} if rest else {},
        cost_estimate=pl.CostEstimate(flops=4 * tokens * steps * tile * depth, bytes_accessed=4 * tokens * steps * tile, transcendentals=0),
        compiler_params=pltpu.CompilerParams(vmem_limit_bytes=VMEM_LIMIT),
        name="head_dtable",
    )(dz_a, hn_a, dz_b, hn_b, *rest)


def norm(values, gain):
    return values * lax.rsqrt(jnp.mean(values * values, axis=-1, keepdims=True) + EPS) * gain

def mlp_kernel(chunk, x_ref, g1_ref, g2_ref, wg_ref, wu_ref, wd_ref, a_ref, gt_ref, up_ref, q_ref, h_ref, hn_ref):
    x = x_ref[...]
    a = norm(x, g1_ref[...]).astype(jnp.bfloat16)
    a_ref[...] = a
    total = None
    for lo in range(0, gt_ref.shape[1], chunk):
        cols = slice(lo, lo + chunk)
        gt = jnp.dot(a, wg_ref[:, cols], preferred_element_type=jnp.float32).astype(jnp.bfloat16)
        up = jnp.dot(a, wu_ref[:, cols], preferred_element_type=jnp.float32).astype(jnp.bfloat16)
        gt_ref[:, cols] = gt
        up_ref[:, cols] = up
        gate = gt.astype(jnp.float32)
        q = (gate * jax.nn.sigmoid(gate) * up.astype(jnp.float32)).astype(jnp.bfloat16)
        q_ref[:, cols] = q
        part = jnp.dot(q, wd_ref[cols, :], preferred_element_type=jnp.float32)
        total = part if total is None else total + part
    h = x + total.astype(jnp.bfloat16).astype(jnp.float32)
    h_ref[...] = h
    hn_ref[...] = norm(h, g2_ref[...]).astype(jnp.bfloat16)

def mlp_forward_kernel(x, g1, g2, wg, wu, wd, tokens, blk=256, chunk=1024):
    depth = x.shape[1]
    width = wg.shape[1]
    row = lambda n: pl.BlockSpec((blk, n), lambda i: (i, 0))
    whole = lambda s: pl.BlockSpec(s, lambda i: (0, 0), pipeline_mode=pl.Buffered(1))
    shape = lambda n, t: jax.ShapeDtypeStruct((tokens, n), t)
    return pl.pallas_call(
        functools.partial(mlp_kernel, chunk),
        grid=(tokens // blk,),
        in_specs=[row(depth), whole((1, depth)), whole((1, depth)), whole(wg.shape), whole(wu.shape), whole(wd.shape)],
        out_specs=[row(depth), row(width), row(width), row(width), row(depth), row(depth)],
        out_shape=[shape(depth, jnp.bfloat16), shape(width, jnp.bfloat16), shape(width, jnp.bfloat16), shape(width, jnp.bfloat16), shape(depth, jnp.float32), shape(depth, jnp.bfloat16)],
        cost_estimate=pl.CostEstimate(flops=6 * tokens * width * depth, bytes_accessed=6 * tokens * width, transcendentals=tokens * width),
        compiler_params=pltpu.CompilerParams(vmem_limit_bytes=VMEM_LIMIT),
        name="mlp_forward",
    )(x, g1.reshape(1, -1), g2.reshape(1, -1), wg, wu, wd)

def dact_kernel(chunk, dm_ref, wd_ref, gt_ref, up_ref, dgt_ref, dup_ref):
    dm = dm_ref[...]
    for lo in range(0, gt_ref.shape[1], chunk):
        cols = slice(lo, lo + chunk)
        dq = lax.dot_general(dm, wd_ref[cols, :], NT, preferred_element_type=jnp.float32)
        gate = gt_ref[:, cols].astype(jnp.float32)
        up = up_ref[:, cols].astype(jnp.float32)
        sig = jax.nn.sigmoid(gate)
        dgt_ref[:, cols] = (dq * up * (sig * (1.0 + gate * (1.0 - sig)))).astype(jnp.bfloat16)
        dup_ref[:, cols] = (dq * (gate * sig)).astype(jnp.bfloat16)

def mlp_dact(dm, wd, gt, up, blk=256, chunk=1024):
    tokens, depth = dm.shape
    width = wd.shape[0]
    row = lambda n: pl.BlockSpec((blk, n), lambda i: (i, 0))
    return pl.pallas_call(
        functools.partial(dact_kernel, chunk),
        grid=(tokens // blk,),
        in_specs=[row(depth), pl.BlockSpec(wd.shape, lambda i: (0, 0), pipeline_mode=pl.Buffered(1)), row(width), row(width)],
        out_specs=[row(width), row(width)],
        out_shape=[jax.ShapeDtypeStruct((tokens, width), jnp.bfloat16)] * 2,
        cost_estimate=pl.CostEstimate(flops=2 * tokens * width * depth, bytes_accessed=8 * tokens * width, transcendentals=tokens * width),
        compiler_params=pltpu.CompilerParams(vmem_limit_bytes=VMEM_LIMIT),
        name="mlp_dact",
    )(dm, wd, gt, up)


def add_rows_kernel(bound_ref, ids_ref, base_ref, own_ref, theirs_ref, out_ref):
    tile = pl.program_id(0)
    out_ref[...] = base_ref[...]
    start = tile * out_ref.shape[0]
    for part, rows_ref in enumerate((own_ref, theirs_ref)):
        def body(t, carry, part=part, rows_ref=rows_ref):
            row = ids_ref[part, t] - start
            out_ref[pl.ds(row, 1), :] = out_ref[pl.ds(row, 1), :] + rows_ref[pl.ds(t, 1), :]
            return carry
        lax.fori_loop(bound_ref[part, tile], bound_ref[part, tile + 1], body, 0)


def add_rows(base, own, theirs, ids, bounds, tile):
    vocab, depth = base.shape
    whole = pl.BlockSpec(own.shape, lambda i, *_: (0, 0), pipeline_mode=pl.Buffered(1))
    return pl.pallas_call(
        add_rows_kernel,
        grid_spec=pltpu.PrefetchScalarGridSpec(
            num_scalar_prefetch=2,
            grid=(vocab // tile,),
            in_specs=[pl.BlockSpec((tile, depth), lambda i, *_: (i, 0)), whole, whole],
            out_specs=pl.BlockSpec((tile, depth), lambda i, *_: (i, 0)),
        ),
        out_shape=jax.ShapeDtypeStruct(base.shape, base.dtype),
        input_output_aliases={2: 0},
        cost_estimate=pl.CostEstimate(flops=2 * vocab * depth, bytes_accessed=8 * vocab * depth, transcendentals=0),
        compiler_params=pltpu.CompilerParams(vmem_limit_bytes=VMEM_LIMIT),
        name="add_rows",
    )(bounds, ids, base, own, theirs)


def place_kernel(start_ref, block_ref, out_ref, *scratch):
    rows = scratch[0] if scratch else out_ref
    _, cap, depth = block_ref.shape
    start = start_ref[pl.program_id(0)]
    sub = lax.broadcasted_iota(jnp.int32, (8, depth), 0)
    base = pl.multiple_of(start // 8 * 8, 8)
    shift = start % 8
    before = rows[pl.ds(base, 8), :]
    for j in range(0, cap, 16):
        piece = block_ref[0, j:j + 16, :].astype(jnp.float32)
        for k in (0, 8):
            turned = pltpu.roll(piece[k:k + 8], shift, 0)
            rows[pl.ds(pl.multiple_of(base + (j + k), 8), 8), :] = jnp.where(sub < shift, before, turned)
            before = turned
    tail = pl.ds(pl.multiple_of(base + cap, 8), 8)
    rows[tail, :] = jnp.where(sub < shift, before, rows[tail, :])
    if scratch:
        @pl.when(pl.program_id(0) == pl.num_programs(0) - 1)
        def _():
            out_ref[...] = rows[:out_ref.shape[0]].astype(out_ref.dtype)


def place_rows(blocks, starts, count, dtype):
    number, cap, depth = blocks.shape
    return pl.pallas_call(
        place_kernel,
        grid_spec=pltpu.PrefetchScalarGridSpec(
            num_scalar_prefetch=1,
            grid=(number,),
            in_specs=[pl.BlockSpec((1, cap, depth), lambda b, *_: (b, 0, 0))],
            out_specs=pl.BlockSpec((count, depth), lambda b, *_: (0, 0)),
            scratch_shapes=[] if dtype == jnp.float32 else [pltpu.VMEM((count + 8, depth), jnp.float32)],
        ),
        out_shape=jax.ShapeDtypeStruct((count, depth), dtype),
        cost_estimate=pl.CostEstimate(flops=8 * count * depth, bytes_accessed=8 * count * depth, transcendentals=0),
        compiler_params=pltpu.CompilerParams(vmem_limit_bytes=VMEM_LIMIT),
        name="place_rows",
    )(starts, blocks)


def window_kernel(first_ref, a_ref, b_ref, out_ref):
    count, _ = a_ref.shape
    cap = out_ref.shape[1]
    first = first_ref[pl.program_id(0)]
    base = pl.multiple_of(jnp.minimum(first // 8, (count - cap) // 8 - 1) * 8, 8)
    keep = 8 - (first - base)
    sub = lax.broadcasted_iota(jnp.int32, (8, a_ref.shape[1]), 0)
    here = None
    for j in range(0, cap + 8, 8):
        rows = pl.ds(pl.multiple_of(base + j, 8), 8)
        turned = pltpu.roll(a_ref[rows, :] + b_ref[rows, :], keep % 8, 0)
        if j:
            out_ref[0, j - 8:j, :] = jnp.where(sub < keep, here, turned)
        here = turned


def sum_windows(a, b, first, cap):
    count, depth = a.shape
    whole = pl.BlockSpec((count, depth), lambda c, *_: (0, 0), pipeline_mode=pl.Buffered(1))
    return pl.pallas_call(
        window_kernel,
        grid_spec=pltpu.PrefetchScalarGridSpec(
            num_scalar_prefetch=1,
            grid=(first.shape[0],),
            in_specs=[whole, whole],
            out_specs=pl.BlockSpec((1, cap, depth), lambda c, *_: (c, 0, 0)),
        ),
        out_shape=jax.ShapeDtypeStruct((first.shape[0], cap, depth), jnp.float32),
        cost_estimate=pl.CostEstimate(flops=8 * a.size, bytes_accessed=12 * a.size, transcendentals=0),
        compiler_params=pltpu.CompilerParams(vmem_limit_bytes=VMEM_LIMIT),
        name="sum_windows",
    )(first, a, b)


def swap_cores(values):
    return lax.ppermute(values, "fsdp", [(0, 1), (1, 0)])


def by_core(core, mine, theirs):
    return jnp.where(core == 0, jnp.concatenate([mine, theirs]), jnp.concatenate([theirs, mine]))


def owned_rows(sorted_ids, starts, dev_cap, table_shard):
    vocab, depth = table_shard.shape
    core = lax.axis_index("fsdp")
    device = lax.axis_index("model") * sorted_ids.shape[0] + core
    padded = jnp.pad(sorted_ids, ((0, 0), (0, dev_cap)))
    first = lax.dynamic_index_in_dim(starts, device, 1, keepdims=False)
    ids = jnp.concatenate([lax.dynamic_slice(padded, (part, first[part]), (1, dev_cap))[0] for part in (1 - core, core)])
    rows = jnp.take(table_shard, jnp.clip(ids - device * vocab, 0, vocab - 1), axis=0, mode="clip")
    theirs = swap_cores(rows[:dev_cap])
    return by_core(core, rows[dev_cap:], theirs).reshape(2, dev_cap, depth)


def fast_step(sorted_ids, sorted_labels, starts, sizes, pair, halves, table_shard, gain_in, gain_out):
    model_size, fsdp_size, dev_cap, chip_cap = sizes
    vocab, depth = table_shard.shape
    chip = lax.axis_index("model")
    core = lax.axis_index("fsdp")
    device = chip * fsdp_size + core
    count = sorted_ids.shape[1]
    num_tokens = count * fsdp_size
    half = depth // 2
    own = lambda values: lax.dynamic_index_in_dim(values, core, 0, keepdims=False)
    other = lambda values: lax.dynamic_index_in_dim(values, 1 - core, 0, keepdims=False)

    my_starts = own(starts)
    blocks = lax.all_gather(pair, "model", axis=0, tiled=True)
    w_gate, w_up, w_down = (by_core(core, mine, theirs) for mine, theirs in halves)
    x_buf = place_rows(blocks, my_starts, count + dev_cap + 8, jnp.float32)
    normed_bf, gate_bf, up_bf, act_bf, h_res, hn_own = mlp_forward_kernel(x_buf, gain_in, gain_out, w_gate, w_up, w_down, count)
    hn_other = swap_cores(hn_own)
    lane = lax.broadcasted_iota(jnp.int32, (fsdp_size, count, LANES), 2)
    local_labels = (sorted_labels - device * vocab)[:, :, None]
    offs = jnp.where((local_labels >= 0) & (local_labels < vocab), lane - local_labels, 1)
    off_own, off_other = own(offs), other(offs)
    z_own, stat_own = head_logits(hn_own, table_shard, off_own)
    z_other, stat_other = head_logits(hn_other, table_shard, off_other)
    part = by_core(core, stat_own[:, :3].T, stat_other[:, :3].T)
    all_stats = lax.all_gather(part, ("model", "fsdp"), axis=0).reshape(-1, fsdp_size, 3, count)
    row_max = jnp.max(all_stats[:, :, 0], axis=0)
    sum_exp = jnp.sum(all_stats[:, :, 1] * jnp.exp(all_stats[:, :, 0] - row_max[None]), axis=0)
    label_logit = jnp.sum(all_stats[:, :, 2], axis=0)
    loss = jnp.sum(row_max + jnp.log(sum_exp) - label_logit) / num_tokens
    max_lanes = jnp.broadcast_to(row_max[:, :, None], (fsdp_size, count, LANES))
    scale_lanes = jnp.broadcast_to((1.0 / sum_exp / num_tokens)[:, :, None], (fsdp_size, count, LANES))
    inv_tokens = 1.0 / num_tokens
    dz_other, d_hn_other = head_dlogits(z_other, table_shard, other(max_lanes), other(scale_lanes), off_other, inv_tokens, half)
    d_hn_theirs = swap_cores(d_hn_other)
    dz_own, d_hn_own = head_dlogits(z_own, table_shard, own(max_lanes), own(scale_lanes), off_own, inv_tokens, half)

    first = jnp.minimum(my_starts[0:model_size * fsdp_size:fsdp_size], count - chip_cap)
    windows = sum_windows(d_hn_own, d_hn_theirs, first, chip_cap)
    windows, dz_other, dz_own = lax.optimization_barrier((windows, dz_other, dz_own))
    d_hn_left = lax.psum_scatter(windows.reshape(model_size * chip_cap, half), "model", scatter_dimension=0, tiled=True)
    d_hn_other = head_dhn(dz_other, table_shard, half, 1)
    d_hn_theirs = swap_cores(d_hn_other)
    d_hn_own = head_dhn(dz_own, table_shard, half, 1)
    windows = sum_windows(d_hn_own, d_hn_theirs, first, chip_cap)
    windows, dz_other, dz_own = lax.optimization_barrier((windows, dz_other, dz_own))
    d_hn_right = lax.psum_scatter(windows.reshape(model_size * chip_cap, half), "model", scatter_dimension=0, tiled=True)
    d_head = head_dtable(dz_own, hn_own, dz_other, hn_other, None)
    d_hn_left, d_hn_right, d_head = lax.optimization_barrier((d_hn_left, d_hn_right, d_head))
    d_hn = jnp.concatenate([d_hn_left, d_hn_right], axis=1)
    my_first = lax.dynamic_index_in_dim(first, chip, 0, keepdims=False)
    h_window = lax.dynamic_slice(h_res, (my_first, 0), (chip_cap, depth))
    _, norm_out_back = jax.vjp(lambda values: rms_scale(values, gain_out), h_window)
    d_hidden = norm_out_back(d_hn)[0]
    dm_blocks = lax.all_gather(d_hidden.astype(jnp.bfloat16), "model", axis=0)
    d_head = head_dtable(dz_own, hn_own, dz_other, hn_other, d_head)
    dm_blocks, d_head = lax.optimization_barrier((dm_blocks, d_head))
    d_mlp = place_rows(dm_blocks, first, count, jnp.bfloat16)

    d_gate, d_up = mlp_dact(d_mlp, w_down, gate_bf, up_bf)
    grad_down = jnp.einsum("tf,td->fd", act_bf, d_mlp, preferred_element_type=jnp.float32)
    grad_gate = jnp.einsum("td,tf->df", normed_bf, d_gate, preferred_element_type=jnp.float32)
    grad_up = jnp.einsum("td,tf->df", normed_bf, d_up, preferred_element_type=jnp.float32)
    d_gate_own = lax.dynamic_slice(d_gate, (my_first, 0), (chip_cap, d_gate.shape[1]))
    d_up_own = lax.dynamic_slice(d_up, (my_first, 0), (chip_cap, d_up.shape[1]))
    x_window = lax.dynamic_slice(x_buf, (my_first, 0), (chip_cap, depth))
    d_normed = jnp.einsum("tf,df->td", d_gate_own, w_gate, preferred_element_type=jnp.float32) + jnp.einsum("tf,df->td", d_up_own, w_up, preferred_element_type=jnp.float32)
    _, norm_in_back = jax.vjp(lambda values: rms_scale(values, gain_in), x_window)
    d_x = d_hidden + norm_in_back(d_normed)[0]
    d_x_theirs = swap_cores(d_x)

    tile = vocab // 6
    pair_first = jnp.minimum(lax.dynamic_index_in_dim(starts, chip * fsdp_size, 1, keepdims=False), count - chip_cap)
    own_ids = jnp.stack([lax.dynamic_slice(sorted_ids, (p, pair_first[p]), (1, chip_cap))[0] for p in (core, 1 - core)]) - device * vocab
    edges = jnp.arange(vocab // tile + 1, dtype=jnp.int32) * tile
    bounds = jnp.sum((own_ids[:, :, None] < edges[None, None, :]).astype(jnp.int32), axis=1)
    grad_table = add_rows(d_head, d_x, d_x_theirs, own_ids, bounds, tile)

    grad_gate = lax.psum_scatter(grad_gate, "fsdp", scatter_dimension=0, tiled=True)
    grad_up = lax.psum_scatter(grad_up, "fsdp", scatter_dimension=0, tiled=True)
    grad_down = lax.psum_scatter(grad_down, "fsdp", scatter_dimension=0, tiled=True)
    return loss, grad_table, grad_gate, grad_up, grad_down


def capacity(tokens, shares, lists):
    mean = tokens / shares
    deviation = (mean * (1 - 1 / shares)) ** 0.5
    return -(-int((mean + 4.5 * deviation) / lists) // 16) * 16


def solution(mesh):
    fsdp_size = mesh.shape["fsdp"]
    model_size = mesh.shape["model"]
    tok_spec = P("fsdp", None)
    row_spec = P(("model", "fsdp"), None)
    weight_spec = P("fsdp", None)

    def device_step(tok_ids, tok_labels, table_shard, gate_shard, up_shard, down_shard, gain_in, gain_out):
        count = tok_ids.shape[0] * tok_ids.shape[1]
        vocab = table_shard.shape[0]
        devices = model_size * fsdp_size
        both = lax.all_gather(jnp.stack([tok_ids.reshape(-1), tok_labels.reshape(-1)]), "fsdp", axis=1, tiled=True)
        both, gate_shard, up_shard, down_shard = lax.optimization_barrier((both, gate_shard, up_shard, down_shard))
        ids, labels = lax.sort((both[0], both[1]), num_keys=1)
        sorted_ids = ids.reshape(count, fsdp_size).T
        sorted_labels = labels.reshape(count, fsdp_size).T
        edges = jnp.arange(devices + 1, dtype=jnp.int32) * vocab
        starts = jnp.sum((sorted_ids[:, :, None] < edges[None, None, :]).astype(jnp.int32), axis=1)
        dev_cap = capacity(count * fsdp_size, devices, fsdp_size)
        chip_cap = capacity(count * fsdp_size, model_size, fsdp_size)
        dev_counts = starts[:, 1:] - starts[:, :-1]
        chip_starts = starts[:, ::fsdp_size]
        chip_counts = chip_starts[:, 1:] - chip_starts[:, :-1]
        fits = (jnp.max(dev_counts) <= dev_cap) & (jnp.max(chip_counts) <= chip_cap)
        core = lax.axis_index("fsdp")
        pair = owned_rows(sorted_ids, starts, dev_cap, table_shard)
        halves = tuple((shard, swap_cores(shard)) for shard in (gate_shard, up_shard, down_shard))
        weights = (halves, table_shard, gain_in, gain_out)
        return lax.cond(
            fits,
            lambda: fast_step(sorted_ids, sorted_labels, starts, (model_size, fsdp_size, dev_cap, chip_cap), pair, *weights),
            lambda: slow_step(tok_ids, tok_labels, *weights),
        )

    return jax.shard_map(device_step, mesh=mesh, in_specs=(tok_spec, tok_spec, row_spec, weight_spec, weight_spec, weight_spec, P(), P()), out_specs=(P(), row_spec, weight_spec, weight_spec, weight_spec), check_vma=False)
```

time: 790 us -> 729 us (0.923)
  waiting for transfers between devices: 165 us -> 65.8 us
  other arithmetic: 29.9 us -> 53.4 us
  Pallas kernels: 411 us -> 425 us
    pallas_call x4 -> x8, Pallas kernels: 104 us -> 139 us  [the longest x2 69.2 us: head_dtable(): pl.pallas_call(dtable_kernel, grid=(steps,), in_specs=[dz_spec, hn_spec,...]
    all_gather x1, waiting for transfers between devices: 57.7 us -> 27.7 us  [fast_step(): blocks = lax.all_gather(pair, 'model', axis=0, tiled=True)]
    all_gather x3 -> x0, waiting for transfers between devices: 25.6 us -> none  [the longest x1 19 us: fast_step(): w_up = lax.all_gather(up_shard, 'fsdp', axis=0, tiled=True)]
    all_gather x1, waiting for transfers between devices: 52.2 us -> 28.1 us  [fast_step(): dm_blocks = lax.all_gather(d_hidden.astype(jnp.bfloat16), 'model', axis=0)]
    select_n x4 -> x5, other arithmetic: 8.47 us -> 31.1 us  [the longest x4 30 us: by_core(): jnp.where(core == 0, jnp.concatenate([mine, theirs]), jnp.concatenate([th...]
    pallas_call x2, Pallas kernels: 84.8 us -> 69 us  [head_dlogits(): pl.pallas_call(functools.partial(dlogits_kernel, inv_tokens, chunk), grid...]
    reduce_scatter x1 -> x2, waiting for transfers between devices: 25.3 us -> 9.87 us  [fast_step(): lax.psum_scatter(windows.reshape(model_size * chip_cap, half), 'model', s...]
    gather x3 -> x1, local copies, waits for them, and re-layouts: 16 us -> 10.3 us  [owned_rows(): jnp.take(table_shard, jnp.clip(ids - device * vocab, 0, vocab - 1), axis=...]
  transfers between devices with their start and end apart: 13 -> 15, of which waited for: 6 -> 3; matrix products, arithmetic and copies ran while one was open for 14% -> 19% of each run, Pallas kernels for 24% -> 35%
where the time goes in v2:
time: 729 us; the launch traced here: 722 us
  Pallas kernels  425 us (58%)
  matrix products  90.5 us (12%)
  waiting for transfers between devices  65.8 us (9%)
  other arithmetic  53.4 us (7%)
  local copies, waits for them, and re-layouts  32.9 us (5%)
  between operations  21 us (3%)
  loops' own time  17 us (2%)
  blocking collectives  14.6 us (2%)
    pallas_call x2, Pallas kernels, head_logits(): pl.pallas_call(functools.partial(logits_kernel, chunk), grid=(tokens // b...  89.2 us
    pallas_call x1, Pallas kernels, mlp_forward_kernel(): pl.pallas_call(functools.partial(mlp_kernel, chunk), grid=(tokens // blk,...  69.7 us
    pallas_call x2, Pallas kernels, head_dtable(): pl.pallas_call(dtable_kernel, grid=(steps,), in_specs=[dz_spec, hn_spec,...  69.2 us
    pallas_call x2, Pallas kernels, head_dlogits(): pl.pallas_call(functools.partial(dlogits_kernel, inv_tokens, chunk), grid...  69 us
    pallas_call x2, Pallas kernels, head_dhn(): pl.pallas_call(dhn_kernel, grid=(tokens // blk,), in_specs=[pl.BlockSpec(...  40 us
    pallas_call x1, Pallas kernels, mlp_dact(): pl.pallas_call(functools.partial(dact_kernel, chunk), grid=(tokens // blk...  36.5 us
    select_n x4, other arithmetic, by_core(): jnp.where(core == 0, jnp.concatenate([mine, theirs]), jnp.concatenate([th...  30 us
    all_gather x1, waiting for transfers between devices, fast_step(): dm_blocks = lax.all_gather(d_hidden.astype(jnp.bfloat16), 'model', axis=0)  28.1 us
  transfers between devices with their start and end apart: 15, of which 3 were waited for; matrix products, arithmetic and copies ran while one was open for 19% of the time, Pallas kernels for 35%

profile of v2, /device:TPU:0, one launch (start us, length us, event | category | flops | bytes accessed | tf_op | source)
XLA Modules:
  0.0 722.4 jit_solution(13316167835610686268)
XLA Ops:
  7.2 0.7 pad_add_fusion
  7.9 2.3 all_gather.19
  10.2 0.4 collective-permute-start.4
  11.1 5.9 sort.23
  17.1 1.0 reshape.323
  18.8 0.6 fusion.67
  23.7 10.3 %gather_fusion.1 = bf16[608,1024]{1,0:T(8,128)(2,1)S(1)} fusion(bf16[6288,1024]{1,0:T(8,128)(2,1)} %param.12, s32[1024]{0:T(1024)S(1)} %pad_clamp_fusion), kind=kCustom, calls=%fused_computation.1 | custom fusion | bytes 2492800 | tf_op jit(solution)/shard_map/jit(_take)/gather | solution.py:423
  34.0 1.1 fusion.65
  35.3 1.0 reshape.324
  36.3 0.6 subtract_reduce_fusion.2
  37.6 0.6 fusion.59
  38.9 0.8 copy-done.9
  39.7 2.2 pad_maximum_fusion.2
  42.0 671.9 %conditional.1 = (f32[]{:T(128)}, f32[6288,1024]{1,0:T(8,128)}, f32[512,4096]{1,0:T(8,128)}, f32[512,4096]{1,0:T(8,128)}, f32[2048,1024]{1,0:T(8,128)}) conditional(s32[]{:T(128)} %convert_element_type.57, (s32[1,2048]{1,0:T(1,128)}, bf16[6288,1024]{1,0:T(8,128)(2,1)}, f32[1024]{0:T(1024)S(1)}, bf16[512,4096]{1,0:T(8,128)(2,1)}, ...), branch_computations={%region_4.23_spmd, %region_23.38_spmd} | conditional | flops 313810911232 | bytes 1838356736 | solution.py:546
  50.2 1.2 broadcast_select_fusion
  51.5 0.9 copy.56
  52.4 0.8 copy.55
  53.2 0.5 fusion.16.start_ref
  53.7 10.6 %maximum_select_fusion.2.wd_ref = bf16[4096,1024]{1,0:T(8,128)(2,1)} fusion(bf16[2048,1024]{1,0:T(8,128)(2,1)} %get-tuple-element.82, bf16[2048,1024]{1,0:T(8,128)(2,1)} %get-tuple-element.81, pred[]{:T(512)S(6)} %eq.16), kind=kLoop, calls=%fused_computation.5 | loop fusion | flops 37748736 | bytes 16777216 | tf_op jit(solution)/shard_map/cond/branch_1_fun/jit(_where)/select_n | solution.py:413
  64.4 1.0 copy-done.8
  65.4 16.0 %maximum_select_fusion = (bf16[1024,4096]{1,0:T(8,128)(2,1)}, bf16[1024,4096]{1,0:T(8,128)(2,1)}) fusion(bf16[512,4096]{1,0:T(8,128)(2,1)} %get-tuple-element.78, bf16[512,4096]{1,0:T(8,128)(2,1)S(1)} %copy-done.7, pred[]{:T(512)S(6)} %eq.16, bf16[512,4096]{1,0:T(8,128)(2,1)S(1)} %copy-done.8, bf16[512,4096]{1,0:T(8,128)(2,1)} %get-tuple-element.80), kind=kLoop, calls=%fused_computation.3 | loop fusion | flops 75497472 | bytes 33554432 | tf_op jit(solution)/shard_map/cond/branch_1_fun/jit(_where)/select_n | solution.py:413
  81.4 27.7 %all-gather.7.cloned.1.call-done.block_ref = bf16[8,304,1024]{2,1,0:T(8,128)(2,1)} async-done(((bf16[2,304,1024]{2,1,0:T(8,128)(2,1)}), bf16[8,304,1024]{2,1,0:T(8,128)(2,1)}) %all-gather.7.cloned.1.call-update) | async-done | bytes 4980752 | tf_op jit(solution)/shard_map/cond/branch_1_fun/all_gather | solution.py:441
  109.1 9.4 %place_rows.2.x_ref = f32[2360,1024]{1,0:T(8,128)} custom-call(s32[9]{0:T(128)} %fusion.16.start_ref, bf16[8,304,1024]{2,1,0:T(8,128)(2,1)} %all-gather.7.cloned.1.call-done.block_ref), custom_call_target="tpu_custom_call" | custom-call | flops 19333120 | bytes 19333120 | tf_op jit(solution)/shard_map/cond/branch_1_fun/place_rows/pallas_call | solution.py:358
  118.5 69.7 %mlp_forward.1 = (bf16[2048,1024]{1,0:T(8,128)(2,1)}, bf16[2048,4096]{1,0:T(8,128)(2,1)}, bf16[2048,4096]{1,0:T(8,128)(2,1)}, bf16[2048,4096]{1,0:T(8,128)(2,1)}...) custom-call(f32[2360,1024]{1,0:T(8,128)} %place_rows.2.x_ref, f32[1,1024]{1,0:T(1,128)S(1)} %bitcast.104, ...), custom_call_target="tpu_custom_call" | custom-call | flops 51539607552 | bytes 50331648 | tf_op jit(solution)/shard_map/cond/branch_1_fun/mlp_forward/pallas_call | solution.py:265
  188.3 1.1 subtract_select_fusion
  189.4 1.5 dynamic-slice_bitcast_fusion.1
  190.9 44.7 %head_logits.2 = (f32[2048,6288]{1,0:T(8,128)}, f32[2048,128]{1,0:T(8,128)}) custom-call(bf16[2048,1024]{1,0:T(8,128)(2,1)} %get-tuple-element.83.hn_ref.ha_ref, bf16[6288,1024]{1,0:T(8,128)(2,1)} %get-tuple-element.84.emb_ref, s32[2048,128]{1,0:T(8,128)} %get-tuple-element.195.off_ref), custom_call_target="tpu_custom_call" | custom-call | flops 26373783552 | bytes 51511296 | tf_op jit(solution)/shard_map/cond/branch_1_fun/head_logits/pallas_call | solution.py:126
  235.6 2.3 slice_bitcast_fusion.1
  237.9 44.5 %head_logits.3 = (f32[2048,6288]{1,0:T(8,128)}, f32[2048,128]{1,0:T(8,128)}) custom-call(bf16[2048,1024]{1,0:T(8,128)(2,1)} %collective-permute-done.hn_ref.hb_ref, bf16[6288,1024]{1,0:T(8,128)(2,1)} %get-tuple-element.84.emb_ref, s32[2048,128]{1,0:T(8,128)} %get-tuple-element.196.off_ref), custom_call_target="tpu_custom_call" | custom-call | flops 26373783552 | bytes 51511296 | tf_op jit(solution)/shard_map/cond/branch_1_fun/head_logits/pallas_call | solution.py:126
  282.4 1.3 slice_bitcast_fusion
  283.7 2.2 maximum_select_fusion.3
  286.2 12.3 %all_gather.15 = f32[8,6,2048]{2,1,0:T(8,128)S(1)} all-gather(f32[1,6,2048]{2,1,0:T(8,128)S(1)} %copy.48), channel_id=1, replica_groups=mesh['model'=4,'fsdp'=2] {'model','fsdp'}, dimensions={0}, use_global_device_ids=true | all-gather | bytes 442368 | tf_op jit(solution)/shard_map/cond/branch_1_fun/all_gather | solution.py:453
  298.9 0.6 divide_multiply_fusion
  299.5 1.3 broadcast_in_dim.104.scale_ref
  300.8 1.4 broadcast_in_dim.102.max_ref
  302.2 34.7 %head_dlogits.3 = (bf16[2048,6288]{1,0:T(8,128)(2,1)}, f32[2048,512]{1,0:T(8,128)}) custom-call(f32[2048,6288]{1,0:T(8,128)} %get-tuple-element.91.z_ref, bf16[6288,1024]{1,0:T(8,128)(2,1)} %get-tuple-element.84.emb_ref, f32[2048,128]{1,0:T(8,128)} %broadcast_in_dim.102.max_ref, f32[2048,128]{1,0:T(8,128)} %broadcast_in_dim.104.scale_ref, ...), custom_call_target="tpu_custom_call" | custom-call | flops 13186891776 | bytes 77266944 | tf_op jit(solution)/shard_map/cond/branch_1_fun/head_dlogits/pallas_call | solution.py:166
  337.0 0.5 broadcast_minimum_fusion.first_ref.start_ref
  337.5 1.3 broadcast_in_dim.100.scale_ref
  338.9 1.3 broadcast_in_dim.98.max_ref
  340.2 34.3 %head_dlogits.2 = (bf16[2048,6288]{1,0:T(8,128)(2,1)}, f32[2048,512]{1,0:T(8,128)}) custom-call(f32[2048,6288]{1,0:T(8,128)} %get-tuple-element.89.z_ref, bf16[6288,1024]{1,0:T(8,128)(2,1)} %get-tuple-element.84.emb_ref, f32[2048,128]{1,0:T(8,128)} %broadcast_in_dim.98.max_ref, f32[2048,128]{1,0:T(8,128)} %broadcast_in_dim.100.scale_ref, ...), custom_call_target="tpu_custom_call" | custom-call | flops 13186891776 | bytes 77266944 | tf_op jit(solution)/shard_map/cond/branch_1_fun/head_dlogits/pallas_call | solution.py:166
  374.4 6.8 sum_windows.2
  381.4 20.1 %head_dhn.3 = f32[2048,512]{1,0:T(8,128)} custom-call(bf16[2048,6288]{1,0:T(8,128)(2,1)} %get-tuple-element.100.dz_ref.b_ref, bf16[6288,1024]{1,0:T(8,128)(2,1)} %get-tuple-element.84.emb_ref), custom_call_target="tpu_custom_call" | custom-call | flops 13186891776 | bytes 25755648 | tf_op jit(solution)/shard_map/cond/branch_1_fun/head_dhn/pallas_call | solution.py:193
  401.4 0.5 collective-permute-start.2
  401.9 20.0 %head_dhn.2.a_ref = f32[2048,512]{1,0:T(8,128)} custom-call(bf16[2048,6288]{1,0:T(8,128)(2,1)} %get-tuple-element.99.dz_ref.a_ref, bf16[6288,1024]{1,0:T(8,128)(2,1)} %get-tuple-element.84.emb_ref), custom_call_target="tpu_custom_call" | custom-call | flops 13186891776 | bytes 25755648 | tf_op jit(solution)/shard_map/cond/branch_1_fun/head_dhn/pallas_call | solution.py:193
  421.9 7.0 sum_windows.3
  429.0 0.7 dynamic_slice.56
  431.7 46.0 %head_dtable.2.refs_0_ = f32[6288,1024]{1,0:T(8,128)} custom-call(bf16[2048,6288]{1,0:T(8,128)(2,1)} %get-tuple-element.99.dz_ref.a_ref, bf16[2048,1024]{1,0:T(8,128)(2,1)} %get-tuple-element.83.hn_ref.ha_ref, bf16[2048,6288]{1,0:T(8,128)(2,1)} %get-tuple-element.100.dz_ref.b_ref, bf16[2048,1024]{1,0:T(8,128)(2,1)} %collective-permute-done.hn_ref.hb_ref), custom_call_target="tpu_custom_call" | custom-call | flops 37580963840 | bytes 36700160 | tf_op jit(solution)/shard_map/cond/branch_1_fun/head_dtable/pallas_call | solution.py:223
  477.7 9.9 %reduce-scatter.20.cloned.1.call-done = f32[576,512]{1,0:T(8,128)} async-done(((f32[2304,512]{1,0:T(8,128)}), f32[576,512]{1,0:T(8,128)}) %reduce-scatter.20.cloned.1.call-update) | async-done | bytes 1179664 | tf_op jit(solution)/shard_map/cond/branch_1_fun/reduce_scatter | solution.py:474
  487.6 3.0 multiply_reduce_fusion.3
  490.6 0.6 copy-done.26
  491.2 4.0 fusion.17
  495.2 23.2 %head_dtable.3.base_ref = f32[6288,1024]{1,0:T(8,128)} custom-call(bf16[2048,6288]{1,0:T(8,128)(2,1)} %get-tuple-element.99.dz_ref.a_ref, bf16[2048,1024]{1,0:T(8,128)(2,1)} %get-tuple-element.83.hn_ref.ha_ref, bf16[2048,6288]{1,0:T(8,128)(2,1)} %get-tuple-element.100.dz_ref.b_ref, ...), custom_call_target="tpu_custom_call", output_to_operand_aliasing={{}: (4, {})} | custom-call | flops 16106127360 | bytes 15728640 | tf_op jit(solution)/shard_map/cond/branch_1_fun/head_dtable/pallas_call | solution.py:223
  518.4 28.1 %all-gather.9.cloned.1.call-done = bf16[2304,1024]{1,0:T(8,128)(2,1)} async-done(((bf16[576,1024]{1,0:T(8,128)(2,1)}), bf16[2304,1024]{1,0:T(8,128)(2,1)}) %all-gather.9.cloned.1.call-update) | async-done | bytes 4718608 | tf_op jit(solution)/shard_map/cond/branch_1_fun/all_gather | solution.py:482
  546.5 6.6 place_rows.3.dm_ref
  553.1 23.7 %fusion.70 = f32[4096,1024]{1,0:T(8,128)} fusion(bf16[2048,4096]{1,0:T(8,128)(2,1)} %get-tuple-element.112, bf16[2048,1024]{1,0:T(8,128)(2,1)} %place_rows.3.dm_ref), kind=kOutput, calls=%fused_computation.162 | convolution fusion | flops 17179869184 | bytes 37748736 | tf_op jit(solution)/shard_map/cond/branch_1_fun/tf,td->fd/dot_general | solution.py:488
  576.9 36.5 %mlp_dact.1 = (bf16[2048,4096]{1,0:T(8,128)(2,1)}, bf16[2048,4096]{1,0:T(8,128)(2,1)}) custom-call(bf16[2048,1024]{1,0:T(8,128)(2,1)} %place_rows.3.dm_ref, bf16[4096,1024]{1,0:T(8,128)(2,1)} %maximum_select_fusion.2.wd_ref, bf16[2048,4096]{1,0:T(8,128)(2,1)} %get-tuple-element.107.gt_ref, bf16[2048,4096]{1,0:T(8,128)(2,1)} %get-tuple-element.108.up_ref), custom_call_target="tpu_custom_call" | custom-call | flops 17179869184 | bytes 67108864 | tf_op jit(solution)/shard_map/cond/branch_1_fun/mlp_dact/pallas_call | solution.py:291
  613.3 23.7 %fusion.69 = f32[1024,4096]{1,0:T(8,128)} fusion(bf16[2048,1024]{1,0:T(8,128)(2,1)} %get-tuple-element.111, bf16[2048,4096]{1,0:T(8,128)(2,1)} %get-tuple-element.110), kind=kOutput, calls=%fused_computation.161 | convolution fusion | flops 17179869184 | bytes 37748736 | tf_op jit(solution)/shard_map/cond/branch_1_fun/td,tf->df/dot_general | solution.py:490
  637.1 24.0 %fusion.68 = f32[1024,4096]{1,0:T(8,128)} fusion(bf16[2048,1024]{1,0:T(8,128)(2,1)} %get-tuple-element.111, bf16[2048,4096]{1,0:T(8,128)(2,1)} %get-tuple-element.109), kind=kOutput, calls=%fused_computation.160 | convolution fusion | flops 17179869184 | bytes 37748736 | tf_op jit(solution)/shard_map/cond/branch_1_fun/td,tf->df/dot_general | solution.py:489
  662.6 9.0 %fusion = f32[576,1024]{1,0:T(8,128)S(1)} fusion(bf16[1024,4096]{1,0:T(8,128)(2,1)} %get-tuple-element.213.wu_ref, bf16[2048,4096]{1,0:T(8,128)(2,1)} %get-tuple-element.110, s32[]{:T(128)S(6)} %select_n.176), kind=kOutput, calls=%fused_computation.6 | convolution fusion | flops 4831838208 | bytes 15466500 | tf_op jit(solution)/shard_map/cond/branch_1_fun/tf,df->td/dot_general | solution.py:494
  671.6 10.0 %multiply_reduce_fusion.1 = (f32[576]{0:T(1024)S(1)}, f32[576]{0:T(1024)S(1)}, f32[576,1024]{1,0:T(8,128)S(1)}) fusion(f32[2360,1024]{1,0:T(8,128)} %place_rows.2.x_ref, s32[]{:T(128)S(6)} %select_n.177, f32[1024]{0:T(1024)S(1)} %copy-done.53, f32[576,1024]{1,0:T(8,128)S(1)} %fusion, bf16[1024,4096]{1,0:T(8,128)(2,1)} %get-tuple-element.212.wg_ref, ...), kind=kOutput, calls=%fused_computation.15 | convolution fusion | flops 4835376128 | bytes 20193800 | tf_op jit(solution)/shard_map/cond/branch_1_fun/tf,df->td/dot_general | solution.py:494
  681.7 3.1 fusion.4.own_ref
  684.9 0.7 constant_dynamic-slice_fusion.5
  690.4 0.7 copy.50.bound_ref
  691.7 21.9 %add_rows.1 = f32[6288,1024]{1,0:T(8,128)} custom-call(s32[2,7]{1,0:T(2,128)} %copy.50.bound_ref, s32[2,576]{1,0:T(2,128)} %copy-done.25, f32[6288,1024]{1,0:T(8,128)} %head_dtable.3.base_ref, f32[576,1024]{1,0:T(8,128)} %copy-done.6, f32[576,1024]{1,0:T(8,128)} %collective-permute-done.3.theirs_ref), custom_call_target="tpu_custom_call", output_to_operand_aliasing={{}: (2, {})} | custom-call | flops 12877824 | bytes 51511296 | tf_op jit(solution)/shard_map/cond/branch_1_fun/add_rows/pallas_call | solution.py:318
  (110 shorter events, 4.1 us)
Async XLA Ops:
  10.2 31.7 %collective-permute-start.4 = (bf16[512,4096]{1,0:T(8,128)(2,1)}, bf16[512,4096]{1,0:T(8,128)(2,1)}, u32[]{:S(2)}, u32[]{:S(2)}) collective-permute-start(bf16[512,4096]{1,0:T(8,128)(2,1)} %param.13), channel_id=1, source_target_pairs={{0,1},{1,0},{2,3},{3,2},{4,5},{5,4},{6,7},{7,6}} | collective-permute-start | bytes 12582920 | tf_op jit(solution)/shard_map/ppermute | solution.py:409
  10.6 31.3 %collective-permute-start.5 = (bf16[512,4096]{1,0:T(8,128)(2,1)}, bf16[512,4096]{1,0:T(8,128)(2,1)}, u32[]{:S(2)}, u32[]{:S(2)}) collective-permute-start(bf16[512,4096]{1,0:T(8,128)(2,1)} %param.14), channel_id=1, source_target_pairs={{0,1},{1,0},{2,3},{3,2},{4,5},{5,4},{6,7},{7,6}} | collective-permute-start | bytes 12582920 | tf_op jit(solution)/shard_map/ppermute | solution.py:409
  10.8 31.2 %collective-permute-start.6 = (bf16[2048,1024]{1,0:T(8,128)(2,1)}, bf16[2048,1024]{1,0:T(8,128)(2,1)}, u32[]{:S(2)}, u32[]{:S(2)}) collective-permute-start(bf16[2048,1024]{1,0:T(8,128)(2,1)} %param.15), channel_id=1, source_target_pairs={{0,1},{1,0},{2,3},{3,2},{4,5},{5,4},{6,7},{7,6}} | collective-permute-start | bytes 12582920 | tf_op jit(solution)/shard_map/ppermute | solution.py:409
  18.1 18.2 %copy-start.2 = (s32[2048,2]{1,0:T(8,128)}, s32[2048,2]{1,0:T(8,128)S(1)}, u32[]{:S(2)}) copy-start(s32[2048,2]{1,0:T(8,128)S(1)} %reshape.323) | copy-start | bytes 49156
  18.8 20.1 %copy-start.12 = (s32[2,9]{0,1:T(8,128)}, s32[2,9]{0,1:T(8,128)S(1)}, u32[]{:S(2)}) copy-start(s32[2,9]{0,1:T(8,128)S(1)} %fusion.58) | copy-start | bytes 220
  23.7 18.2 %copy-start.13 = (f32[1024]{0:T(1024)S(1)}, f32[1024]{0:T(1024)}, u32[]{:S(2)}) copy-start(f32[1024]{0:T(1024)} %param.17) | copy-start | bytes 12292
  23.7 18.2 %copy-start.34 = (s32[1,2048]{1,0:T(1,128)S(1)}, s32[1,2048]{1,0:T(1,128)}, u32[]{:S(2)}) copy-start(s32[1,2048]{1,0:T(1,128)} %param.11) | copy-start | bytes 24580
  23.7 18.2 %copy-start.49 = (f32[1024]{0:T(1024)S(1)}, f32[1024]{0:T(1024)}, u32[]{:S(2)}) copy-start(f32[1024]{0:T(1024)} %param.16) | copy-start | bytes 12292
  35.1 3.8 collective-permute-start.7
  38.9 0.8 copy-start.9
  50.2 68.4 %copy-start.16 = (f32[1024]{0:T(1024)}, f32[1024]{0:T(1024)S(1)}, u32[]{:S(2)}) copy-start(f32[1024]{0:T(1024)S(1)} %get-tuple-element.76) | copy-start | bytes 12292 | tf_op jit(solution)/shard_map/cond
  50.2 68.3 %copy-start.52 = (f32[1024]{0:T(1024)}, f32[1024]{0:T(1024)S(1)}, u32[]{:S(2)}) copy-start(f32[1024]{0:T(1024)S(1)} %get-tuple-element.75) | copy-start | bytes 12292 | tf_op jit(solution)/shard_map/cond
  50.2 58.9 %all-gather.7.cloned.1.call-start = ((), (), s32[]{:S(2)}) async-start(), calls=%async_computation.16 | async-start | bytes 6225920 | tf_op jit(solution)/shard_map/cond/branch_1_fun/all_gather | solution.py:441
  51.4 426.3 %reduce-scatter.18.cloned.1.call-start = ((), (), s32[]{:S(2)}) async-start(), calls=%async_computation.17 | async-start | bytes 5898240 | tf_op jit(solution)/shard_map/cond/branch_1_fun/reduce_scatter | solution.py:468
  53.2 11.2 %copy-start.46 = (s32[2,9]{1,0:T(2,128)}, s32[2,9]{1,0:T(2,128)S(1)}, u32[]{:S(2)}) copy-start(s32[2,9]{1,0:T(2,128)S(1)} %copy.55) | copy-start | bytes 220 | tf_op jit(solution)/shard_map/cond
  53.7 10.7 %copy-start.7 = (bf16[512,4096]{1,0:T(8,128)(2,1)S(1)}, bf16[512,4096]{1,0:T(8,128)(2,1)}, u32[]{:S(2)}) copy-start(bf16[512,4096]{1,0:T(8,128)(2,1)} %get-tuple-element.77) | copy-start | bytes 12582916 | tf_op jit(solution)/shard_map/cond
  53.7 11.7 %copy-start.8 = (bf16[512,4096]{1,0:T(8,128)(2,1)S(1)}, bf16[512,4096]{1,0:T(8,128)(2,1)}, u32[]{:S(2)}) copy-start(bf16[512,4096]{1,0:T(8,128)(2,1)} %get-tuple-element.79) | copy-start | bytes 12582916 | tf_op jit(solution)/shard_map/cond
  118.5 69.7 %copy-start.24 = (s32[2,2048]{1,0:T(2,128)S(1)}, s32[2,2048]{1,0:T(2,128)}, u32[]{:S(2)}) copy-start(s32[2,2048]{1,0:T(2,128)} %copy.56) | copy-start | bytes 49156 | tf_op jit(solution)/shard_map/cond
  188.2 49.6 %collective-permute-start = (bf16[2048,1024]{1,0:T(8,128)(2,1)}, bf16[2048,1024]{1,0:T(8,128)(2,1)}, u32[]{:S(2)}, u32[]{:S(2)}) collective-permute-start(bf16[2048,1024]{1,0:T(8,128)(2,1)} %get-tuple-element.83.hn_ref.ha_ref), channel_id=1, source_target_pairs={{0,1},{1,0},{2,3},{3,2},{4,5},{5,4},{6,7},{7,6}} | collective-permute-start | bytes 12582920 | tf_op jit(solution)/shard_map/cond/branch_1_fun/ppermute | solution.py:409
  302.2 34.7 %copy-start.48 = (s32[9]{0:T(128)S(1)}, s32[9]{0:T(128)}, u32[]{:S(2)}) copy-start(s32[9]{0:T(128)} %fusion.16.start_ref) | copy-start | bytes 112 | tf_op jit(solution)/shard_map/cond
  336.9 37.5 %collective-permute-start.1 = (f32[2048,512]{1,0:T(8,128)}, f32[2048,512]{1,0:T(8,128)}, u32[]{:S(2)}, u32[]{:S(2)}) collective-permute-start(f32[2048,512]{1,0:T(8,128)} %get-tuple-element.92), channel_id=1, source_target_pairs={{0,1},{1,0},{2,3},{3,2},{4,5},{5,4},{6,7},{7,6}} | collective-permute-start | bytes 12582920 | tf_op jit(solution)/shard_map/cond/branch_1_fun/ppermute | solution.py:409
  381.3 106.2 %reduce-scatter.20.cloned.1.call-start = ((), (), s32[]{:S(2)}) async-start(), calls=%async_computation.18 | async-start | bytes 5898240 | tf_op jit(solution)/shard_map/cond/branch_1_fun/reduce_scatter | solution.py:474
  401.4 20.5 %collective-permute-start.2 = (f32[2048,512]{1,0:T(8,128)}, f32[2048,512]{1,0:T(8,128)}, u32[]{:S(2)}, u32[]{:S(2)}) collective-permute-start(f32[2048,512]{1,0:T(8,128)} %head_dhn.3), channel_id=1, source_target_pairs={{0,1},{1,0},{2,3},{3,2},{4,5},{5,4},{6,7},{7,6}} | collective-permute-start | bytes 12582920 | tf_op jit(solution)/shard_map/cond/branch_1_fun/ppermute | solution.py:409
  421.9 7.1 copy-start.45
  428.9 117.6 %all-gather.9.cloned.1.call-start = ((), (), s32[]{:S(2)}) async-start(), calls=%async_computation.22 | async-start | bytes 5898240 | tf_op jit(solution)/shard_map/cond/branch_1_fun/all_gather | solution.py:482
  431.7 55.9 %copy-start.17 = (f32[1024]{0:T(1024)S(1)}, f32[1024]{0:T(1024)}, u32[]{:S(2)}) copy-start(f32[1024]{0:T(1024)} %copy-done.16) | copy-start | bytes 12292 | tf_op jit(solution)/shard_map/cond
  490.6 0.6 copy-start.26
  490.6 0.6 copy-start.28
  495.1 218.4 %reduce-scatter.26.cloned.1.call-start = ((), (), s32[]{:S(2)}) async-start(), calls=%async_computation.21 | async-start | bytes 25165824 | tf_op jit(solution)/shard_map/cond/branch_1_fun/reduce_scatter | solution.py:508
  576.8 136.8 %reduce-scatter.24.cloned.1.call-start = ((), (), s32[]{:S(2)}) async-start(), calls=%async_computation.20 | async-start | bytes 25165824 | tf_op jit(solution)/shard_map/cond/branch_1_fun/reduce_scatter | solution.py:507
  637.1 76.5 %reduce-scatter.22.cloned.1.call-start = ((), (), s32[]{:S(2)}) async-start(), calls=%async_computation.19 | async-start | bytes 25165824 | tf_op jit(solution)/shard_map/cond/branch_1_fun/reduce_scatter | solution.py:506
  662.6 9.0 %copy-start.53 = (f32[1024]{0:T(1024)S(1)}, f32[1024]{0:T(1024)}, u32[]{:S(2)}) copy-start(f32[1024]{0:T(1024)} %copy-done.52) | copy-start | bytes 12292 | tf_op jit(solution)/shard_map/cond
  671.6 10.1 %copy-start.4 = (f32[576,512]{1,0:T(8,128)S(1)}, f32[576,512]{1,0:T(8,128)}, u32[]{:S(2)}) copy-start(f32[576,512]{1,0:T(8,128)} %reduce-scatter.18.cloned.1.call-done) | copy-start | bytes 3538948 | tf_op jit(solution)/shard_map/cond
  671.6 10.1 %copy-start.5 = (f32[576,512]{1,0:T(8,128)S(1)}, f32[576,512]{1,0:T(8,128)}, u32[]{:S(2)}) copy-start(f32[576,512]{1,0:T(8,128)} %reduce-scatter.20.cloned.1.call-done) | copy-start | bytes 3538948 | tf_op jit(solution)/shard_map/cond
  671.6 10.1 %copy-start.18 = (f32[1024]{0:T(1024)S(1)}, f32[1024]{0:T(1024)}, u32[]{:S(2)}) copy-start(f32[1024]{0:T(1024)} %copy-done.16) | copy-start | bytes 12292 | tf_op jit(solution)/shard_map/cond
  671.6 10.1 %copy-start.27 = (f32[576]{0:T(1024)S(1)}, f32[576]{0:T(1024)}, u32[]{:S(2)}) copy-start(f32[576]{0:T(1024)} %copy-done.26) | copy-start | bytes 6916 | tf_op jit(solution)/shard_map/cond
  671.6 10.1 %copy-start.29 = (f32[576]{0:T(1024)S(1)}, f32[576]{0:T(1024)}, u32[]{:S(2)}) copy-start(f32[576]{0:T(1024)} %copy-done.28) | copy-start | bytes 6916 | tf_op jit(solution)/shard_map/cond
  681.6 3.3 copy-start.47
  681.6 6.7 copy-start.3
  684.8 3.9 copy-start.6
  684.8 6.9 collective-permute-start.3
  690.1 1.5 copy-start.25
Sparse Core Ops, SparseCore 0:
  53.3 55.6 all-gather.6
  381.4 51.3 reduce-scatter.17
  436.3 51.1 reduce-scatter.19
  495.3 51.1 all-gather.8
  576.9 21.7 reduce-scatter.25
  637.2 21.8 reduce-scatter.23
  662.0 22.8 reduce-scatter.21

commit v3 on v2

--- a/solution.py
+++ b/solution.py
@@ -10,6 +10,7 @@
 EPS = 1e-6
 VMEM_LIMIT = 63 * 1024 * 1024
 LANES = 128
+NN = (((1,), (0,)), ((), ()))
 TN = (((0,), (0,)), ((), ()))
 NT = (((1,), (1,)), ((), ()))
 
@@ -98,7 +99,7 @@
     run_sum = jnp.zeros((rows, LANES), jnp.float32)
     run_lab = jnp.zeros((rows, LANES), jnp.float32)
     for lo, width in lane_chunks(vocab, chunk):
-        z = lax.dot_general(hn, emb_ref[lo:lo + width, :], NT, preferred_element_type=jnp.float32)
+        z = lax.dot_general(hn, emb_ref[:, lo:lo + width], NN, preferred_element_type=jnp.float32)
         z_ref[:, lo:lo + width] = z
         groups = width // LANES
         parts = [z[:, g * LANES:(g + 1) * LANES] for g in range(groups)]
@@ -120,15 +121,15 @@
     stat_ref[...] = jnp.where(lane == 0, row_max, jnp.where(lane == 1, row_sum, row_lab))
 
 
-def head_logits(hn, table, off, blk=256, chunk=1024):
+def head_logits(hn, table_t, off, blk=256, chunk=1024):
     tokens, depth = hn.shape
-    vocab = table.shape[0]
+    vocab = table_t.shape[1]
     return pl.pallas_call(
         functools.partial(logits_kernel, chunk),
         grid=(tokens // blk,),
         in_specs=[
             pl.BlockSpec((blk, depth), lambda i: (i, 0)),
-            pl.BlockSpec((vocab, depth), lambda i: (0, 0), pipeline_mode=pl.Buffered(1)),
+            pl.BlockSpec((depth, vocab), lambda i: (0, 0), pipeline_mode=pl.Buffered(1)),
             pl.BlockSpec((blk, LANES), lambda i: (i, 0)),
         ],
         out_specs=[
@@ -139,7 +140,7 @@
         cost_estimate=pl.CostEstimate(flops=2 * tokens * vocab * depth, bytes_accessed=4 * tokens * vocab, transcendentals=tokens * vocab),
         compiler_params=pltpu.CompilerParams(vmem_limit_bytes=VMEM_LIMIT),
         name="head_logits",
-    )(hn, table, off)
+    )(hn, table_t, off)
 
 
 def dlogits_kernel(inv_tokens, chunk, z_ref, emb_ref, max_ref, scale_ref, off_ref, dz_ref, dhn_ref):
@@ -273,31 +274,33 @@
         name="mlp_forward",
     )(x, g1.reshape(1, -1), g2.reshape(1, -1), wg, wu, wd)
 
-def dact_kernel(chunk, dm_ref, wd_ref, gt_ref, up_ref, dgt_ref, dup_ref):
-    dm = dm_ref[...]
-    for lo in range(0, gt_ref.shape[1], chunk):
-        cols = slice(lo, lo + chunk)
-        dq = lax.dot_general(dm, wd_ref[cols, :], NT, preferred_element_type=jnp.float32)
-        gate = gt_ref[:, cols].astype(jnp.float32)
-        up = up_ref[:, cols].astype(jnp.float32)
+def dact_kernel(rows, dm_ref, wd_ref, gt_ref, up_ref, q_ref, dgt_ref, dup_ref, dwd_ref):
+    for lo in range(0, dm_ref.shape[0], rows):
+        part = slice(lo, lo + rows)
+        dq = lax.dot_general(dm_ref[part, :], wd_ref[...], NT, preferred_element_type=jnp.float32)
+        gate = gt_ref[part, :].astype(jnp.float32)
+        up = up_ref[part, :].astype(jnp.float32)
         sig = jax.nn.sigmoid(gate)
-        dgt_ref[:, cols] = (dq * up * (sig * (1.0 + gate * (1.0 - sig)))).astype(jnp.bfloat16)
-        dup_ref[:, cols] = (dq * (gate * sig)).astype(jnp.bfloat16)
-
-def mlp_dact(dm, wd, gt, up, blk=256, chunk=1024):
+        dgt_ref[part, :] = (dq * up * (sig * (1.0 + gate * (1.0 - sig)))).astype(jnp.bfloat16)
+        dup_ref[part, :] = (dq * (gate * sig)).astype(jnp.bfloat16)
+    dwd_ref[...] = lax.dot_general(q_ref[...], dm_ref[...], TN, preferred_element_type=jnp.float32)
+
+
+def mlp_dact(dm, wd, gt, up, q, cols=512, rows=512):
     tokens, depth = dm.shape
     width = wd.shape[0]
-    row = lambda n: pl.BlockSpec((blk, n), lambda i: (i, 0))
-    return pl.pallas_call(
-        functools.partial(dact_kernel, chunk),
-        grid=(tokens // blk,),
-        in_specs=[row(depth), pl.BlockSpec(wd.shape, lambda i: (0, 0), pipeline_mode=pl.Buffered(1)), row(width), row(width)],
-        out_specs=[row(width), row(width)],
-        out_shape=[jax.ShapeDtypeStruct((tokens, width), jnp.bfloat16)] * 2,
-        cost_estimate=pl.CostEstimate(flops=2 * tokens * width * depth, bytes_accessed=8 * tokens * width, transcendentals=tokens * width),
+    col = pl.BlockSpec((tokens, cols), lambda j: (0, j))
+    row = pl.BlockSpec((cols, depth), lambda j: (j, 0))
+    return pl.pallas_call(
+        functools.partial(dact_kernel, rows),
+        grid=(width // cols,),
+        in_specs=[pl.BlockSpec((tokens, depth), lambda j: (0, 0), pipeline_mode=pl.Buffered(1)), row, col, col, col],
+        out_specs=[col, col, row],
+        out_shape=[jax.ShapeDtypeStruct((tokens, width), jnp.bfloat16)] * 2 + [jax.ShapeDtypeStruct((width, depth), jnp.float32)],
+        cost_estimate=pl.CostEstimate(flops=4 * tokens * width * depth, bytes_accessed=10 * tokens * width, transcendentals=tokens * width),
         compiler_params=pltpu.CompilerParams(vmem_limit_bytes=VMEM_LIMIT),
         name="mlp_dact",
-    )(dm, wd, gt, up)
+    )(dm, wd, gt, up, q)
 
 
 def add_rows_kernel(bound_ref, ids_ref, base_ref, own_ref, theirs_ref, out_ref):
@@ -433,13 +436,15 @@
     device = chip * fsdp_size + core
     count = sorted_ids.shape[1]
     num_tokens = count * fsdp_size
-    half = depth // 2
+    right = depth // 2
+    left = depth - right
     own = lambda values: lax.dynamic_index_in_dim(values, core, 0, keepdims=False)
     other = lambda values: lax.dynamic_index_in_dim(values, 1 - core, 0, keepdims=False)
 
     my_starts = own(starts)
     blocks = lax.all_gather(pair, "model", axis=0, tiled=True)
     w_gate, w_up, w_down = (by_core(core, mine, theirs) for mine, theirs in halves)
+    blocks, table_t, w_gate, w_up, w_down = lax.optimization_barrier((blocks, table_shard.T, w_gate, w_up, w_down))
     x_buf = place_rows(blocks, my_starts, count + dev_cap + 8, jnp.float32)
     normed_bf, gate_bf, up_bf, act_bf, h_res, hn_own = mlp_forward_kernel(x_buf, gain_in, gain_out, w_gate, w_up, w_down, count)
     hn_other = swap_cores(hn_own)
@@ -447,8 +452,8 @@
     local_labels = (sorted_labels - device * vocab)[:, :, None]
     offs = jnp.where((local_labels >= 0) & (local_labels < vocab), lane - local_labels, 1)
     off_own, off_other = own(offs), other(offs)
-    z_own, stat_own = head_logits(hn_own, table_shard, off_own)
-    z_other, stat_other = head_logits(hn_other, table_shard, off_other)
+    z_own, stat_own = head_logits(hn_own, table_t, off_own)
+    z_other, stat_other = head_logits(hn_other, table_t, off_other)
     part = by_core(core, stat_own[:, :3].T, stat_other[:, :3].T)
     all_stats = lax.all_gather(part, ("model", "fsdp"), axis=0).reshape(-1, fsdp_size, 3, count)
     row_max = jnp.max(all_stats[:, :, 0], axis=0)
@@ -458,20 +463,20 @@
     max_lanes = jnp.broadcast_to(row_max[:, :, None], (fsdp_size, count, LANES))
     scale_lanes = jnp.broadcast_to((1.0 / sum_exp / num_tokens)[:, :, None], (fsdp_size, count, LANES))
     inv_tokens = 1.0 / num_tokens
-    dz_other, d_hn_other = head_dlogits(z_other, table_shard, other(max_lanes), other(scale_lanes), off_other, inv_tokens, half)
+    dz_other, d_hn_other = head_dlogits(z_other, table_shard, other(max_lanes), other(scale_lanes), off_other, inv_tokens, left)
     d_hn_theirs = swap_cores(d_hn_other)
-    dz_own, d_hn_own = head_dlogits(z_own, table_shard, own(max_lanes), own(scale_lanes), off_own, inv_tokens, half)
+    dz_own, d_hn_own = head_dlogits(z_own, table_shard, own(max_lanes), own(scale_lanes), off_own, inv_tokens, left)
 
     first = jnp.minimum(my_starts[0:model_size * fsdp_size:fsdp_size], count - chip_cap)
     windows = sum_windows(d_hn_own, d_hn_theirs, first, chip_cap)
     windows, dz_other, dz_own = lax.optimization_barrier((windows, dz_other, dz_own))
-    d_hn_left = lax.psum_scatter(windows.reshape(model_size * chip_cap, half), "model", scatter_dimension=0, tiled=True)
-    d_hn_other = head_dhn(dz_other, table_shard, half, 1)
+    d_hn_left = lax.psum_scatter(windows.reshape(model_size * chip_cap, left), "model", scatter_dimension=0, tiled=True)
+    d_hn_other = head_dhn(dz_other, table_shard, right, left // right)
     d_hn_theirs = swap_cores(d_hn_other)
-    d_hn_own = head_dhn(dz_own, table_shard, half, 1)
+    d_hn_own = head_dhn(dz_own, table_shard, right, left // right)
     windows = sum_windows(d_hn_own, d_hn_theirs, first, chip_cap)
     windows, dz_other, dz_own = lax.optimization_barrier((windows, dz_other, dz_own))
-    d_hn_right = lax.psum_scatter(windows.reshape(model_size * chip_cap, half), "model", scatter_dimension=0, tiled=True)
+    d_hn_right = lax.psum_scatter(windows.reshape(model_size * chip_cap, right), "model", scatter_dimension=0, tiled=True)
     d_head = head_dtable(dz_own, hn_own, dz_other, hn_other, None)
     d_hn_left, d_hn_right, d_head = lax.optimization_barrier((d_hn_left, d_hn_right, d_head))
     d_hn = jnp.concatenate([d_hn_left, d_hn_right], axis=1)
@@ -484,8 +489,7 @@
     dm_blocks, d_head = lax.optimization_barrier((dm_blocks, d_head))
     d_mlp = place_rows(dm_blocks, first, count, jnp.bfloat16)
 
-    d_gate, d_up = mlp_dact(d_mlp, w_down, gate_bf, up_bf)
-    grad_down = jnp.einsum("tf,td->fd", act_bf, d_mlp, preferred_element_type=jnp.float32)
+    d_gate, d_up, grad_down = mlp_dact(d_mlp, w_down, gate_bf, up_bf, act_bf)
     grad_gate = jnp.einsum("td,tf->df", normed_bf, d_gate, preferred_element_type=jnp.float32)
     grad_up = jnp.einsum("td,tf->df", normed_bf, d_up, preferred_element_type=jnp.float32)
     d_gate_own = lax.dynamic_slice(d_gate, (my_first, 0), (chip_cap, d_gate.shape[1]))

time: 729 us -> 717 us (0.984)
  matrix products: 90.5 us -> 67.2 us
  local copies, waits for them, and re-layouts: 32.9 us -> 49.8 us
  waiting for transfers between devices: 65.8 us -> 49.6 us
  Pallas kernels: 425 us -> 436 us
    dot_general x1 -> x0, matrix products: 23.7 us -> none  [fast_step(): jnp.einsum('tf,td->fd', act_bf, d_mlp, preferred_element_type=jnp.float32)]
    all_gather x1, waiting for transfers between devices: 27.7 us -> 10.7 us  [fast_step(): blocks = lax.all_gather(pair, 'model', axis=0, tiled=True)]
    another operation x5 -> x6, local copies, waits for them, and re-layouts: 2.06 us -> 19 us
    pallas_call x1, Pallas kernels: 36.5 us -> 52 us  [mlp_dact(): pl.pallas_call(functools.partial(dact_kernel, rows), grid=(width // cols,...]
  transfers between devices with their start and end apart: 15 -> 15, of which waited for: 3 -> 3; matrix products, arithmetic and copies ran while one was open for 19% -> 18% of each run, Pallas kernels for 35% -> 30%
where the time goes in v3:
time: 717 us; the launch traced here: 710 us
  Pallas kernels  436 us (61%)
  matrix products  67.2 us (9%)
  other arithmetic  53.5 us (7%)
  local copies, waits for them, and re-layouts  49.8 us (7%)
  waiting for transfers between devices  49.6 us (7%)
  between operations  21 us (3%)
  loops' own time  16.9 us (2%)
  blocking collectives  14.6 us (2%)
    pallas_call x2, Pallas kernels, head_logits(): pl.pallas_call(functools.partial(logits_kernel, chunk), grid=(tokens // b...  83.7 us
    pallas_call x1, Pallas kernels, mlp_forward_kernel(): pl.pallas_call(functools.partial(mlp_kernel, chunk), grid=(tokens // blk,...  69.7 us
    pallas_call x2, Pallas kernels, head_dtable(): pl.pallas_call(dtable_kernel, grid=(steps,), in_specs=[dz_spec, hn_spec,...  69.2 us
    pallas_call x2, Pallas kernels, head_dlogits(): pl.pallas_call(functools.partial(dlogits_kernel, inv_tokens, chunk), grid...  68.9 us
    pallas_call x1, Pallas kernels, mlp_dact(): pl.pallas_call(functools.partial(dact_kernel, rows), grid=(width // cols,...  52 us
    pallas_call x2, Pallas kernels, head_dhn(): pl.pallas_call(dhn_kernel, grid=(tokens // blk,), in_specs=[pl.BlockSpec(...  40 us
    select_n x4, other arithmetic, by_core(): jnp.where(core == 0, jnp.concatenate([mine, theirs]), jnp.concatenate([th...  30 us
    all_gather x1, waiting for transfers between devices, fast_step(): dm_blocks = lax.all_gather(d_hidden.astype(jnp.bfloat16), 'model', axis=0)  28.1 us
  transfers between devices with their start and end apart: 15, of which 3 were waited for; matrix products, arithmetic and copies ran while one was open for 18% of the time, Pallas kernels for 30%

profile of v3, /device:TPU:0, one launch (start us, length us, event | category | flops | bytes accessed | tf_op | source)
XLA Modules:
  0.0 710.1 jit_solution(586543924568604555)
XLA Ops:
  7.2 0.7 pad_add_fusion
  7.9 2.3 all_gather.19
  10.8 0.4 collective-permute-start.6
  11.1 5.9 sort.23
  17.1 1.0 reshape.323
  18.8 0.6 fusion.67
  23.7 10.3 %gather_fusion.1 = bf16[608,1024]{1,0:T(8,128)(2,1)S(1)} fusion(bf16[6288,1024]{1,0:T(8,128)(2,1)} %param.12, s32[1024]{0:T(1024)S(1)} %pad_clamp_fusion), kind=kCustom, calls=%fused_computation.1 | custom fusion | bytes 2492800 | tf_op jit(solution)/shard_map/jit(_take)/gather | solution.py:426
  34.0 1.1 fusion.65
  35.3 1.0 reshape.324
  36.3 0.6 subtract_reduce_fusion.2
  37.6 0.6 fusion.59
  38.9 0.8 copy-done.9
  39.7 2.2 pad_maximum_fusion.2
  42.0 659.7 %conditional.1 = (f32[]{:T(128)}, f32[6288,1024]{1,0:T(8,128)}, f32[512,4096]{1,0:T(8,128)}, f32[512,4096]{1,0:T(8,128)}, f32[2048,1024]{1,0:T(8,128)}) conditional(s32[]{:T(128)} %convert_element_type.57, (s32[1,2048]{1,0:T(1,128)}, bf16[6288,1024]{1,0:T(8,128)(2,1)}, f32[1024]{0:T(1024)S(1)}, bf16[512,4096]{1,0:T(8,128)(2,1)}, ...), branch_computations={%region_4.23_spmd, %region_23.38_spmd} | conditional | flops 313810911232 | bytes 1838356736 | solution.py:550
  50.5 1.2 broadcast_select_fusion
  51.7 17.7 %copy.51 = bf16[6288,1024]{0,1:T(8,128)(2,1)} copy(bf16[6288,1024]{1,0:T(8,128)(2,1)} %get-tuple-element.75.emb_ref) | data formatting | bytes 25755648 | tf_op jit(solution)/shard_map
  69.5 0.9 copy.60
  70.4 0.5 fusion.16.start_ref
  70.9 10.6 %maximum_select_fusion.2.wd_ref = bf16[4096,1024]{1,0:T(8,128)(2,1)} fusion(bf16[2048,1024]{1,0:T(8,128)(2,1)} %get-tuple-element.81, bf16[2048,1024]{1,0:T(8,128)(2,1)} %get-tuple-element.80, pred[]{:T(512)S(6)} %eq.16), kind=kLoop, calls=%fused_computation.5 | loop fusion | flops 37748736 | bytes 16777216 | tf_op jit(solution)/shard_map/cond/branch_1_fun/jit(_where)/select_n | solution.py:416
  81.6 1.0 copy-done.8
  82.6 16.0 %maximum_select_fusion = (bf16[1024,4096]{1,0:T(8,128)(2,1)}, bf16[1024,4096]{1,0:T(8,128)(2,1)}) fusion(bf16[512,4096]{1,0:T(8,128)(2,1)} %get-tuple-element.77, bf16[512,4096]{1,0:T(8,128)(2,1)S(1)} %copy-done.7, pred[]{:T(512)S(6)} %eq.16, bf16[512,4096]{1,0:T(8,128)(2,1)S(1)} %copy-done.8, bf16[512,4096]{1,0:T(8,128)(2,1)} %get-tuple-element.79), kind=kLoop, calls=%fused_computation.3 | loop fusion | flops 75497472 | bytes 33554432 | tf_op jit(solution)/shard_map/cond/branch_1_fun/jit(_where)/select_n | solution.py:416
  98.6 10.7 %all-gather.7.cloned.1.call-done.block_ref = bf16[8,304,1024]{2,1,0:T(8,128)(2,1)} async-done(((bf16[2,304,1024]{2,1,0:T(8,128)(2,1)}), bf16[8,304,1024]{2,1,0:T(8,128)(2,1)}) %all-gather.7.cloned.1.call-update) | async-done | bytes 4980752 | tf_op jit(solution)/shard_map/cond/branch_1_fun/all_gather | solution.py:445
  109.3 9.5 %place_rows.2.x_ref = f32[2360,1024]{1,0:T(8,128)} custom-call(s32[9]{0:T(128)} %fusion.16.start_ref, bf16[8,304,1024]{2,1,0:T(8,128)(2,1)} %all-gather.7.cloned.1.call-done.block_ref), custom_call_target="tpu_custom_call" | custom-call | flops 19333120 | bytes 19333120 | tf_op jit(solution)/shard_map/cond/branch_1_fun/place_rows/pallas_call | solution.py:361
  118.8 69.7 %mlp_forward.1 = (bf16[2048,1024]{1,0:T(8,128)(2,1)}, bf16[2048,4096]{1,0:T(8,128)(2,1)}, bf16[2048,4096]{1,0:T(8,128)(2,1)}, bf16[2048,4096]{1,0:T(8,128)(2,1)}...) custom-call(f32[2360,1024]{1,0:T(8,128)} %place_rows.2.x_ref, f32[1,1024]{1,0:T(1,128)S(1)} %bitcast.105, ...), custom_call_target="tpu_custom_call" | custom-call | flops 51539607552 | bytes 50331648 | tf_op jit(solution)/shard_map/cond/branch_1_fun/mlp_forward/pallas_call | solution.py:266
  188.5 1.1 subtract_select_fusion
  189.7 1.5 dynamic-slice_bitcast_fusion.1
  191.1 41.9 %head_logits.2 = (f32[2048,6288]{1,0:T(8,128)}, f32[2048,128]{1,0:T(8,128)}) custom-call(bf16[2048,1024]{1,0:T(8,128)(2,1)} %get-tuple-element.88.hn_ref.ha_ref, bf16[1024,6288]{1,0:T(8,128)(2,1)} %bitcast.81, s32[2048,128]{1,0:T(8,128)} %get-tuple-element.201.off_ref), custom_call_target="tpu_custom_call" | custom-call | flops 26373783552 | bytes 51511296 | tf_op jit(solution)/shard_map/cond/branch_1_fun/head_logits/pallas_call | solution.py:127
  233.1 2.3 slice_bitcast_fusion.1
  235.3 41.8 %head_logits.3 = (f32[2048,6288]{1,0:T(8,128)}, f32[2048,128]{1,0:T(8,128)}) custom-call(bf16[2048,1024]{1,0:T(8,128)(2,1)} %collective-permute-done.hn_ref.hb_ref, bf16[1024,6288]{1,0:T(8,128)(2,1)} %bitcast.82, s32[2048,128]{1,0:T(8,128)} %get-tuple-element.202.off_ref), custom_call_target="tpu_custom_call" | custom-call | flops 26373783552 | bytes 51511296 | tf_op jit(solution)/shard_map/cond/branch_1_fun/head_logits/pallas_call | solution.py:127
  277.1 1.3 slice_bitcast_fusion
  278.4 2.2 maximum_select_fusion.3
  280.9 12.3 %all_gather.15 = f32[8,6,2048]{2,1,0:T(8,128)S(1)} all-gather(f32[1,6,2048]{2,1,0:T(8,128)S(1)} %copy.52), channel_id=1, replica_groups=mesh['model'=4,'fsdp'=2] {'model','fsdp'}, dimensions={0}, use_global_device_ids=true | all-gather | bytes 442368 | tf_op jit(solution)/shard_map/cond/branch_1_fun/all_gather | solution.py:458
  293.6 0.7 divide_multiply_fusion
  294.4 1.3 broadcast_in_dim.104.scale_ref
  295.7 1.3 broadcast_in_dim.102.max_ref
  297.0 34.6 %head_dlogits.3 = (bf16[2048,6288]{1,0:T(8,128)(2,1)}, f32[2048,512]{1,0:T(8,128)}) custom-call(f32[2048,6288]{1,0:T(8,128)} %get-tuple-element.96.z_ref, bf16[6288,1024]{1,0:T(8,128)(2,1)} %get-tuple-element.75.emb_ref, f32[2048,128]{1,0:T(8,128)} %broadcast_in_dim.102.max_ref, f32[2048,128]{1,0:T(8,128)} %broadcast_in_dim.104.scale_ref, ...), custom_call_target="tpu_custom_call" | custom-call | flops 13186891776 | bytes 77266944 | tf_op jit(solution)/shard_map/cond/branch_1_fun/head_dlogits/pallas_call | solution.py:167
  331.8 0.5 broadcast_minimum_fusion.first_ref.start_ref
  332.3 1.3 broadcast_in_dim.100.scale_ref
  333.6 1.3 broadcast_in_dim.98.max_ref
  334.9 34.3 %head_dlogits.2 = (bf16[2048,6288]{1,0:T(8,128)(2,1)}, f32[2048,512]{1,0:T(8,128)}) custom-call(f32[2048,6288]{1,0:T(8,128)} %get-tuple-element.94.z_ref, bf16[6288,1024]{1,0:T(8,128)(2,1)} %get-tuple-element.75.emb_ref, f32[2048,128]{1,0:T(8,128)} %broadcast_in_dim.98.max_ref, f32[2048,128]{1,0:T(8,128)} %broadcast_in_dim.100.scale_ref, ...), custom_call_target="tpu_custom_call" | custom-call | flops 13186891776 | bytes 77266944 | tf_op jit(solution)/shard_map/cond/branch_1_fun/head_dlogits/pallas_call | solution.py:167
  369.2 6.9 sum_windows.2
  376.2 20.1 %head_dhn.3 = f32[2048,512]{1,0:T(8,128)} custom-call(bf16[2048,6288]{1,0:T(8,128)(2,1)} %get-tuple-element.105.dz_ref.b_ref, bf16[6288,1024]{1,0:T(8,128)(2,1)} %get-tuple-element.75.emb_ref), custom_call_target="tpu_custom_call" | custom-call | flops 13186891776 | bytes 25755648 | tf_op jit(solution)/shard_map/cond/branch_1_fun/head_dhn/pallas_call | solution.py:194
  396.2 0.5 collective-permute-start.2
  396.7 20.0 %head_dhn.2.a_ref = f32[2048,512]{1,0:T(8,128)} custom-call(bf16[2048,6288]{1,0:T(8,128)(2,1)} %get-tuple-element.104.dz_ref.a_ref, bf16[6288,1024]{1,0:T(8,128)(2,1)} %get-tuple-element.75.emb_ref), custom_call_target="tpu_custom_call" | custom-call | flops 13186891776 | bytes 25755648 | tf_op jit(solution)/shard_map/cond/branch_1_fun/head_dhn/pallas_call | solution.py:194
  416.7 7.0 sum_windows.3
  423.8 0.6 dynamic_slice.56
  426.3 46.0 %head_dtable.2.refs_0_ = f32[6288,1024]{1,0:T(8,128)} custom-call(bf16[2048,6288]{1,0:T(8,128)(2,1)} %get-tuple-element.104.dz_ref.a_ref, bf16[2048,1024]{1,0:T(8,128)(2,1)} %get-tuple-element.88.hn_ref.ha_ref, bf16[2048,6288]{1,0:T(8,128)(2,1)} %get-tuple-element.105.dz_ref.b_ref, bf16[2048,1024]{1,0:T(8,128)(2,1)} %collective-permute-done.hn_ref.hb_ref), custom_call_target="tpu_custom_call" | custom-call | flops 37580963840 | bytes 36700160 | tf_op jit(solution)/shard_map/cond/branch_1_fun/head_dtable/pallas_call | solution.py:224
  472.3 10.1 %reduce-scatter.20.cloned.1.call-done = f32[576,512]{1,0:T(8,128)} async-done(((f32[2304,512]{1,0:T(8,128)}), f32[576,512]{1,0:T(8,128)}) %reduce-scatter.20.cloned.1.call-update) | async-done | bytes 1179664 | tf_op jit(solution)/shard_map/cond/branch_1_fun/reduce_scatter | solution.py:479
  482.4 3.0 multiply_reduce_fusion.3
  485.4 0.6 copy-done.27
  486.0 4.0 fusion.17
  490.0 23.2 %head_dtable.3.base_ref = f32[6288,1024]{1,0:T(8,128)} custom-call(bf16[2048,6288]{1,0:T(8,128)(2,1)} %get-tuple-element.104.dz_ref.a_ref, bf16[2048,1024]{1,0:T(8,128)(2,1)} %get-tuple-element.88.hn_ref.ha_ref, bf16[2048,6288]{1,0:T(8,128)(2,1)} %get-tuple-element.105.dz_ref.b_ref, ...), custom_call_target="tpu_custom_call", output_to_operand_aliasing={{}: (4, {})} | custom-call | flops 16106127360 | bytes 15728640 | tf_op jit(solution)/shard_map/cond/branch_1_fun/head_dtable/pallas_call | solution.py:224
  513.2 28.1 %all-gather.9.cloned.1.call-done = bf16[2304,1024]{1,0:T(8,128)(2,1)} async-done(((bf16[576,1024]{1,0:T(8,128)(2,1)}), bf16[2304,1024]{1,0:T(8,128)(2,1)}) %all-gather.9.cloned.1.call-update) | async-done | bytes 4718608 | tf_op jit(solution)/shard_map/cond/branch_1_fun/all_gather | solution.py:487
  541.3 6.6 place_rows.3.dm_ref
  547.9 52.0 %mlp_dact.1 = (bf16[2048,4096]{1,0:T(8,128)(2,1)}, bf16[2048,4096]{1,0:T(8,128)(2,1)}, f32[4096,1024]{1,0:T(8,128)}) custom-call(bf16[2048,1024]{1,0:T(8,128)(2,1)} %place_rows.3.dm_ref, bf16[4096,1024]{1,0:T(8,128)(2,1)} %maximum_select_fusion.2.wd_ref, bf16[2048,4096]{1,0:T(8,128)(2,1)} %get-tuple-element.112.gt_ref, ...), custom_call_target="tpu_custom_call" | custom-call | flops 34359738368 | bytes 83886080 | tf_op jit(solution)/shard_map/cond/branch_1_fun/mlp_dact/pallas_call | solution.py:294
  599.9 24.1 %fusion.69 = f32[1024,4096]{1,0:T(8,128)} fusion(bf16[2048,1024]{1,0:T(8,128)(2,1)} %get-tuple-element.117, bf16[2048,4096]{1,0:T(8,128)(2,1)} %get-tuple-element.116), kind=kOutput, calls=%fused_computation.161 | convolution fusion | flops 17179869184 | bytes 37748736 | tf_op jit(solution)/shard_map/cond/branch_1_fun/td,tf->df/dot_general | solution.py:494
  624.0 23.9 %fusion.68 = f32[1024,4096]{1,0:T(8,128)} fusion(bf16[2048,1024]{1,0:T(8,128)(2,1)} %get-tuple-element.117, bf16[2048,4096]{1,0:T(8,128)(2,1)} %get-tuple-element.115), kind=kOutput, calls=%fused_computation.160 | convolution fusion | flops 17179869184 | bytes 37748736 | tf_op jit(solution)/shard_map/cond/branch_1_fun/td,tf->df/dot_general | solution.py:493
  648.1 0.7 reduce-scatter.26.cloned.1.call-update
  650.0 9.2 %fusion = f32[576,1024]{1,0:T(8,128)S(1)} fusion(bf16[1024,4096]{1,0:T(8,128)(2,1)} %get-tuple-element.86.wu_ref, bf16[2048,4096]{1,0:T(8,128)(2,1)} %get-tuple-element.116, s32[]{:T(128)S(6)} %select_n.176), kind=kOutput, calls=%fused_computation.6 | convolution fusion | flops 4831838208 | bytes 15466500 | tf_op jit(solution)/shard_map/cond/branch_1_fun/tf,df->td/dot_general | solution.py:498
  659.3 10.0 %multiply_reduce_fusion.1 = (f32[576]{0:T(1024)S(1)}, f32[576]{0:T(1024)S(1)}, f32[576,1024]{1,0:T(8,128)S(1)}) fusion(f32[2360,1024]{1,0:T(8,128)} %place_rows.2.x_ref, s32[]{:T(128)S(6)} %select_n.177, f32[1024]{0:T(1024)S(1)} %copy-done.54, f32[576,1024]{1,0:T(8,128)S(1)} %fusion, bf16[1024,4096]{1,0:T(8,128)(2,1)} %get-tuple-element.85.wg_ref, ...), kind=kOutput, calls=%fused_computation.15 | convolution fusion | flops 4835376128 | bytes 20193800 | tf_op jit(solution)/shard_map/cond/branch_1_fun/tf,df->td/dot_general | solution.py:498
  669.4 3.1 fusion.4.own_ref
  672.6 0.7 constant_dynamic-slice_fusion.5
  677.9 0.7 copy.54.bound_ref
  679.3 22.1 %add_rows.1 = f32[6288,1024]{1,0:T(8,128)} custom-call(s32[2,7]{1,0:T(2,128)} %copy.54.bound_ref, s32[2,576]{1,0:T(2,128)} %copy-done.26, f32[6288,1024]{1,0:T(8,128)} %head_dtable.3.base_ref, f32[576,1024]{1,0:T(8,128)} %copy-done.6, f32[576,1024]{1,0:T(8,128)} %collective-permute-done.3.theirs_ref), custom_call_target="tpu_custom_call", output_to_operand_aliasing={{}: (2, {})} | custom-call | flops 12877824 | bytes 51511296 | tf_op jit(solution)/shard_map/cond/branch_1_fun/add_rows/pallas_call | solution.py:321
  (112 shorter events, 4.2 us)
Async XLA Ops:
  10.2 31.7 %collective-permute-start.4 = (bf16[512,4096]{1,0:T(8,128)(2,1)}, bf16[512,4096]{1,0:T(8,128)(2,1)}, u32[]{:S(2)}, u32[]{:S(2)}) collective-permute-start(bf16[512,4096]{1,0:T(8,128)(2,1)} %param.13), channel_id=1, source_target_pairs={{0,1},{1,0},{2,3},{3,2},{4,5},{5,4},{6,7},{7,6}} | collective-permute-start | bytes 12582920 | tf_op jit(solution)/shard_map/ppermute | solution.py:412
  10.6 31.3 %collective-permute-start.5 = (bf16[512,4096]{1,0:T(8,128)(2,1)}, bf16[512,4096]{1,0:T(8,128)(2,1)}, u32[]{:S(2)}, u32[]{:S(2)}) collective-permute-start(bf16[512,4096]{1,0:T(8,128)(2,1)} %param.14), channel_id=1, source_target_pairs={{0,1},{1,0},{2,3},{3,2},{4,5},{5,4},{6,7},{7,6}} | collective-permute-start | bytes 12582920 | tf_op jit(solution)/shard_map/ppermute | solution.py:412
  10.8 31.2 %collective-permute-start.6 = (bf16[2048,1024]{1,0:T(8,128)(2,1)}, bf16[2048,1024]{1,0:T(8,128)(2,1)}, u32[]{:S(2)}, u32[]{:S(2)}) collective-permute-start(bf16[2048,1024]{1,0:T(8,128)(2,1)} %param.15), channel_id=1, source_target_pairs={{0,1},{1,0},{2,3},{3,2},{4,5},{5,4},{6,7},{7,6}} | collective-permute-start | bytes 12582920 | tf_op jit(solution)/shard_map/ppermute | solution.py:412
  18.1 18.2 %copy-start.2 = (s32[2048,2]{1,0:T(8,128)}, s32[2048,2]{1,0:T(8,128)S(1)}, u32[]{:S(2)}) copy-start(s32[2048,2]{1,0:T(8,128)S(1)} %reshape.323) | copy-start | bytes 49156
  18.8 20.1 %copy-start.12 = (s32[2,9]{0,1:T(8,128)}, s32[2,9]{0,1:T(8,128)S(1)}, u32[]{:S(2)}) copy-start(s32[2,9]{0,1:T(8,128)S(1)} %fusion.58) | copy-start | bytes 220
  23.7 18.2 %copy-start.14 = (f32[1024]{0:T(1024)S(1)}, f32[1024]{0:T(1024)}, u32[]{:S(2)}) copy-start(f32[1024]{0:T(1024)} %param.17) | copy-start | bytes 12292
  23.7 18.2 %copy-start.35 = (s32[1,2048]{1,0:T(1,128)S(1)}, s32[1,2048]{1,0:T(1,128)}, u32[]{:S(2)}) copy-start(s32[1,2048]{1,0:T(1,128)} %param.11) | copy-start | bytes 24580
  23.7 18.2 %copy-start.50 = (f32[1024]{0:T(1024)S(1)}, f32[1024]{0:T(1024)}, u32[]{:S(2)}) copy-start(f32[1024]{0:T(1024)} %param.16) | copy-start | bytes 12292
  35.1 3.8 collective-permute-start.7
  38.9 0.8 copy-start.9
  50.4 68.4 %copy-start.17 = (f32[1024]{0:T(1024)}, f32[1024]{0:T(1024)S(1)}, u32[]{:S(2)}) copy-start(f32[1024]{0:T(1024)S(1)} %get-tuple-element.84) | copy-start | bytes 12292 | tf_op jit(solution)/shard_map/cond
  50.4 68.4 %copy-start.53 = (f32[1024]{0:T(1024)}, f32[1024]{0:T(1024)S(1)}, u32[]{:S(2)}) copy-start(f32[1024]{0:T(1024)S(1)} %get-tuple-element.83) | copy-start | bytes 12292 | tf_op jit(solution)/shard_map/cond
  50.4 58.9 %all-gather.7.cloned.1.call-start = ((), (), s32[]{:S(2)}) async-start(), calls=%async_computation.16 | async-start | bytes 6225920 | tf_op jit(solution)/shard_map/cond/branch_1_fun/all_gather | solution.py:445
  51.7 420.7 %reduce-scatter.18.cloned.1.call-start = ((), (), s32[]{:S(2)}) async-start(), calls=%async_computation.17 | async-start | bytes 5898240 | tf_op jit(solution)/shard_map/cond/branch_1_fun/reduce_scatter | solution.py:473
  51.7 17.7 %copy-start.13 = (s32[2,9]{0,1:T(8,128)S(1)}, s32[2,9]{0,1:T(8,128)}, u32[]{:S(2)}) copy-start(s32[2,9]{0,1:T(8,128)} %get-tuple-element.171) | copy-start | bytes 220 | tf_op jit(solution)/shard_map/cond
  69.5 12.1 %copy-start.47 = (s32[2,9]{1,0:T(2,128)}, s32[2,9]{1,0:T(2,128)S(1)}, u32[]{:S(2)}) copy-start(s32[2,9]{1,0:T(2,128)S(1)} %copy.59) | copy-start | bytes 220 | tf_op jit(solution)/shard_map/cond
  70.9 10.7 %copy-start.7 = (bf16[512,4096]{1,0:T(8,128)(2,1)S(1)}, bf16[512,4096]{1,0:T(8,128)(2,1)}, u32[]{:S(2)}) copy-start(bf16[512,4096]{1,0:T(8,128)(2,1)} %get-tuple-element.76) | copy-start | bytes 12582916 | tf_op jit(solution)/shard_map/cond
  70.9 11.7 %copy-start.8 = (bf16[512,4096]{1,0:T(8,128)(2,1)S(1)}, bf16[512,4096]{1,0:T(8,128)(2,1)}, u32[]{:S(2)}) copy-start(bf16[512,4096]{1,0:T(8,128)(2,1)} %get-tuple-element.78) | copy-start | bytes 12582916 | tf_op jit(solution)/shard_map/cond
  118.8 69.7 %copy-start.25 = (s32[2,2048]{1,0:T(2,128)S(1)}, s32[2,2048]{1,0:T(2,128)}, u32[]{:S(2)}) copy-start(s32[2,2048]{1,0:T(2,128)} %copy.60) | copy-start | bytes 49156 | tf_op jit(solution)/shard_map/cond
  188.5 46.9 %collective-permute-start = (bf16[2048,1024]{1,0:T(8,128)(2,1)}, bf16[2048,1024]{1,0:T(8,128)(2,1)}, u32[]{:S(2)}, u32[]{:S(2)}) collective-permute-start(bf16[2048,1024]{1,0:T(8,128)(2,1)} %get-tuple-element.88.hn_ref.ha_ref), channel_id=1, source_target_pairs={{0,1},{1,0},{2,3},{3,2},{4,5},{5,4},{6,7},{7,6}} | collective-permute-start | bytes 12582920 | tf_op jit(solution)/shard_map/cond/branch_1_fun/ppermute | solution.py:412
  297.0 34.7 %copy-start.49 = (s32[9]{0:T(128)S(1)}, s32[9]{0:T(128)}, u32[]{:S(2)}) copy-start(s32[9]{0:T(128)} %fusion.16.start_ref) | copy-start | bytes 112 | tf_op jit(solution)/shard_map/cond
  331.6 37.5 %collective-permute-start.1 = (f32[2048,512]{1,0:T(8,128)}, f32[2048,512]{1,0:T(8,128)}, u32[]{:S(2)}, u32[]{:S(2)}) collective-permute-start(f32[2048,512]{1,0:T(8,128)} %get-tuple-element.97), channel_id=1, source_target_pairs={{0,1},{1,0},{2,3},{3,2},{4,5},{5,4},{6,7},{7,6}} | collective-permute-start | bytes 12582920 | tf_op jit(solution)/shard_map/cond/branch_1_fun/ppermute | solution.py:412
  376.1 106.3 %reduce-scatter.20.cloned.1.call-start = ((), (), s32[]{:S(2)}) async-start(), calls=%async_computation.18 | async-start | bytes 5898240 | tf_op jit(solution)/shard_map/cond/branch_1_fun/reduce_scatter | solution.py:479
  396.2 20.5 %collective-permute-start.2 = (f32[2048,512]{1,0:T(8,128)}, f32[2048,512]{1,0:T(8,128)}, u32[]{:S(2)}, u32[]{:S(2)}) collective-permute-start(f32[2048,512]{1,0:T(8,128)} %head_dhn.3), channel_id=1, source_target_pairs={{0,1},{1,0},{2,3},{3,2},{4,5},{5,4},{6,7},{7,6}} | collective-permute-start | bytes 12582920 | tf_op jit(solution)/shard_map/cond/branch_1_fun/ppermute | solution.py:412
  416.7 7.1 copy-start.46
  423.7 117.6 %all-gather.9.cloned.1.call-start = ((), (), s32[]{:S(2)}) async-start(), calls=%async_computation.22 | async-start | bytes 5898240 | tf_op jit(solution)/shard_map/cond/branch_1_fun/all_gather | solution.py:487
  426.3 56.1 %copy-start.18 = (f32[1024]{0:T(1024)S(1)}, f32[1024]{0:T(1024)}, u32[]{:S(2)}) copy-start(f32[1024]{0:T(1024)} %copy-done.17) | copy-start | bytes 12292 | tf_op jit(solution)/shard_map/cond
  485.4 0.6 copy-start.27
  485.4 0.6 copy-start.29
  490.0 211.3 %reduce-scatter.24.cloned.1.call-start = ((), (), s32[]{:S(2)}) async-start(), calls=%async_computation.20 | async-start | bytes 25165824 | tf_op jit(solution)/shard_map/cond/branch_1_fun/reduce_scatter | solution.py:511
  624.0 77.3 %reduce-scatter.22.cloned.1.call-start = ((), (), s32[]{:S(2)}) async-start(), calls=%async_computation.19 | async-start | bytes 25165824 | tf_op jit(solution)/shard_map/cond/branch_1_fun/reduce_scatter | solution.py:510
  648.0 53.3 %reduce-scatter.26.cloned.1.call-start = ((), (), s32[]{:S(2)}) async-start(), calls=%async_computation.21 | async-start | bytes 25165824 | tf_op jit(solution)/shard_map/cond/branch_1_fun/reduce_scatter | solution.py:512
  650.0 9.2 %copy-start.54 = (f32[1024]{0:T(1024)S(1)}, f32[1024]{0:T(1024)}, u32[]{:S(2)}) copy-start(f32[1024]{0:T(1024)} %copy-done.53) | copy-start | bytes 12292 | tf_op jit(solution)/shard_map/cond
  659.3 10.1 %copy-start.4 = (f32[576,512]{1,0:T(8,128)S(1)}, f32[576,512]{1,0:T(8,128)}, u32[]{:S(2)}) copy-start(f32[576,512]{1,0:T(8,128)} %reduce-scatter.18.cloned.1.call-done) | copy-start | bytes 3538948 | tf_op jit(solution)/shard_map/cond
  659.3 10.1 %copy-start.5 = (f32[576,512]{1,0:T(8,128)S(1)}, f32[576,512]{1,0:T(8,128)}, u32[]{:S(2)}) copy-start(f32[576,512]{1,0:T(8,128)} %reduce-scatter.20.cloned.1.call-done) | copy-start | bytes 3538948 | tf_op jit(solution)/shard_map/cond
  659.3 10.1 %copy-start.19 = (f32[1024]{0:T(1024)S(1)}, f32[1024]{0:T(1024)}, u32[]{:S(2)}) copy-start(f32[1024]{0:T(1024)} %copy-done.17) | copy-start | bytes 12292 | tf_op jit(solution)/shard_map/cond
  659.3 10.1 %copy-start.28 = (f32[576]{0:T(1024)S(1)}, f32[576]{0:T(1024)}, u32[]{:S(2)}) copy-start(f32[576]{0:T(1024)} %copy-done.27) | copy-start | bytes 6916 | tf_op jit(solution)/shard_map/cond
  659.3 10.1 %copy-start.30 = (f32[576]{0:T(1024)S(1)}, f32[576]{0:T(1024)}, u32[]{:S(2)}) copy-start(f32[576]{0:T(1024)} %copy-done.29) | copy-start | bytes 6916 | tf_op jit(solution)/shard_map/cond
  669.3 3.3 copy-start.48
  669.3 6.5 copy-start.3
  672.5 3.7 copy-start.6
  672.5 6.7 collective-permute-start.3
  677.6 1.7 copy-start.26
Sparse Core Ops, SparseCore 0:
  53.6 55.6 all-gather.6
  376.3 51.3 reduce-scatter.17
  431.2 51.2 reduce-scatter.19
  490.1 51.1 all-gather.8
  624.1 21.8 reduce-scatter.23
  648.7 22.9 reduce-scatter.21
  674.5 23.0 reduce-scatter.25

commit v4 on v3

--- a/solution.py
+++ b/solution.py
@@ -490,8 +490,6 @@
     d_mlp = place_rows(dm_blocks, first, count, jnp.bfloat16)
 
     d_gate, d_up, grad_down = mlp_dact(d_mlp, w_down, gate_bf, up_bf, act_bf)
-    grad_gate = jnp.einsum("td,tf->df", normed_bf, d_gate, preferred_element_type=jnp.float32)
-    grad_up = jnp.einsum("td,tf->df", normed_bf, d_up, preferred_element_type=jnp.float32)
     d_gate_own = lax.dynamic_slice(d_gate, (my_first, 0), (chip_cap, d_gate.shape[1]))
     d_up_own = lax.dynamic_slice(d_up, (my_first, 0), (chip_cap, d_up.shape[1]))
     x_window = lax.dynamic_slice(x_buf, (my_first, 0), (chip_cap, depth))
@@ -505,6 +503,9 @@
     own_ids = jnp.stack([lax.dynamic_slice(sorted_ids, (p, pair_first[p]), (1, chip_cap))[0] for p in (core, 1 - core)]) - device * vocab
     edges = jnp.arange(vocab // tile + 1, dtype=jnp.int32) * tile
     bounds = jnp.sum((own_ids[:, :, None] < edges[None, None, :]).astype(jnp.int32), axis=1)
+    d_gate, d_up, d_x, own_ids, bounds = lax.optimization_barrier((d_gate, d_up, d_x, own_ids, bounds))
+    grad_gate = jnp.einsum("td,tf->df", normed_bf, d_gate, preferred_element_type=jnp.float32)
+    grad_up = jnp.einsum("td,tf->df", normed_bf, d_up, preferred_element_type=jnp.float32)
     grad_table = add_rows(d_head, d_x, d_x_theirs, own_ids, bounds, tile)
 
     grad_gate = lax.psum_scatter(grad_gate, "fsdp", scatter_dimension=0, tiled=True)

time: 717 us -> 734 us (1.024)
  waiting for transfers between devices: 49.6 us -> 66.4 us
    reduce_scatter x1, waiting for transfers between devices: 0.01 us -> 22.2 us  [fast_step(): lax.psum_scatter(grad_down, 'fsdp', scatter_dimension=0, tiled=True)]
    all_gather x1, waiting for transfers between devices: 28.1 us -> 20.2 us  [fast_step(): dm_blocks = lax.all_gather(d_hidden.astype(jnp.bfloat16), 'model', axis=0)]
  transfers between devices with their start and end apart: 15 -> 15, of which waited for: 3 -> 5; matrix products, arithmetic and copies ran while one was open for 18% -> 15% of each run, Pallas kernels for 30% -> 30%
where the time goes in v4:
time: 734 us; the launch traced here: 726 us
  Pallas kernels  436 us (59%)
  waiting for transfers between devices  66.4 us (9%)
  matrix products  66.2 us (9%)
  other arithmetic  54.2 us (7%)
  local copies, waits for them, and re-layouts  50.1 us (7%)
  between operations  20.8 us (3%)
  loops' own time  16.3 us (2%)
  blocking collectives  14.7 us (2%)
    pallas_call x2, Pallas kernels, head_logits(): pl.pallas_call(functools.partial(logits_kernel, chunk), grid=(tokens // b...  83.7 us
    pallas_call x1, Pallas kernels, mlp_forward_kernel(): pl.pallas_call(functools.partial(mlp_kernel, chunk), grid=(tokens // blk,...  69.8 us
    pallas_call x2, Pallas kernels, head_dtable(): pl.pallas_call(dtable_kernel, grid=(steps,), in_specs=[dz_spec, hn_spec,...  69.4 us
    pallas_call x2, Pallas kernels, head_dlogits(): pl.pallas_call(functools.partial(dlogits_kernel, inv_tokens, chunk), grid...  68.6 us
    pallas_call x1, Pallas kernels, mlp_dact(): pl.pallas_call(functools.partial(dact_kernel, rows), grid=(width // cols,...  52 us
    pallas_call x2, Pallas kernels, head_dhn(): pl.pallas_call(dhn_kernel, grid=(tokens // blk,), in_specs=[pl.BlockSpec(...  40 us
    select_n x4, other arithmetic, by_core(): jnp.where(core == 0, jnp.concatenate([mine, theirs]), jnp.concatenate([th...  30 us
    dot_general x1, matrix products, fast_step(): jnp.einsum('td,tf->df', normed_bf, d_gate, preferred_element_type=jnp.flo...  23.8 us
  transfers between devices with their start and end apart: 15, of which 5 were waited for; matrix products, arithmetic and copies ran while one was open for 15% of the time, Pallas kernels for 30%

profile of v4, /device:TPU:0, one launch (start us, length us, event | category | flops | bytes accessed | tf_op | source)
XLA Modules:
  0.0 726.3 jit_solution(9807207687398059385)
XLA Ops:
  7.2 0.7 pad_add_fusion
  7.9 2.3 all_gather.19
  11.1 5.9 sort.23
  17.1 1.0 reshape.323
  18.8 0.6 fusion.67
  23.7 10.3 %gather_fusion.1 = bf16[608,1024]{1,0:T(8,128)(2,1)S(1)} fusion(bf16[6288,1024]{1,0:T(8,128)(2,1)} %param.12, s32[1024]{0:T(1024)S(1)} %pad_clamp_fusion), kind=kCustom, calls=%fused_computation.1 | custom fusion | bytes 2492800 | tf_op jit(solution)/shard_map/jit(_take)/gather | solution.py:426
  34.0 1.1 fusion.65
  35.3 1.0 reshape.324
  36.3 0.6 subtract_reduce_fusion.2
  37.6 0.6 fusion.59
  38.9 0.8 copy-done.9
  39.7 2.2 pad_maximum_fusion.2
  42.0 676.1 %conditional.1 = (f32[]{:T(128)}, f32[6288,1024]{1,0:T(8,128)}, f32[512,4096]{1,0:T(8,128)}, f32[512,4096]{1,0:T(8,128)}, f32[2048,1024]{1,0:T(8,128)}) conditional(s32[]{:T(128)} %convert_element_type.57, (s32[1,2048]{1,0:T(1,128)}, bf16[6288,1024]{1,0:T(8,128)(2,1)}, f32[1024]{0:T(1024)S(1)}, bf16[512,4096]{1,0:T(8,128)(2,1)}, ...), branch_computations={%region_4.23_spmd, %region_23.38_spmd} | conditional | flops 313810911232 | bytes 1838356736 | solution.py:551
  50.4 1.2 broadcast_select_fusion
  51.7 17.7 %copy.51 = bf16[6288,1024]{0,1:T(8,128)(2,1)} copy(bf16[6288,1024]{1,0:T(8,128)(2,1)} %get-tuple-element.75.emb_ref) | data formatting | bytes 25755648 | tf_op jit(solution)/shard_map
  69.5 0.9 copy.60
  70.9 10.6 %maximum_select_fusion.2.wd_ref = bf16[4096,1024]{1,0:T(8,128)(2,1)} fusion(bf16[2048,1024]{1,0:T(8,128)(2,1)} %get-tuple-element.81, bf16[2048,1024]{1,0:T(8,128)(2,1)} %get-tuple-element.80, pred[]{:T(512)S(6)} %eq.16), kind=kLoop, calls=%fused_computation.5 | loop fusion | flops 37748736 | bytes 16777216 | tf_op jit(solution)/shard_map/cond/branch_1_fun/jit(_where)/select_n | solution.py:416
  81.5 1.1 copy-done.8
  82.6 16.0 %maximum_select_fusion = (bf16[1024,4096]{1,0:T(8,128)(2,1)}, bf16[1024,4096]{1,0:T(8,128)(2,1)}) fusion(bf16[512,4096]{1,0:T(8,128)(2,1)} %get-tuple-element.77, bf16[512,4096]{1,0:T(8,128)(2,1)S(1)} %copy-done.7, pred[]{:T(512)S(6)} %eq.16, bf16[512,4096]{1,0:T(8,128)(2,1)S(1)} %copy-done.8, bf16[512,4096]{1,0:T(8,128)(2,1)} %get-tuple-element.79), kind=kLoop, calls=%fused_computation.3 | loop fusion | flops 75497472 | bytes 33554432 | tf_op jit(solution)/shard_map/cond/branch_1_fun/jit(_where)/select_n | solution.py:416
  98.6 10.1 %all-gather.7.cloned.1.call-done.block_ref = bf16[8,304,1024]{2,1,0:T(8,128)(2,1)} async-done(((bf16[2,304,1024]{2,1,0:T(8,128)(2,1)}), bf16[8,304,1024]{2,1,0:T(8,128)(2,1)}) %all-gather.7.cloned.1.call-update) | async-done | bytes 4980752 | tf_op jit(solution)/shard_map/cond/branch_1_fun/all_gather | solution.py:445
  108.7 9.5 %place_rows.2.x_ref = f32[2360,1024]{1,0:T(8,128)} custom-call(s32[9]{0:T(128)} %fusion.16.start_ref, bf16[8,304,1024]{2,1,0:T(8,128)(2,1)} %all-gather.7.cloned.1.call-done.block_ref), custom_call_target="tpu_custom_call" | custom-call | flops 19333120 | bytes 19333120 | tf_op jit(solution)/shard_map/cond/branch_1_fun/place_rows/pallas_call | solution.py:361
  118.2 69.8 %mlp_forward.1 = (bf16[2048,1024]{1,0:T(8,128)(2,1)}, bf16[2048,4096]{1,0:T(8,128)(2,1)}, bf16[2048,4096]{1,0:T(8,128)(2,1)}, bf16[2048,4096]{1,0:T(8,128)(2,1)}...) custom-call(f32[2360,1024]{1,0:T(8,128)} %place_rows.2.x_ref, f32[1,1024]{1,0:T(1,128)S(1)} %bitcast.105, ...), custom_call_target="tpu_custom_call" | custom-call | flops 51539607552 | bytes 50331648 | tf_op jit(solution)/shard_map/cond/branch_1_fun/mlp_forward/pallas_call | solution.py:266
  188.0 1.1 subtract_select_fusion
  189.1 1.5 dynamic-slice_bitcast_fusion.1
  190.7 42.1 %head_logits.2 = (f32[2048,6288]{1,0:T(8,128)}, f32[2048,128]{1,0:T(8,128)}) custom-call(bf16[2048,1024]{1,0:T(8,128)(2,1)} %get-tuple-element.88.hn_ref.ha_ref, bf16[1024,6288]{1,0:T(8,128)(2,1)} %bitcast.81, s32[2048,128]{1,0:T(8,128)} %get-tuple-element.206.off_ref), custom_call_target="tpu_custom_call" | custom-call | flops 26373783552 | bytes 51511296 | tf_op jit(solution)/shard_map/cond/branch_1_fun/head_logits/pallas_call | solution.py:127
  232.7 2.3 slice_bitcast_fusion.1
  235.0 41.7 %head_logits.3 = (f32[2048,6288]{1,0:T(8,128)}, f32[2048,128]{1,0:T(8,128)}) custom-call(bf16[2048,1024]{1,0:T(8,128)(2,1)} %collective-permute-done.hn_ref.hb_ref, bf16[1024,6288]{1,0:T(8,128)(2,1)} %bitcast.82, s32[2048,128]{1,0:T(8,128)} %get-tuple-element.207.off_ref), custom_call_target="tpu_custom_call" | custom-call | flops 26373783552 | bytes 51511296 | tf_op jit(solution)/shard_map/cond/branch_1_fun/head_logits/pallas_call | solution.py:127
  276.6 1.3 slice_bitcast_fusion
  277.9 2.2 maximum_select_fusion.3
  280.4 12.3 %all_gather.15 = f32[8,6,2048]{2,1,0:T(8,128)S(1)} all-gather(f32[1,6,2048]{2,1,0:T(8,128)S(1)} %copy.52), channel_id=1, replica_groups=mesh['model'=4,'fsdp'=2] {'model','fsdp'}, dimensions={0}, use_global_device_ids=true | all-gather | bytes 442368 | tf_op jit(solution)/shard_map/cond/branch_1_fun/all_gather | solution.py:458
  293.2 0.7 divide_multiply_fusion
  293.9 1.3 broadcast_in_dim.104.scale_ref
  295.2 1.3 broadcast_in_dim.102.max_ref
  296.5 34.3 %head_dlogits.3 = (bf16[2048,6288]{1,0:T(8,128)(2,1)}, f32[2048,512]{1,0:T(8,128)}) custom-call(f32[2048,6288]{1,0:T(8,128)} %get-tuple-element.95.z_ref, bf16[6288,1024]{1,0:T(8,128)(2,1)} %get-tuple-element.75.emb_ref, f32[2048,128]{1,0:T(8,128)} %broadcast_in_dim.102.max_ref, f32[2048,128]{1,0:T(8,128)} %broadcast_in_dim.104.scale_ref, ...), custom_call_target="tpu_custom_call" | custom-call | flops 13186891776 | bytes 77266944 | tf_op jit(solution)/shard_map/cond/branch_1_fun/head_dlogits/pallas_call | solution.py:167
  331.0 0.6 broadcast_minimum_fusion.first_ref.start_ref
  331.5 1.3 broadcast_in_dim.100.scale_ref
  332.8 1.4 broadcast_in_dim.98.max_ref
  334.2 34.3 %head_dlogits.2 = (bf16[2048,6288]{1,0:T(8,128)(2,1)}, f32[2048,512]{1,0:T(8,128)}) custom-call(f32[2048,6288]{1,0:T(8,128)} %get-tuple-element.93.z_ref, bf16[6288,1024]{1,0:T(8,128)(2,1)} %get-tuple-element.75.emb_ref, f32[2048,128]{1,0:T(8,128)} %broadcast_in_dim.98.max_ref, f32[2048,128]{1,0:T(8,128)} %broadcast_in_dim.100.scale_ref, ...), custom_call_target="tpu_custom_call" | custom-call | flops 13186891776 | bytes 77266944 | tf_op jit(solution)/shard_map/cond/branch_1_fun/head_dlogits/pallas_call | solution.py:167
  368.5 7.0 sum_windows.2
  375.6 20.1 %head_dhn.3 = f32[2048,512]{1,0:T(8,128)} custom-call(bf16[2048,6288]{1,0:T(8,128)(2,1)} %get-tuple-element.104.dz_ref.b_ref, bf16[6288,1024]{1,0:T(8,128)(2,1)} %get-tuple-element.75.emb_ref), custom_call_target="tpu_custom_call" | custom-call | flops 13186891776 | bytes 25755648 | tf_op jit(solution)/shard_map/cond/branch_1_fun/head_dhn/pallas_call | solution.py:194
  396.2 20.0 %head_dhn.2.a_ref = f32[2048,512]{1,0:T(8,128)} custom-call(bf16[2048,6288]{1,0:T(8,128)(2,1)} %get-tuple-element.103.dz_ref.a_ref, bf16[6288,1024]{1,0:T(8,128)(2,1)} %get-tuple-element.75.emb_ref), custom_call_target="tpu_custom_call" | custom-call | flops 13186891776 | bytes 25755648 | tf_op jit(solution)/shard_map/cond/branch_1_fun/head_dhn/pallas_call | solution.py:194
  416.2 6.9 sum_windows.3
  423.2 0.6 dynamic_slice.51
  425.5 45.8 %head_dtable.2.refs_0_ = f32[6288,1024]{1,0:T(8,128)} custom-call(bf16[2048,6288]{1,0:T(8,128)(2,1)} %get-tuple-element.103.dz_ref.a_ref, bf16[2048,1024]{1,0:T(8,128)(2,1)} %get-tuple-element.88.hn_ref.ha_ref, bf16[2048,6288]{1,0:T(8,128)(2,1)} %get-tuple-element.104.dz_ref.b_ref, bf16[2048,1024]{1,0:T(8,128)(2,1)} %collective-permute-done.hn_ref.hb_ref), custom_call_target="tpu_custom_call" | custom-call | flops 37580963840 | bytes 36700160 | tf_op jit(solution)/shard_map/cond/branch_1_fun/head_dtable/pallas_call | solution.py:224
  471.3 9.9 %reduce-scatter.20.cloned.1.call-done = f32[576,512]{1,0:T(8,128)} async-done(((f32[2304,512]{1,0:T(8,128)}), f32[576,512]{1,0:T(8,128)}) %reduce-scatter.20.cloned.1.call-update) | async-done | bytes 1179664 | tf_op jit(solution)/shard_map/cond/branch_1_fun/reduce_scatter | solution.py:479
  481.3 3.0 multiply_reduce_fusion.3
  484.3 4.0 fusion.17
  488.4 0.5 constant_dynamic-slice_fusion.1
  494.4 0.6 copy-done.25
  495.0 0.9 fusion.10
  495.9 23.6 %head_dtable.3.base_ref = f32[6288,1024]{1,0:T(8,128)} custom-call(bf16[2048,6288]{1,0:T(8,128)(2,1)} %get-tuple-element.103.dz_ref.a_ref, bf16[2048,1024]{1,0:T(8,128)(2,1)} %get-tuple-element.88.hn_ref.ha_ref, bf16[2048,6288]{1,0:T(8,128)(2,1)} %get-tuple-element.104.dz_ref.b_ref, ...), custom_call_target="tpu_custom_call", output_to_operand_aliasing={{}: (4, {})} | custom-call | flops 16106127360 | bytes 15728640 | tf_op jit(solution)/shard_map/cond/branch_1_fun/head_dtable/pallas_call | solution.py:224
  519.5 20.2 %all-gather.9.cloned.1.call-done = bf16[2304,1024]{1,0:T(8,128)(2,1)} async-done(((bf16[576,1024]{1,0:T(8,128)(2,1)}), bf16[2304,1024]{1,0:T(8,128)(2,1)}) %all-gather.9.cloned.1.call-update) | async-done | bytes 4718608 | tf_op jit(solution)/shard_map/cond/branch_1_fun/all_gather | solution.py:487
  539.6 6.6 place_rows.3.dm_ref
  546.2 52.0 %mlp_dact.1 = (bf16[2048,4096]{1,0:T(8,128)(2,1)}, bf16[2048,4096]{1,0:T(8,128)(2,1)}, f32[4096,1024]{1,0:T(8,128)}) custom-call(bf16[2048,1024]{1,0:T(8,128)(2,1)} %place_rows.3.dm_ref, bf16[4096,1024]{1,0:T(8,128)(2,1)} %maximum_select_fusion.2.wd_ref, bf16[2048,4096]{1,0:T(8,128)(2,1)} %get-tuple-element.110.gt_ref, ...), custom_call_target="tpu_custom_call" | custom-call | flops 34359738368 | bytes 83886080 | tf_op jit(solution)/shard_map/cond/branch_1_fun/mlp_dact/pallas_call | solution.py:294
  598.2 9.0 %fusion = f32[576,1024]{1,0:T(8,128)S(1)} fusion(bf16[1024,4096]{1,0:T(8,128)(2,1)} %get-tuple-element.86.wu_ref, bf16[2048,4096]{1,0:T(8,128)(2,1)} %get-tuple-element.122, s32[]{:T(128)S(6)} %select_n.173), kind=kOutput, calls=%fused_computation.6 | convolution fusion | flops 4831838208 | bytes 15466500 | tf_op jit(solution)/shard_map/cond/branch_1_fun/tf,df->td/dot_general | solution.py:496
  607.2 10.1 %multiply_reduce_fusion.1 = (f32[576]{0:T(1024)S(1)}, f32[576]{0:T(1024)S(1)}, f32[576,1024]{1,0:T(8,128)S(1)}) fusion(f32[2360,1024]{1,0:T(8,128)} %place_rows.2.x_ref, s32[]{:T(128)S(6)} %select_n.174, f32[1024]{0:T(1024)S(1)} %copy-done.50, f32[576,1024]{1,0:T(8,128)S(1)} %fusion, bf16[1024,4096]{1,0:T(8,128)(2,1)} %get-tuple-element.85.wg_ref, ...), kind=kOutput, calls=%fused_computation.15 | convolution fusion | flops 4835376128 | bytes 20193800 | tf_op jit(solution)/shard_map/cond/branch_1_fun/tf,df->td/dot_general | solution.py:496
  617.4 3.2 fusion.4.own_ref
  621.0 23.3 %fusion.69 = f32[1024,4096]{1,0:T(8,128)} fusion(bf16[2048,1024]{1,0:T(8,128)(2,1)S(1)} %copy-done.51, bf16[2048,4096]{1,0:T(8,128)(2,1)} %get-tuple-element.122), kind=kOutput, calls=%fused_computation.161 | convolution fusion | flops 17179869184 | bytes 37748736 | tf_op jit(solution)/shard_map/cond/branch_1_fun/td,tf->df/dot_general | solution.py:508
  644.5 23.8 %fusion.68 = f32[1024,4096]{1,0:T(8,128)} fusion(bf16[2048,1024]{1,0:T(8,128)(2,1)} %get-tuple-element.120, bf16[2048,4096]{1,0:T(8,128)(2,1)} %get-tuple-element.121), kind=kOutput, calls=%fused_computation.160 | convolution fusion | flops 17179869184 | bytes 37748736 | tf_op jit(solution)/shard_map/cond/branch_1_fun/td,tf->df/dot_general | solution.py:507
  668.3 0.7 reduce-scatter.26.cloned.1.call-update
  669.7 0.7 copy.54.bound_ref
  670.4 3.2 collective-permute-done.3.theirs_ref
  673.6 22.1 %add_rows.1 = f32[6288,1024]{1,0:T(8,128)} custom-call(s32[2,7]{1,0:T(2,128)} %copy.54.bound_ref, s32[2,576]{1,0:T(2,128)} %copy-done.25, f32[6288,1024]{1,0:T(8,128)} %head_dtable.3.base_ref, f32[576,1024]{1,0:T(8,128)} %copy-done.6, f32[576,1024]{1,0:T(8,128)} %collective-permute-done.3.theirs_ref), custom_call_target="tpu_custom_call", output_to_operand_aliasing={{}: (2, {})} | custom-call | flops 12877824 | bytes 51511296 | tf_op jit(solution)/shard_map/cond/branch_1_fun/add_rows/pallas_call | solution.py:321
  695.6 22.2 %reduce-scatter.26.cloned.1.call-done = f32[2048,1024]{1,0:T(8,128)} async-done(((f32[4096,1024]{1,0:T(8,128)}), f32[2048,1024]{1,0:T(8,128)}) %reduce-scatter.26.cloned.1.call-update) | async-done | bytes 8388624 | tf_op jit(solution)/shard_map/cond/branch_1_fun/reduce_scatter | solution.py:513
  (106 shorter events, 5.6 us)
Async XLA Ops:
  10.2 31.7 %collective-permute-start.4 = (bf16[512,4096]{1,0:T(8,128)(2,1)}, bf16[512,4096]{1,0:T(8,128)(2,1)}, u32[]{:S(2)}, u32[]{:S(2)}) collective-permute-start(bf16[512,4096]{1,0:T(8,128)(2,1)} %param.13), channel_id=1, source_target_pairs={{0,1},{1,0},{2,3},{3,2},{4,5},{5,4},{6,7},{7,6}} | collective-permute-start | bytes 12582920 | tf_op jit(solution)/shard_map/ppermute | solution.py:412
  10.6 31.3 %collective-permute-start.5 = (bf16[512,4096]{1,0:T(8,128)(2,1)}, bf16[512,4096]{1,0:T(8,128)(2,1)}, u32[]{:S(2)}, u32[]{:S(2)}) collective-permute-start(bf16[512,4096]{1,0:T(8,128)(2,1)} %param.14), channel_id=1, source_target_pairs={{0,1},{1,0},{2,3},{3,2},{4,5},{5,4},{6,7},{7,6}} | collective-permute-start | bytes 12582920 | tf_op jit(solution)/shard_map/ppermute | solution.py:412
  10.8 31.2 %collective-permute-start.6 = (bf16[2048,1024]{1,0:T(8,128)(2,1)}, bf16[2048,1024]{1,0:T(8,128)(2,1)}, u32[]{:S(2)}, u32[]{:S(2)}) collective-permute-start(bf16[2048,1024]{1,0:T(8,128)(2,1)} %param.15), channel_id=1, source_target_pairs={{0,1},{1,0},{2,3},{3,2},{4,5},{5,4},{6,7},{7,6}} | collective-permute-start | bytes 12582920 | tf_op jit(solution)/shard_map/ppermute | solution.py:412
  18.1 18.2 %copy-start.2 = (s32[2048,2]{1,0:T(8,128)}, s32[2048,2]{1,0:T(8,128)S(1)}, u32[]{:S(2)}) copy-start(s32[2048,2]{1,0:T(8,128)S(1)} %reshape.323) | copy-start | bytes 49156
  18.8 20.1 %copy-start.12 = (s32[2,9]{0,1:T(8,128)}, s32[2,9]{0,1:T(8,128)S(1)}, u32[]{:S(2)}) copy-start(s32[2,9]{0,1:T(8,128)S(1)} %fusion.58) | copy-start | bytes 220
  23.7 18.2 %copy-start.14 = (f32[1024]{0:T(1024)S(1)}, f32[1024]{0:T(1024)}, u32[]{:S(2)}) copy-start(f32[1024]{0:T(1024)} %param.17) | copy-start | bytes 12292
  23.7 18.2 %copy-start.30 = (s32[1,2048]{1,0:T(1,128)S(1)}, s32[1,2048]{1,0:T(1,128)}, u32[]{:S(2)}) copy-start(s32[1,2048]{1,0:T(1,128)} %param.11) | copy-start | bytes 24580
  23.7 18.2 %copy-start.46 = (f32[1024]{0:T(1024)S(1)}, f32[1024]{0:T(1024)}, u32[]{:S(2)}) copy-start(f32[1024]{0:T(1024)} %param.16) | copy-start | bytes 12292
  35.1 3.8 collective-permute-start.7
  38.9 0.8 copy-start.9
  50.4 67.8 %copy-start.17 = (f32[1024]{0:T(1024)}, f32[1024]{0:T(1024)S(1)}, u32[]{:S(2)}) copy-start(f32[1024]{0:T(1024)S(1)} %get-tuple-element.84) | copy-start | bytes 12292 | tf_op jit(solution)/shard_map/cond
  50.4 67.8 %copy-start.49 = (f32[1024]{0:T(1024)}, f32[1024]{0:T(1024)S(1)}, u32[]{:S(2)}) copy-start(f32[1024]{0:T(1024)S(1)} %get-tuple-element.83) | copy-start | bytes 12292 | tf_op jit(solution)/shard_map/cond
  50.4 58.3 %all-gather.7.cloned.1.call-start = ((), (), s32[]{:S(2)}) async-start(), calls=%async_computation.16 | async-start | bytes 6225920 | tf_op jit(solution)/shard_map/cond/branch_1_fun/all_gather | solution.py:445
  51.6 419.7 %reduce-scatter.18.cloned.1.call-start = ((), (), s32[]{:S(2)}) async-start(), calls=%async_computation.17 | async-start | bytes 5898240 | tf_op jit(solution)/shard_map/cond/branch_1_fun/reduce_scatter | solution.py:473
  51.7 17.7 %copy-start.13 = (s32[2,9]{0,1:T(8,128)S(1)}, s32[2,9]{0,1:T(8,128)}, u32[]{:S(2)}) copy-start(s32[2,9]{0,1:T(8,128)} %get-tuple-element.176) | copy-start | bytes 220 | tf_op jit(solution)/shard_map/cond
  69.5 12.0 %copy-start.43 = (s32[2,9]{1,0:T(2,128)}, s32[2,9]{1,0:T(2,128)S(1)}, u32[]{:S(2)}) copy-start(s32[2,9]{1,0:T(2,128)S(1)} %copy.59) | copy-start | bytes 220 | tf_op jit(solution)/shard_map/cond
  70.9 10.6 %copy-start.7 = (bf16[512,4096]{1,0:T(8,128)(2,1)S(1)}, bf16[512,4096]{1,0:T(8,128)(2,1)}, u32[]{:S(2)}) copy-start(bf16[512,4096]{1,0:T(8,128)(2,1)} %get-tuple-element.76) | copy-start | bytes 12582916 | tf_op jit(solution)/shard_map/cond
  70.9 11.7 %copy-start.8 = (bf16[512,4096]{1,0:T(8,128)(2,1)S(1)}, bf16[512,4096]{1,0:T(8,128)(2,1)}, u32[]{:S(2)}) copy-start(bf16[512,4096]{1,0:T(8,128)(2,1)} %get-tuple-element.78) | copy-start | bytes 12582916 | tf_op jit(solution)/shard_map/cond
  118.1 69.8 %copy-start.24 = (s32[2,2048]{1,0:T(2,128)S(1)}, s32[2,2048]{1,0:T(2,128)}, u32[]{:S(2)}) copy-start(s32[2,2048]{1,0:T(2,128)} %copy.60) | copy-start | bytes 49156 | tf_op jit(solution)/shard_map/cond
  187.9 47.0 %collective-permute-start = (bf16[2048,1024]{1,0:T(8,128)(2,1)}, bf16[2048,1024]{1,0:T(8,128)(2,1)}, u32[]{:S(2)}, u32[]{:S(2)}) collective-permute-start(bf16[2048,1024]{1,0:T(8,128)(2,1)} %get-tuple-element.88.hn_ref.ha_ref), channel_id=1, source_target_pairs={{0,1},{1,0},{2,3},{3,2},{4,5},{5,4},{6,7},{7,6}} | collective-permute-start | bytes 12582920 | tf_op jit(solution)/shard_map/cond/branch_1_fun/ppermute | solution.py:412
  296.5 34.3 %copy-start.45 = (s32[9]{0:T(128)S(1)}, s32[9]{0:T(128)}, u32[]{:S(2)}) copy-start(s32[9]{0:T(128)} %fusion.16.start_ref) | copy-start | bytes 112 | tf_op jit(solution)/shard_map/cond
  330.9 37.7 %collective-permute-start.1 = (f32[2048,512]{1,0:T(8,128)}, f32[2048,512]{1,0:T(8,128)}, u32[]{:S(2)}, u32[]{:S(2)}) collective-permute-start(f32[2048,512]{1,0:T(8,128)} %get-tuple-element.96), channel_id=1, source_target_pairs={{0,1},{1,0},{2,3},{3,2},{4,5},{5,4},{6,7},{7,6}} | collective-permute-start | bytes 12582920 | tf_op jit(solution)/shard_map/cond/branch_1_fun/ppermute | solution.py:412
  375.6 105.7 %reduce-scatter.20.cloned.1.call-start = ((), (), s32[]{:S(2)}) async-start(), calls=%async_computation.18 | async-start | bytes 5898240 | tf_op jit(solution)/shard_map/cond/branch_1_fun/reduce_scatter | solution.py:479
  395.7 20.5 %collective-permute-start.2 = (f32[2048,512]{1,0:T(8,128)}, f32[2048,512]{1,0:T(8,128)}, u32[]{:S(2)}, u32[]{:S(2)}) collective-permute-start(f32[2048,512]{1,0:T(8,128)} %head_dhn.3), channel_id=1, source_target_pairs={{0,1},{1,0},{2,3},{3,2},{4,5},{5,4},{6,7},{7,6}} | collective-permute-start | bytes 12582920 | tf_op jit(solution)/shard_map/cond/branch_1_fun/ppermute | solution.py:412
  416.2 7.0 copy-start.42
  423.1 116.5 %all-gather.9.cloned.1.call-start = ((), (), s32[]{:S(2)}) async-start(), calls=%async_computation.22 | async-start | bytes 5898240 | tf_op jit(solution)/shard_map/cond/branch_1_fun/all_gather | solution.py:487
  425.5 55.8 %copy-start.18 = (f32[1024]{0:T(1024)S(1)}, f32[1024]{0:T(1024)}, u32[]{:S(2)}) copy-start(f32[1024]{0:T(1024)} %copy-done.17) | copy-start | bytes 12292 | tf_op jit(solution)/shard_map/cond
  471.3 17.0 %copy-start.44 = (s32[2,9]{1,0:T(2,128)S(1)}, s32[2,9]{1,0:T(2,128)}, u32[]{:S(2)}) copy-start(s32[2,9]{1,0:T(2,128)} %copy-done.43) | copy-start | bytes 220 | tf_op jit(solution)/shard_map/cond
  471.3 21.3 %copy-start.3 = (s32[2,2048]{0,1:T(8,128)S(1)}, s32[2,2048]{0,1:T(8,128)}, u32[]{:S(2)}) copy-start(s32[2,2048]{0,1:T(8,128)} %get-tuple-element.190) | copy-start | bytes 49156 | tf_op jit(solution)/shard_map/cond
  488.3 207.4 %reduce-scatter.24.cloned.1.call-start = ((), (), s32[]{:S(2)}) async-start(), calls=%async_computation.20 | async-start | bytes 25165824 | tf_op jit(solution)/shard_map/cond/branch_1_fun/reduce_scatter | solution.py:512
  494.4 0.6 copy-start.25
  598.2 9.0 %copy-start.50 = (f32[1024]{0:T(1024)S(1)}, f32[1024]{0:T(1024)}, u32[]{:S(2)}) copy-start(f32[1024]{0:T(1024)} %copy-done.49) | copy-start | bytes 12292 | tf_op jit(solution)/shard_map/cond
  607.2 10.2 %copy-start.4 = (f32[576,512]{1,0:T(8,128)S(1)}, f32[576,512]{1,0:T(8,128)}, u32[]{:S(2)}) copy-start(f32[576,512]{1,0:T(8,128)} %reduce-scatter.18.cloned.1.call-done) | copy-start | bytes 3538948 | tf_op jit(solution)/shard_map/cond
  607.2 10.2 %copy-start.5 = (f32[576,512]{1,0:T(8,128)S(1)}, f32[576,512]{1,0:T(8,128)}, u32[]{:S(2)}) copy-start(f32[576,512]{1,0:T(8,128)} %reduce-scatter.20.cloned.1.call-done) | copy-start | bytes 3538948 | tf_op jit(solution)/shard_map/cond
  617.4 3.6 copy-start.51
  620.6 48.4 %copy-start.6 = (f32[576,1024]{1,0:T(8,128)}, f32[576,1024]{1,0:T(8,128)S(1)}, u32[]{:S(2)}) copy-start(f32[576,1024]{1,0:T(8,128)S(1)} %fusion.4.own_ref) | copy-start | bytes 7077892 | tf_op jit(solution)/shard_map/cond
  644.4 51.2 %reduce-scatter.22.cloned.1.call-start = ((), (), s32[]{:S(2)}) async-start(), calls=%async_computation.19 | async-start | bytes 25165824 | tf_op jit(solution)/shard_map/cond/branch_1_fun/reduce_scatter | solution.py:511
  668.3 49.6 %reduce-scatter.26.cloned.1.call-start = ((), (), s32[]{:S(2)}) async-start(), calls=%async_computation.21 | async-start | bytes 25165824 | tf_op jit(solution)/shard_map/cond/branch_1_fun/reduce_scatter | solution.py:513
  668.3 1.4 copy-start.41
  669.0 4.6 collective-permute-start.3
Sparse Core Ops, SparseCore 0:
  53.0 55.6 all-gather.6
  375.7 51.3 reduce-scatter.17
  430.0 51.1 reduce-scatter.19
  488.4 51.2 all-gather.8
  644.5 21.7 reduce-scatter.23
  669.1 23.0 reduce-scatter.21
  694.9 22.8 reduce-scatter.25
